TPU v7x, 32 devices: a whole 2x2x4 slice. The times are simulated.
32 devices in a mesh: seq: 8 (over z, y), tp: 4 (over x, core).
Axes of the slice: x: 2, y: 2, z: 4, core: 2. Of those that a mesh axis runs over, the one named last changes fastest.
Arguments:
- tokens: bfloat16 [8192, 2048], P('seq', 'tp'), may hold values from -8 to 8
- col_order: int32 [8192], P('seq'), may hold values from 0 to 8191, as said below
- in_gain: float32 [2, 2048], replicated, may hold values from 0.5 to 1.5
- w_in: bfloat16 [2, 2048, 2, 2048], P(None, None, None, 'tp'), may hold values from -0.125 to 0.125
- w_bc: bfloat16 [2, 2048, 256], replicated, may hold values from -0.0625 to 0.0625
- w_dt: bfloat16 [2, 2048, 32], P(None, None, 'tp'), may hold values from -2 to 2
- conv_x: float32 [2, 4, 2048], P(None, None, 'tp'), may hold values from -3 to 3
- conv_bc: float32 [2, 4, 256], replicated, may hold values from -3 to 3
- dt_bias: float32 [2, 32], P(None, 'tp'), may hold values from -1 to 0.5
- a_log: float32 [2, 32], P(None, 'tp'), may hold values from -16 to -2, as said below
- d_skip: float32 [2, 32], P(None, 'tp'), may hold values from 0.5 to 2
- out_gain: float32 [2, 2048], P(None, 'tp'), may hold values from 0.5 to 1.5
- w_out: bfloat16 [2, 2048, 2048], P(None, 'tp'), may hold values from -0.125 to 0.125
Outputs:
- mixed_out: bfloat16 [8192, 2048], P('seq', 'tp')
Inputs may be any that keep to these rules, and one draw needn't show every extreme that they name: `col_order`: A permutation of the 8192 positions of a frame of 16 rows and 512 columns stored row by row: the column order visits the columns one after another in a drawn order, each from top to bottom or from bottom to top as drawn. So every aligned block of 1024 positions takes exactly 128 row-order positions from each aligned block of 1024 row-order positions. Each head's decay rate exp(a_log) is either between about one in fifty and one in seventeen a step or between 0.3 / 8192 and 2 / 8192 a step.
All inputs are finite; a program needn't handle non-finite values.
Results may differ from a plain program's by a relative error of at most 0.024.
Values may be sent and summed in bfloat16 or wider, within the bound.
A program may use at most 128 MiB of HBM per device.

v0:
```python
import functools

import jax
import jax.numpy as jnp
from jax import lax
from jax.experimental import pallas as pl
from jax.experimental.pallas import tpu as pltpu
from jax.sharding import PartitionSpec as P

HEAD_DIM = 64
STATE = 128
STRETCH = 128
LANES = 128
HALO = 16
ROWS = 256

highest = lax.Precision.HIGHEST
epsilon = 1e-05
f32 = jnp.float32
bf16 = jnp.bfloat16


def expander(inner):
    head = lax.broadcasted_iota(jnp.int32, (LANES, inner), 0)
    channel = lax.broadcasted_iota(jnp.int32, (LANES, inner), 1)
    return (head == channel // HEAD_DIM).astype(f32)


def expand(values, spreader):
    return jnp.dot(values, spreader, preferred_element_type=f32, precision=highest)


def scan_kernel(
    full_ref, halo_ref, gain_ref, w_ref, taps_ref, bias_ref, rate_ref, skip_ref,
    y_ref, z_ref, c_ref, cum_ref, end_ref, ext_ref, state_ref, sofar_ref,
):
    i = pl.program_id(0)
    rows = full_ref.shape[0]
    inner = y_ref.shape[1]
    mixed = inner + 2 * STATE
    heads = inner // HEAD_DIM
    spreader = expander(inner)

    def normed(v):
        wide = v.astype(f32)
        scale = lax.rsqrt(jnp.mean(wide * wide, axis=-1, keepdims=True) + epsilon)
        return (wide * scale * gain_ref[...]).astype(bf16)

    @pl.when(i == 0)
    def _():
        before = jnp.dot(normed(halo_ref[...]), w_ref[:, :mixed], preferred_element_type=f32)
        ext_ref[0:8, :] = before[HALO - 8 :, :].astype(bf16).astype(f32)
        state_ref[...] = jnp.zeros_like(state_ref)
        sofar_ref[...] = jnp.zeros_like(sofar_ref)

    projected = jnp.dot(normed(full_ref[...]), w_ref[...], preferred_element_type=f32)
    ext_ref[8 : 8 + rows, :] = projected[:, :mixed].astype(bf16).astype(f32)
    conv = jnp.zeros((rows, mixed), f32)
    count = taps_ref.shape[0]
    for k in range(count):
        conv = conv + taps_ref[k : k + 1, :] * ext_ref[9 - count + k : 9 - count + k + rows, :]
    conv = conv * jax.nn.sigmoid(conv)
    ext_ref[0:8, :] = ext_ref[rows : rows + 8, :]
    z_ref[...] = projected[:, mixed : mixed + inner].astype(bf16)
    raw = projected[:, mixed + inner :] + bias_ref[...]
    step = jnp.maximum(raw, 0.0) + jnp.log1p(jnp.exp(-jnp.abs(raw)))
    logs = -step * rate_ref[...]
    x = conv[:, :inner]
    b_all = conv[:, inner : inner + STATE]
    c_all = conv[:, inner + STATE :].astype(bf16)
    c_ref[...] = c_all
    feed = x * expand(step, spreader)

    row = lax.broadcasted_iota(jnp.int32, (STRETCH, STRETCH), 0)
    col = lax.broadcasted_iota(jnp.int32, (STRETCH, STRETCH), 1)
    lower = row >= col
    tri = lower.astype(f32)
    left = lax.broadcasted_iota(jnp.int32, (STRETCH, 2 * HEAD_DIM), 1) < HEAD_DIM
    skip = expand(jnp.broadcast_to(skip_ref[...], (8, LANES)), spreader)[0:1]
    state = state_ref[...]
    sofar = sofar_ref[...]
    for block in range(rows // STRETCH):
        part = slice(block * STRETCH, (block + 1) * STRETCH)
        cum = jnp.dot(tri, logs[part], preferred_element_type=f32, precision=highest)
        cum_t = cum.T
        last = cum[STRETCH - 1 : STRETCH, :]
        b_rows = b_all[part]
        c_rows = c_all[part]
        meet = lax.dot_general(
            c_rows, b_rows.astype(bf16), (((1,), (1,)), ((), ())), preferred_element_type=f32
        )
        factors = expand(
            jnp.concatenate([jnp.exp(cum), jnp.exp(last - cum)], axis=0), spreader
        )
        grown = factors[:STRETCH]
        feed_rows = feed[part]
        carried = jnp.dot(c_rows, state.astype(bf16), preferred_element_type=f32) * grown
        fresh = jnp.dot(
            b_rows.T.astype(bf16),
            (feed_rows * factors[STRETCH:]).astype(bf16),
            preferred_element_type=f32,
        )
        state = state * grown[STRETCH - 1 : STRETCH, :] + fresh
        carried = carried + skip * x[part]
        for pair in range(heads // 2):
            lanes = slice(pair * 2 * HEAD_DIM, (pair + 1) * 2 * HEAD_DIM)
            weights = []
            for h in (2 * pair, 2 * pair + 1):
                spread = jnp.where(lower, cum[:, h : h + 1] - cum_t[h : h + 1, :], -jnp.inf)
                weights.append((meet * jnp.exp(spread)).astype(bf16))
            fed = feed_rows[:, lanes]
            stacked = jnp.concatenate(
                [jnp.where(left, fed, 0.0), jnp.where(left, 0.0, fed)], axis=0
            ).astype(bf16)
            inside = jnp.dot(
                jnp.concatenate(weights, axis=1), stacked, preferred_element_type=f32
            )
            y_ref[part, lanes] = inside + carried[:, lanes]
        cum_ref[part, :] = cum + sofar[0:1, :]
        sofar = sofar + last
    state_ref[...] = state
    sofar_ref[...] = sofar

    @pl.when(i == pl.num_programs(0) - 1)
    def _():
        end_ref[0:STATE, :] = state.astype(bf16)
        end_ref[STATE:, :] = log_rows(expand(sofar, spreader)[0:1])


def out_kernel(y_ref, z_ref, c_ref, cum_ref, arriving_ref, gain_ref, w_ref, o_ref):
    inner = y_ref.shape[1]
    correction = jnp.dot(c_ref[...], arriving_ref[...], preferred_element_type=f32)
    correction = correction * expand(jnp.exp(cum_ref[...]), expander(inner))
    gate = z_ref[...].astype(f32)
    gated = (y_ref[...] + correction) * (gate * jax.nn.sigmoid(gate))
    pair = 2 * HEAD_DIM
    one = lax.broadcasted_iota(jnp.int32, (2 * pair, pair), 0) % pair // HEAD_DIM
    two = lax.broadcasted_iota(jnp.int32, (2 * pair, pair), 1) // HEAD_DIM
    averager = jnp.where(one == two, 1.0 / HEAD_DIM, 0.0).astype(bf16)
    square = gated * gated
    high = square.astype(bf16)
    low = (square - high.astype(f32)).astype(bf16)
    pieces = []
    for p in range(inner // pair):
        lanes = slice(p * pair, (p + 1) * pair)
        both = jnp.concatenate([high[:, lanes], low[:, lanes]], axis=1)
        mean = jnp.dot(both, averager, preferred_element_type=f32)
        pieces.append(
            (gated[:, lanes] * lax.rsqrt(mean + epsilon) * gain_ref[:, lanes]).astype(bf16)
        )
    mixed_heads = jnp.concatenate(pieces, axis=1)
    o_ref[...] = jnp.dot(mixed_heads, w_ref[...], preferred_element_type=f32).astype(bf16)


def meet_all(partners):
    barrier = pltpu.get_barrier_semaphore()
    for partner in partners:
        pl.semaphore_signal(
            barrier, inc=1, device_id=partner, device_id_type=pl.DeviceIdType.MESH
        )
    pl.semaphore_wait(barrier, len(partners))


def log_of(tail):
    wide = tail.astype(f32)
    return wide[0:1] + wide[1:2] + wide[2:3]


def log_rows(log):
    total = jnp.broadcast_to(log, (HALO, log.shape[1]))
    high = total.astype(bf16).astype(f32)
    middle = (total - high).astype(bf16).astype(f32)
    low = (total - high) - middle
    line = lax.broadcasted_iota(jnp.int32, total.shape, 0)
    return jnp.where(line == 0, high, jnp.where(line == 1, middle, low)).astype(bf16)


def exchange_kernel(
    count, end_ref, arriving_ref, send_ref, got_ref, total_ref, prefix_ref, send_sem, recv_sem
):
    own = lax.axis_index("seq")
    other = lax.axis_index("tp")
    partners, uppers = [], []
    size = 2
    while size <= count:
        place = own % size
        base = own - place
        partner = base + (1 - place if size == 2 else size - 2 - place + 2 * (place % 2))
        partners.append((partner, other))
        uppers.append(place // (size // 2) == 1)
        size *= 2
    meet_all(partners)
    total_ref[...] = end_ref[:STATE, :].astype(f32)
    prefix_ref[...] = jnp.zeros_like(prefix_ref)
    total_log = log_of(end_ref[STATE:, :])
    prefix_log = jnp.zeros_like(total_log)
    for step, (partner, upper) in enumerate(zip(partners, uppers)):
        if step:
            send_ref[step - 1, :STATE, :] = total_ref[...].astype(bf16)
            send_ref[step - 1, STATE:, :] = log_rows(total_log)
        copy = pltpu.make_async_remote_copy(
            src_ref=send_ref.at[step - 1] if step else end_ref,
            dst_ref=got_ref.at[step],
            send_sem=send_sem.at[step],
            recv_sem=recv_sem.at[step],
            device_id=partner,
            device_id_type=pl.DeviceIdType.MESH,
        )
        copy.start()
        copy.wait()
        theirs = got_ref[step, :STATE, :].astype(f32)
        their_log = log_of(got_ref[step, STATE:, :])
        prefix = prefix_ref[...]
        prefix_ref[...] = jnp.where(upper, theirs * jnp.exp(prefix_log) + prefix, prefix)
        prefix_log = jnp.where(upper, prefix_log + their_log, prefix_log)
        if step + 1 < len(partners):
            mine = total_ref[...]
            first = jnp.where(upper, theirs, mine)
            then = jnp.where(upper, mine, theirs)
            total_ref[...] = first * jnp.exp(jnp.where(upper, total_log, their_log)) + then
            total_log = total_log + their_log
    arriving_ref[...] = prefix_ref[...].astype(bf16)


def exchange_states(end):
    count = lax.axis_size("seq")
    steps = count.bit_length() - 1
    inner = end.shape[1]
    vmem = pl.BlockSpec(memory_space=pltpu.VMEM)
    return pl.pallas_call(
        functools.partial(exchange_kernel, count),
        in_specs=[vmem],
        out_specs=vmem,
        out_shape=jax.ShapeDtypeStruct((STATE, inner), bf16),
        scratch_shapes=[
            pltpu.VMEM((max(steps - 1, 1),) + end.shape, bf16),
            pltpu.VMEM((steps,) + end.shape, bf16),
            pltpu.VMEM((STATE, inner), f32),
            pltpu.VMEM((STATE, inner), f32),
            pltpu.SemaphoreType.DMA((steps,)),
            pltpu.SemaphoreType.DMA((steps,)),
        ],
        compiler_params=pltpu.CompilerParams(collective_id=0, has_side_effects=True),
        name="exchange_states",
    )(end)


def collect_kernel(
    partial_ref, stream_ref, out_ref, near_ref, sum_ref, far_ref,
    near_send, near_recv, far_send, far_recv,
):
    seq = lax.axis_index("seq")
    own = lax.axis_index("tp")
    chip, core = own // 2, own % 2
    partner = (seq, chip * 2 + 1 - core)
    across = (seq, (1 - chip) * 2 + core)
    rows, width = out_ref.shape
    chunks = near_send.shape[1]
    size = rows // chunks

    def columns(block):
        return pl.ds(pl.multiple_of(block * width, LANES), width)

    meet_all([partner, across])
    near = []
    for side, block in ((0, (1 - chip) * 2 + 1 - core), (1, chip * 2 + 1 - core)):
        for k in range(chunks):
            part = pl.ds(k * size, size)
            copy = pltpu.make_async_remote_copy(
                src_ref=partial_ref.at[part, columns(block)],
                dst_ref=near_ref.at[side, part],
                send_sem=near_send.at[side, k],
                recv_sem=near_recv.at[side, k],
                device_id=partner,
                device_id_type=pl.DeviceIdType.MESH,
            )
            copy.start()
            near.append(copy)
    far = []
    for k in range(chunks):
        part = pl.ds(k * size, size)
        near[k].wait_recv()
        sum_ref[part, :] = (
            partial_ref[part, columns((1 - chip) * 2 + core)].astype(f32)
            + near_ref[0, part, :].astype(f32)
        ).astype(bf16)
        copy = pltpu.make_async_remote_copy(
            src_ref=sum_ref.at[part],
            dst_ref=far_ref.at[part],
            send_sem=far_send.at[k],
            recv_sem=far_recv.at[k],
            device_id=across,
            device_id_type=pl.DeviceIdType.MESH,
        )
        copy.start()
        far.append(copy)
    for k in range(chunks):
        part = pl.ds(k * size, size)
        near[chunks + k].wait_recv()
        far[k].wait_recv()
        out_ref[part, :] = (
            stream_ref[part, :].astype(f32)
            + partial_ref[part, columns(own)].astype(f32)
            + near_ref[1, part, :].astype(f32)
            + far_ref[part, :].astype(f32)
        ).astype(bf16)
    for copy in near + far:
        copy.wait_send()


def collect_heads(partial_sum, stream):
    rows, width = stream.shape
    chunks = 8
    vmem = pl.BlockSpec(memory_space=pltpu.VMEM)
    return pl.pallas_call(
        collect_kernel,
        in_specs=[vmem, vmem],
        out_specs=vmem,
        out_shape=jax.ShapeDtypeStruct(stream.shape, bf16),
        scratch_shapes=[
            pltpu.VMEM((2, rows, width), bf16),
            pltpu.VMEM((rows, width), bf16),
            pltpu.VMEM((rows, width), bf16),
            pltpu.SemaphoreType.DMA((2, chunks)),
            pltpu.SemaphoreType.DMA((2, chunks)),
            pltpu.SemaphoreType.DMA((chunks,)),
            pltpu.SemaphoreType.DMA((chunks,)),
        ],
        compiler_params=pltpu.CompilerParams(
            collective_id=1, has_side_effects=True, vmem_limit_bytes=40 * 1024 * 1024
        ),
        name="collect_heads",
    )(partial_sum, stream)


def whole(shape):
    return pl.BlockSpec(shape, lambda i: (0,) * len(shape))


def blocked(columns):
    return pl.BlockSpec((ROWS, columns), lambda i: (i, 0))


def mixer(full, halo, params):
    gain, weights, taps, bias, rate, skip, out_gain, w_out = params
    row_count, width = full.shape
    inner = w_out.shape[0]
    mixed = inner + 2 * STATE
    steps = row_count // ROWS
    limit = pltpu.CompilerParams(
        dimension_semantics=("arbitrary",), vmem_limit_bytes=48 * 1024 * 1024
    )
    y, z, c, cum, end = pl.pallas_call(
        scan_kernel,
        grid=(steps,),
        in_specs=[
            blocked(width), whole(halo.shape), whole(gain.shape), whole(weights.shape),
            whole(taps.shape), whole(bias.shape), whole(rate.shape), whole(skip.shape),
        ],
        out_specs=[
            blocked(inner), blocked(inner), blocked(STATE), blocked(LANES),
            whole((STATE + HALO, inner)),
        ],
        out_shape=[
            jax.ShapeDtypeStruct((row_count, inner), f32),
            jax.ShapeDtypeStruct((row_count, inner), bf16),
            jax.ShapeDtypeStruct((row_count, STATE), bf16),
            jax.ShapeDtypeStruct((row_count, LANES), f32),
            jax.ShapeDtypeStruct((STATE + HALO, inner), bf16),
        ],
        scratch_shapes=[
            pltpu.VMEM((ROWS + 8, mixed), f32),
            pltpu.VMEM((STATE, inner), f32),
            pltpu.VMEM((8, LANES), f32),
        ],
        compiler_params=limit,
        cost_estimate=pl.CostEstimate(
            flops=2 * row_count * width * weights.shape[1],
            bytes_accessed=2 * row_count * width + 2 * weights.size,
            transcendentals=0,
        ),
        name="scan_rows",
    )(full, halo, gain, weights, taps, bias, rate, skip)
    arriving = exchange_states(end)
    return pl.pallas_call(
        out_kernel,
        grid=(steps,),
        in_specs=[
            blocked(inner), blocked(inner), blocked(STATE), blocked(LANES),
            whole(arriving.shape), whole(out_gain.shape), whole(w_out.shape),
        ],
        out_specs=blocked(w_out.shape[1]),
        out_shape=jax.ShapeDtypeStruct((row_count, w_out.shape[1]), bf16),
        compiler_params=limit,
        cost_estimate=pl.CostEstimate(
            flops=2 * row_count * inner * w_out.shape[1],
            bytes_accessed=2 * row_count * w_out.shape[1] + 2 * w_out.size,
            transcendentals=0,
        ),
        name="project_out",
    )(y, z, c, cum, arriving, out_gain, w_out)


def spread_features(piece):
    return lax.all_gather(piece, "tp", axis=1, tiled=True)


def halo_rows(piece):
    count = lax.axis_size("seq")
    tail = piece[piece.shape[0] - HALO :]
    return spread_features(lax.ppermute(tail, "seq", [(i, i + 1) for i in range(count - 1)]))


def plan_kernel(source_ref, local_ref, mine_ref, hand_ref, place_ref):
    own = lax.axis_index("seq")
    count, length = source_ref.shape
    share = length // count
    line = lax.broadcasted_iota(jnp.int32, (length, length), 0)
    lane = lax.broadcasted_iota(jnp.int32, (length, length), 1)
    upto = (line <= lane).astype(bf16)
    device = lax.broadcasted_iota(jnp.int32, (count, length), 0)

    def slots(member):
        ones = jnp.where(member, 1.0, 0.0)
        counted = jnp.dot(ones.astype(bf16), upto, preferred_element_type=f32)
        return jnp.where(member, counted.astype(jnp.int32) - 1, -1)

    slot = slots(source_ref[...] == own)
    short = lax.broadcasted_iota(jnp.int32, (share, length), 0)
    wide = lax.broadcasted_iota(jnp.int32, (share, length), 1)
    for d in range(count):
        chosen = slot[d : d + 1, :] == short
        local = jnp.where(chosen, local_ref[d : d + 1, :], 0).astype(f32)
        wanted = jnp.sum(local, axis=1, keepdims=True).astype(jnp.int32)
        hand_ref[d * share : (d + 1) * share, :] = jnp.where(wanted == wide, 1.0, 0.0).astype(bf16)
    from_each = mine_ref[...] == device
    arrived = jnp.where(from_each, slots(from_each) + share * device, 0).astype(f32)
    target = jnp.sum(arrived, axis=0, keepdims=True).astype(jnp.int32)
    place_ref[...] = jnp.where(line == target, 1.0, 0.0).astype(bf16)


def reorder_plans(col_order, orders):
    length = col_order.shape[0]
    vmem = pl.BlockSpec(memory_space=pltpu.VMEM)
    plan = jax.ShapeDtypeStruct((length, length), bf16)
    return pl.pallas_call(
        plan_kernel,
        in_specs=[vmem] * 3,
        out_specs=[vmem] * 2,
        out_shape=[plan, plan],
        compiler_params=pltpu.CompilerParams(vmem_limit_bytes=40 * 1024 * 1024),
        name="reorder_plans",
    )(orders // length, orders % length, (col_order // length)[None])


def pick(plan, rows):
    return jnp.dot(plan, rows, preferred_element_type=f32).astype(bf16)


def reorder_rows(stream, plans):
    hand, place = plans
    arrived = lax.all_to_all(pick(hand, stream), "seq", split_axis=0, concat_axis=0, tiled=True)
    return lax.dot_general(
        place, arrived, (((0,), (0,)), ((), ())), preferred_element_type=f32
    ).astype(bf16)


def body(
    tokens, col_order, in_gain, w_in, w_bc, w_dt, conv_x, conv_bc,
    dt_bias, a_log, d_skip, out_gain, w_out,
):
    pad = LANES - dt_bias.shape[1]

    def layer(which):
        weights = jnp.concatenate(
            [
                w_in[which, :, 0], w_bc[which], w_in[which, :, 1],
                jnp.pad(w_dt[which], ((0, 0), (0, pad))),
            ],
            axis=1,
        )
        return (
            in_gain[which][None],
            weights,
            jnp.concatenate([conv_x[which], conv_bc[which]], axis=1),
            jnp.pad(dt_bias[which], (0, pad))[None],
            jnp.pad(jnp.exp(a_log[which]), (0, pad))[None],
            jnp.pad(d_skip[which], (0, pad))[None],
            out_gain[which][None],
            w_out[which],
        )

    orders = lax.all_gather(col_order, "seq", axis=0)
    tokens, orders = lax.optimization_barrier((tokens, orders))
    plans = reorder_plans(col_order, orders)
    layers = [layer(0), layer(1)]
    full = spread_features(tokens)
    full, plans, layers = lax.optimization_barrier((full, plans, layers))
    first = mixer(full, halo_rows(tokens), layers[0])
    row_result = collect_heads(first, tokens)
    own_rows = reorder_rows(row_result, plans)
    second = mixer(spread_features(own_rows), halo_rows(own_rows), layers[1])
    return collect_heads(second, own_rows)


def solution(mesh):
    placed = (
        P("seq", "tp"),
        P("seq"),
        P(),
        P(None, None, None, "tp"),
        P(),
        P(None, None, "tp"),
        P(None, None, "tp"),
        P(),
        P(None, "tp"),
        P(None, "tp"),
        P(None, "tp"),
        P(None, "tp"),
        P(None, "tp", None),
    )
    return jax.shard_map(
        body, mesh=mesh, in_specs=placed, out_specs=P("seq", "tp"), check_vma=False
    )
```

profile of v0, /device:TPU:0, one launch (start us, length us, event | category | flops | bytes accessed | tf_op | source)
XLA Modules:
  0.0 330.8 jit_solution(148755525926330486)
XLA Ops:
  6.5 32.5 %all-gather = s32[8192]{0:T(1024)S(1)} all-gather(s32[1024]{0:T(1024)} %param.14), channel_id=2, replica_groups=mesh['seq'=8,'tp'=4] {'seq'}, dimensions={0}, use_global_device_ids=true | all-gather | bytes 36864 | tf_op jit(solution)/shard_map/all_gather | solution.py:493
  39.9 3.4 %collective-permute-start = (bf16[16,512]{1,0:T(8,128)(2,1)S(1)}, bf16[16,512]{1,0:T(8,128)(2,1)S(1)}, u32[]{:S(2)}, u32[]{:S(2)}) collective-permute-start(bf16[16,512]{1,0:T(8,128)(2,1)S(1)} %slice.102), channel_id=1, source_target_pairs={{0,4},{4,8},{8,12},{12,16},{16,20},{20,24},{24,28},{1,5},{5,9},{9,... | collective-permute-start | bytes 49160 | tf_op jit(solution)/shard_map/ppermute | solution.py:411
  50.8 4.1 %slice_bitcast_fusion = (bf16[512,2048]{1,0:T(8,128)(2,1)S(1)}, bf16[512,2048]{1,0:T(8,128)(2,1)}) fusion(bf16[2,512,2048]{2,1,0:T(8,128)(2,1)} %param.25), kind=kLoop, calls=%fused_computation.9 | loop fusion | bytes 8388608 | tf_op jit(solution)/shard_map/squeeze | solution.py:490
  56.2 11.8 %fusion.8 = (bf16[1,2048,1,512]{3,2,1,0:T(2,128)(2,1)S(1)}, bf16[1,2048,1,512]{3,2,1,0:T(2,128)(2,1)S(1)}, bf16[1,2048,1,512]{3,2,1,0:T(2,128)(2,1)S(1)}, bf16[1,2048,1,512]{3,2,1,0:T(2,128)(2,1)S(1)}) fusion(bf16[2,2048,2,512]{3,2,1,0:T(2,128)(2,1)S(1)} %copy-done.21), kind=kLoop, calls=%fused_computation.48 | loop fusion | bytes 16777216 | tf_op jit(solution)/shard_map/slice | solution.py:477
  70.6 2.9 fusion.3.w_ref
  73.6 2.9 fusion.2.w_ref
  76.4 2.3 reorder_plans.1
  81.4 5.4 %all_gather.21.halo_ref = bf16[16,2048]{1,0:T(8,128)(2,1)S(1)} all-gather(bf16[16,512]{1,0:T(8,128)(2,1)S(1)} %collective-permute-done), channel_id=1, replica_groups=mesh['seq'=8,'tp'=4] {'tp'}, dimensions={1}, use_global_device_ids=true | all-gather | bytes 81920 | tf_op jit(solution)/shard_map/all_gather | solution.py:405
  86.8 22.3 %scan_rows.2 = (f32[1024,512]{1,0:T(8,128)S(1)}, bf16[1024,512]{1,0:T(8,128)(2,1)S(1)}, bf16[1024,128]{1,0:T(8,128)(2,1)S(1)}, f32[1024,128]{1,0:T(8,128)S(1)}, bf16[144,512]{1,0:T(8,128)(2,1)S(1)}) custom-call(bf16[1024,2048]{1,0:T(8,128)(2,1)} %all-gather.4.cloned.1.call-done.full_ref, bf16[16,2048]{1,0:T(8,128)(2,1)S(1)} %all_gather.21.halo_ref, ...), custom_call_target="tpu_custom_call" | custom-call | flops 5905580032 | bytes 9961472 | tf_op jit(solution)/shard_map/scan_rows/pallas_call | solution.py:353
  112.0 17.9 %exchange_states.2.arriving_ref = bf16[128,512]{1,0:T(8,128)(2,1)} custom-call(bf16[144,512]{1,0:T(8,128)(2,1)} %copy-done.15), custom_call_target="tpu_custom_call" | custom-call | tf_op jit(solution)/shard_map/exchange_states/pallas_call | solution.py:230
  131.5 1.6 copy-done.6
  135.0 6.8 %project_out.2.partial_ref = bf16[1024,2048]{1,0:T(8,128)(2,1)} custom-call(f32[1024,512]{1,0:T(8,128)S(1)} %copy-done.6, bf16[1024,512]{1,0:T(8,128)(2,1)S(1)} %get-tuple-element.52.z_ref, bf16[1024,128]{1,0:T(8,128)(2,1)S(1)} %get-tuple-element.53.c_ref, f32[1024,128]{1,0:T(8,128)S(1)} %copy-done.12, bf16[128,512]{1,0:T(8,128)(2,1)S(1)} %copy-done.9, ...), custom_call_target="tpu_custom_call" | custom-call | flops 2147483648 | bytes 6291456 | tf_op jit(solution)/shard_map/project_out/pallas_call | solution.py:385
  141.8 2.2 copy-done.1
  144.0 27.3 %collect_heads.2 = bf16[1024,512]{1,0:T(8,128)(2,1)S(1)} custom-call(bf16[1024,2048]{1,0:T(8,128)(2,1)S(1)} %copy-done.1, bf16[1024,512]{1,0:T(8,128)(2,1)S(1)} %copy-done.3), custom_call_target="tpu_custom_call" | custom-call | tf_op jit(solution)/shard_map/collect_heads/pallas_call | solution.py:315
  172.5 32.2 %all_to_all.12 = bf16[8,128,512]{2,1,0:T(8,128)(2,1)S(1)} all-to-all(bf16[8,128,512]{2,1,0:T(8,128)(2,1)S(1)} %bitcast.60), channel_id=1, replica_groups=mesh['seq'=8,'tp'=4] {'seq'}, dimensions={0} | all-to-all | bytes 2097152 | tf_op jit(solution)/shard_map/all_to_all | solution.py:462
  204.7 2.3 convolution_convert_fusion.stream_ref
  207.7 3.3 %collective-permute-start.1 = (bf16[16,512]{1,0:T(8,128)(2,1)S(1)}, bf16[16,512]{1,0:T(8,128)(2,1)S(1)}, u32[]{:S(2)}, u32[]{:S(2)}) collective-permute-start(bf16[16,512]{1,0:T(8,128)(2,1)S(1)} %slice.104), channel_id=1, source_target_pairs={{0,4},{4,8},{8,12},{12,16},{16,20},{20,24},{24,28},{1,5},{5,9},{9,... | collective-permute-start | bytes 49160 | tf_op jit(solution)/shard_map/ppermute | solution.py:411
  212.4 5.6 %all_gather.23.halo_ref = bf16[16,2048]{1,0:T(8,128)(2,1)S(1)} all-gather(bf16[16,512]{1,0:T(8,128)(2,1)S(1)} %collective-permute-done.1), channel_id=1, replica_groups=mesh['seq'=8,'tp'=4] {'tp'}, dimensions={1}, use_global_device_ids=true | all-gather | bytes 81920 | tf_op jit(solution)/shard_map/all_gather | solution.py:405
  218.0 22.4 %all-gather.6.cloned.1.call-done.full_ref = bf16[1024,2048]{1,0:T(8,128)(2,1)} async-done(((bf16[1024,512]{1,0:T(8,128)(2,1)}), bf16[1024,2048]{1,0:T(8,128)(2,1)}) %all-gather.6.cloned.1.call-update) | async-done | bytes 4194320 | tf_op jit(solution)/shard_map/all_gather | solution.py:405
  240.4 22.2 %scan_rows.3 = (f32[1024,512]{1,0:T(8,128)S(1)}, bf16[1024,512]{1,0:T(8,128)(2,1)S(1)}, bf16[1024,128]{1,0:T(8,128)(2,1)S(1)}, f32[1024,128]{1,0:T(8,128)S(1)}, bf16[144,512]{1,0:T(8,128)(2,1)S(1)}) custom-call(bf16[1024,2048]{1,0:T(8,128)(2,1)} %all-gather.6.cloned.1.call-done.full_ref, bf16[16,2048]{1,0:T(8,128)(2,1)S(1)} %all_gather.23.halo_ref, ...), custom_call_target="tpu_custom_call" | custom-call | flops 5905580032 | bytes 9961472 | tf_op jit(solution)/shard_map/scan_rows/pallas_call | solution.py:353
  265.5 19.0 %exchange_states.3.arriving_ref = bf16[128,512]{1,0:T(8,128)(2,1)} custom-call(bf16[144,512]{1,0:T(8,128)(2,1)} %copy-done.16), custom_call_target="tpu_custom_call" | custom-call | tf_op jit(solution)/shard_map/exchange_states/pallas_call | solution.py:230
  288.1 6.7 %project_out.3.partial_ref = bf16[1024,2048]{1,0:T(8,128)(2,1)} custom-call(f32[1024,512]{1,0:T(8,128)S(1)} %copy-done.8, bf16[1024,512]{1,0:T(8,128)(2,1)S(1)} %get-tuple-element.65.z_ref, bf16[1024,128]{1,0:T(8,128)(2,1)S(1)} %get-tuple-element.66.c_ref, f32[1024,128]{1,0:T(8,128)S(1)} %copy-done.14, bf16[128,512]{1,0:T(8,128)(2,1)S(1)} %copy-done.10, ...), custom_call_target="tpu_custom_call" | custom-call | flops 2147483648 | bytes 6291456 | tf_op jit(solution)/shard_map/project_out/pallas_call | solution.py:385
  294.8 2.2 copy-done
  297.0 26.0 %collect_heads.3 = bf16[1024,512]{1,0:T(8,128)(2,1)S(1)} custom-call(bf16[1024,2048]{1,0:T(8,128)(2,1)S(1)} %copy-done, bf16[1024,512]{1,0:T(8,128)(2,1)S(1)} %copy-done.4), custom_call_target="tpu_custom_call" | custom-call | tf_op jit(solution)/shard_map/collect_heads/pallas_call | solution.py:315
  (84 shorter events, 31.8 us)
Async XLA Ops:
  6.5 80.3 %all-gather.4.cloned.1.call-start = ((), (), s32[]{:S(2)}) async-start(), calls=%async_computation.1 | async-start | bytes 5242880 | tf_op jit(solution)/shard_map/all_gather | solution.py:405
  39.1 201.3 %all-gather.6.cloned.1.call-start = ((), (), s32[]{:S(2)}) async-start(), calls=%async_computation.2 | async-start | bytes 5242880 | tf_op jit(solution)/shard_map/all_gather | solution.py:405
  39.9 41.5 %collective-permute-start = (bf16[16,512]{1,0:T(8,128)(2,1)S(1)}, bf16[16,512]{1,0:T(8,128)(2,1)S(1)}, u32[]{:S(2)}, u32[]{:S(2)}) collective-permute-start(bf16[16,512]{1,0:T(8,128)(2,1)S(1)} %slice.102), channel_id=1, source_target_pairs={{0,4},{4,8},{8,12},{12,16},{16,20},{20,24},{24,28},{1,5},{5,9},{9,... | collective-permute-start | bytes 49160 | tf_op jit(solution)/shard_map/ppermute | solution.py:411
  46.8 8.1 %copy-start.26 = (f32[2,2048]{1,0:T(2,128)S(1)}, f32[2,2048]{1,0:T(2,128)}, u32[]{:S(2)}) copy-start(f32[2,2048]{1,0:T(2,128)} %param.15) | copy-start | bytes 49156
  46.8 8.1 %copy-start.27 = (f32[2,512]{1,0:T(2,128)S(1)}, f32[2,512]{1,0:T(2,128)}, u32[]{:S(2)}) copy-start(f32[2,512]{1,0:T(2,128)} %param.24) | copy-start | bytes 12292
  46.8 8.2 %copy-start.25 = (bf16[2,2048,256]{2,1,0:T(8,128)(2,1)S(1)}, bf16[2,2048,256]{2,1,0:T(8,128)(2,1)}, u32[]{:S(2)}) copy-start(bf16[2,2048,256]{2,1,0:T(8,128)(2,1)} %param.17) | copy-start | bytes 6291460
  50.8 5.5 %copy-start.21 = (bf16[2,2048,2,512]{3,2,1,0:T(2,128)(2,1)S(1)}, bf16[2,2048,2,512]{3,2,1,0:T(2,128)(2,1)}, u32[]{:S(2)}) copy-start(bf16[2,2048,2,512]{3,2,1,0:T(2,128)(2,1)} %param.16) | copy-start | bytes 25165828
  69.3 1.3 copy-start.22
  69.3 1.3 copy-start.24
  70.6 2.9 copy-start.23
  78.8 1.3 copy-start.17
  80.1 1.3 copy-start.19
  109.2 1.4 copy-start.5
  129.9 1.6 copy-start.2
  131.5 1.6 copy-start.6
  135.0 6.8 %copy-start.3 = (bf16[1024,512]{1,0:T(8,128)(2,1)S(1)}, bf16[1024,512]{1,0:T(8,128)(2,1)}, u32[]{:S(2)}) copy-start(bf16[1024,512]{1,0:T(8,128)(2,1)} %stream_ref) | copy-start | bytes 3145732
  141.8 2.2 copy-start.1
  144.0 27.3 %copy-start.20 = (bf16[1024,1024]{1,0:T(8,128)(2,1)S(1)}, bf16[1024,1024]{1,0:T(8,128)(2,1)}, u32[]{:S(2)}) copy-start(bf16[1024,1024]{1,0:T(8,128)(2,1)} %copy-done.19) | copy-start | bytes 6291460
  171.2 33.5 %copy-start.18 = (bf16[1024,1024]{1,0:T(8,128)(2,1)S(1)}, bf16[1024,1024]{1,0:T(8,128)(2,1)}, u32[]{:S(2)}) copy-start(bf16[1024,1024]{1,0:T(8,128)(2,1)} %copy-done.17) | copy-start | bytes 6291460
  207.7 4.7 %collective-permute-start.1 = (bf16[16,512]{1,0:T(8,128)(2,1)S(1)}, bf16[16,512]{1,0:T(8,128)(2,1)S(1)}, u32[]{:S(2)}, u32[]{:S(2)}) collective-permute-start(bf16[16,512]{1,0:T(8,128)(2,1)S(1)} %slice.104), channel_id=1, source_target_pairs={{0,4},{4,8},{8,12},{12,16},{16,20},{20,24},{24,28},{1,5},{5,9},{9,... | collective-permute-start | bytes 49160 | tf_op jit(solution)/shard_map/ppermute | solution.py:411
  262.7 1.4 copy-start.7
  284.6 1.6 copy-start.8
  288.1 6.7 %copy-start.4 = (bf16[1024,512]{1,0:T(8,128)(2,1)S(1)}, bf16[1024,512]{1,0:T(8,128)(2,1)}, u32[]{:S(2)}) copy-start(bf16[1024,512]{1,0:T(8,128)(2,1)} %convolution_convert_fusion.stream_ref) | copy-start | bytes 3145732
  294.8 2.2 copy-start
  (8 other events, 6.8 us)
Sparse Core Ops, SparseCore 0:
  39.2 35.3 all-gather.3
  207.1 33.3 all-gather.5
where the time goes:
time: 332 us; the launch traced here: 331 us
  Pallas kernels  151 us (45%)
  blocking collectives  75.7 us (23%)
  local copies, waits for them, and re-layouts  50.2 us (15%)
  waiting for transfers between devices  23.9 us (7%)
  between operations  13.7 us (4%)
  starting transfers between devices  6.77 us (2%)
  other arithmetic  6.5 us (2%)
  matrix products  3.5 us (1%)
    pallas_call x2, Pallas kernels, collect_heads(): pl.pallas_call(collect_kernel, in_specs=[vmem, vmem], out_specs=vmem, out...  53.2 us
    pallas_call x2, Pallas kernels, mixer(): pl.pallas_call(scan_kernel, grid=(steps,), in_specs=[blocked(width), whol...  44.6 us
    pallas_call x2, Pallas kernels, exchange_states(): pl.pallas_call(functools.partial(exchange_kernel, count), in_specs=[vmem]...  36.9 us
    all_gather x1, blocking collectives, body(): orders = lax.all_gather(col_order, 'seq', axis=0)  32.5 us
    all_to_all x1, blocking collectives, reorder_rows(): lax.all_to_all(pick(hand, stream), 'seq', split_axis=0, concat_axis=0, ti...  32.2 us
    unnamed x59, local copies, waits for them, and re-layouts  24.5 us
    all_gather x2, waiting for transfers between devices, spread_features(): return lax.all_gather(piece, 'tp', axis=1, tiled=True)  22.4 us
    pallas_call x2, Pallas kernels, mixer(): pl.pallas_call(out_kernel, grid=(steps,), in_specs=[blocked(inner), block...  13.5 us
  transfers between devices with their start and end apart: 4, of which 2 were waited for; matrix products, arithmetic and copies ran while one was open for 10% of the time, Pallas kernels for 1%

commit v1 on v0

v1 whole, which is shorter than its diff:
```python
import functools

import jax
import jax.numpy as jnp
from jax import lax
from jax.experimental import pallas as pl
from jax.experimental.pallas import tpu as pltpu
from jax.sharding import PartitionSpec as P

HEAD_DIM = 64
STATE = 128
STRETCH = 128
LANES = 128
HALO = 16
ROWS = 256

epsilon = 1e-05
f32 = jnp.float32
bf16 = jnp.bfloat16
MESH = pl.DeviceIdType.MESH


def iota(shape, axis):
    return lax.broadcasted_iota(jnp.int32, shape, axis)


def spreader_of(heads, inner):
    row = iota((LANES, inner), 0)
    channel = iota((LANES, inner), 1)
    chosen = (row % heads == channel // HEAD_DIM) & (row < 3 * heads)
    return jnp.where(chosen, 1.0, 0.0).astype(bf16)


def pack_pieces(values, heads):
    values = jnp.where(iota(values.shape, 1) < heads, values, 0.0)
    high = values.astype(bf16).astype(f32)
    rest = values - high
    middle = rest.astype(bf16).astype(f32)
    low = rest - middle
    packed = high + pltpu.roll(middle, heads, 1) + pltpu.roll(low, 2 * heads, 1)
    return packed.astype(bf16)


def expand(values, heads, spreader):
    return jnp.dot(pack_pieces(values, heads), spreader, preferred_element_type=f32)


def running_sum(tri, logs, heads):
    parts = jnp.dot(tri, pack_pieces(logs, heads), preferred_element_type=f32)
    total = parts + pltpu.roll(parts, LANES - heads, 1) + pltpu.roll(parts, LANES - 2 * heads, 1)
    return jnp.where(iota(total.shape, 1) < heads, total, 0.0)


def log_of(tail):
    wide = tail.astype(f32)
    return wide[0:1] + wide[1:2] + wide[2:3]


def log_rows(log):
    total = jnp.broadcast_to(log, (HALO, log.shape[1]))
    high = total.astype(bf16).astype(f32)
    middle = (total - high).astype(bf16).astype(f32)
    low = (total - high) - middle
    line = iota(total.shape, 0)
    return jnp.where(line == 0, high, jnp.where(line == 1, middle, low)).astype(bf16)


def exchange_plan(own, count):
    partners, uppers = [], []
    size = 2
    while size <= count:
        place = own % size
        base = own - place
        partners.append(base + (1 - place if size == 2 else size - 2 - place + 2 * (place % 2)))
        uppers.append(place // (size // 2) == 1)
        size *= 2
    return partners, uppers


def rows_of(k, size):
    return pl.ds(pl.multiple_of(k * size, size), size)


def layer_kernel(
    layer, count, members, with_orders,
    stream_ref, order_ref, in_gain_ref, w_in_ref, w_bc_ref, w_dt_ref, conv_x_ref, conv_bc_ref,
    small_ref, out_gain_ref, w_out_ref,
    out_ref, orders_out_ref,
    full_ref, halo_ref, orders_ref, raw_ref, w_ref, wo_ref, ext_ref, y_ref, z_ref, feed_ref,
    b_ref, c_ref, cum_ref, states_ref, sofar_exp_ref, state_ref, sofar_ref,
    end_ref, send_ref, got_ref, total_ref, prefix_ref,
    partial_ref, near_ref, sum_ref, far_ref,
    load_sem, self_sem, ag_send, ag_recv, halo_send, halo_recv, order_send, order_recv,
    ex_send, ex_recv, near_send, near_recv, far_send, far_recv,
):
    seq = lax.axis_index("seq")
    own = lax.axis_index("tp")
    chip, core = own // 2, own % 2
    near_id = chip * 2 + 1 - core
    across_id = (1 - chip) * 2 + core
    diagonal_id = (1 - chip) * 2 + 1 - core
    sibling = (seq, near_id)
    across = (seq, across_id)
    length, width = stream_ref.shape
    inner = y_ref.shape[1]
    mixed = inner + 2 * STATE
    heads = inner // HEAD_DIM
    chunks = length // ROWS
    per = ROWS // STRETCH
    blocks = length // STRETCH
    partners, uppers = exchange_plan(seq, count)
    following = (seq + 1) % count
    before = (seq + count - 1) % count

    greeted = [sibling, across]
    greeted += [(before, t) for t in range(members)]
    greeted += [(partner, own) for partner in partners]
    if with_orders:
        greeted += [((seq + d) % count, own) for d in range(1, count)]
    barrier = pltpu.get_barrier_semaphore()
    for device in greeted:
        pl.semaphore_signal(barrier, inc=1, device_id=device, device_id_type=MESH)

    loads = [
        pltpu.make_async_copy(w_in_ref.at[layer], raw_ref, load_sem.at[0]),
        pltpu.make_async_copy(
            w_bc_ref.at[layer], w_ref.at[:, inner:mixed], load_sem.at[1]
        ),
        pltpu.make_async_copy(w_out_ref.at[layer], wo_ref, load_sem.at[2]),
        pltpu.make_async_copy(stream_ref, full_ref.at[own], self_sem),
    ]
    for copy in loads:
        copy.start()

    pl.semaphore_wait(barrier, len(greeted))

    def remote(src, dst, send, recv, device):
        return pltpu.make_async_remote_copy(
            src_ref=src, dst_ref=dst, send_sem=send, recv_sem=recv,
            device_id=device, device_id_type=MESH,
        )

    def halo_copy(t):
        return remote(
            stream_ref.at[pl.ds(length - HALO, HALO)], halo_ref.at[own],
            halo_send.at[t], halo_recv.at[own], (following, t),
        )

    def halo_arrival(t):
        return remote(
            stream_ref.at[pl.ds(length - HALO, HALO)], halo_ref.at[t],
            halo_send.at[t], halo_recv.at[t], (following, t),
        )

    def across_copy(k):
        rows = rows_of(k, ROWS)
        return remote(
            stream_ref.at[rows], full_ref.at[own, rows], ag_send.at[0, k], ag_recv.at[0, k], across
        )

    def near_copy(k):
        rows = rows_of(k, ROWS)
        return remote(
            stream_ref.at[rows], full_ref.at[own, rows], ag_send.at[1, k], ag_recv.at[1, k], sibling
        )

    def forward_copy(k):
        rows = rows_of(k, ROWS)
        piece = full_ref.at[across_id, rows]
        return remote(piece, piece, ag_send.at[2, k], ag_recv.at[2, k], sibling)

    def order_copy(d):
        return remote(
            order_ref, orders_ref.at[seq], order_send.at[d - 1], order_recv.at[d - 1],
            ((seq + d) % count, own),
        )

    for t in range(members):
        halo_copy(t).start()
    for k in range(chunks):
        across_copy(k).start()
        near_copy(k).start()
    if with_orders:
        for d in range(1, count):
            order_copy(d).start()

    row = iota((2 * LANES, 2 * LANES), 0)
    col = iota((2 * LANES, 2 * LANES), 1)
    apart = jnp.where(col == 2 * (row % LANES) + row // LANES, 1.0, 0.0).astype(bf16)
    depth = w_ref.shape[0]
    dt = w_dt_ref[layer].astype(f32)
    dt = jnp.concatenate([dt, jnp.zeros((LANES - heads, depth), f32)], axis=0)
    w_ref[:, mixed + inner :] = dt.T.astype(bf16)
    loads[0].wait()

    def split_halves(i, _):
        rows = rows_of(i, LANES)
        both = raw_ref[rows].reshape(2 * LANES, inner)
        halves = jnp.dot(apart, both, preferred_element_type=f32).astype(bf16)
        w_ref[rows, 0:inner] = halves[:LANES]
        w_ref[rows, mixed : mixed + inner] = halves[LANES:]
        return 0

    lax.fori_loop(0, depth // LANES, split_halves, 0)
    loads[1].wait()
    loads[3].wait()

    gain = in_gain_ref[layer : layer + 1, :]

    def normed(v):
        wide = v.astype(f32)
        scale = lax.rsqrt(jnp.mean(wide * wide, axis=-1, keepdims=True) + epsilon)
        return (wide * scale * gain).astype(bf16)

    for t in range(members):
        halo_arrival(t).wait_recv()
    ahead = jnp.concatenate([halo_ref[t] for t in range(members)], axis=1)
    ahead = jnp.dot(normed(ahead), w_ref[:, :mixed], preferred_element_type=f32)
    ahead = ahead[HALO - 8 :, :].astype(bf16).astype(f32)
    ext_ref[0:8, :] = jnp.where(seq > 0, ahead, 0.0)
    state_ref[...] = jnp.zeros_like(state_ref)
    sofar_ref[...] = jnp.zeros_like(sofar_ref)

    spreader = spreader_of(heads, inner)
    line = iota((STRETCH, STRETCH), 0)
    lane = iota((STRETCH, STRETCH), 1)
    lower = line >= lane
    tri = jnp.where(lower, 1.0, 0.0).astype(bf16)
    small = small_ref[layer]
    bias, rate = small[0:1], small[1:2]
    skip = expand(jnp.broadcast_to(small[2:3], (8, LANES)), heads, spreader)[0:1]
    taps_x = conv_x_ref[layer]
    taps_bc = conv_bc_ref[layer]
    taps = jnp.concatenate([taps_x, taps_bc], axis=1)
    tap_count = taps.shape[0]

    def project(k, _):
        rows = rows_of(k, ROWS)
        remote(
            full_ref.at[across_id, rows], full_ref.at[across_id, rows],
            ag_send.at[0, k], ag_recv.at[0, k], across,
        ).wait_recv()
        forward_copy(k).start()
        remote(
            full_ref.at[near_id, rows], full_ref.at[near_id, rows],
            ag_send.at[1, k], ag_recv.at[1, k], sibling,
        ).wait_recv()
        remote(
            full_ref.at[diagonal_id, rows], full_ref.at[diagonal_id, rows],
            ag_send.at[2, k], ag_recv.at[2, k], sibling,
        ).wait_recv()
        tokens = jnp.concatenate([full_ref[t, rows, :] for t in range(members)], axis=1)
        projected = jnp.dot(normed(tokens), w_ref[...], preferred_element_type=f32)
        ext_ref[8 : 8 + ROWS, :] = projected[:, :mixed].astype(bf16).astype(f32)
        conv = jnp.zeros((ROWS, mixed), f32)
        for tap in range(tap_count):
            first = 9 - tap_count + tap
            conv = conv + taps[tap : tap + 1, :] * ext_ref[first : first + ROWS, :]
        conv = conv * jax.nn.sigmoid(conv)
        ext_ref[0:8, :] = ext_ref[ROWS : ROWS + 8, :]
        z_ref[rows, :] = projected[:, mixed : mixed + inner].astype(bf16)
        raw = projected[:, mixed + inner :] + bias
        step = jnp.maximum(raw, 0.0) + jnp.log1p(jnp.exp(-jnp.abs(raw)))
        logs = -step * rate
        x = conv[:, :inner]
        b_all = conv[:, inner : inner + STATE]
        b_ref[rows, :] = b_all.astype(bf16)
        c_ref[rows, :] = conv[:, inner + STATE :].astype(bf16)
        feed = x * expand(step, heads, spreader)
        feed_ref[rows, :] = feed.astype(bf16)
        y_ref[rows, :] = skip * x
        state = state_ref[...]
        sofar = sofar_ref[...]
        for block in range(per):
            part = slice(block * STRETCH, (block + 1) * STRETCH)
            index = k * per + block
            cum = running_sum(tri, logs[part], heads)
            last = cum[STRETCH - 1 : STRETCH, :]
            factors = expand(
                jnp.concatenate(
                    [jnp.exp(last - cum), jnp.exp(jnp.broadcast_to(last, (8, LANES))), jnp.exp(sofar)],
                    axis=0,
                ),
                heads, spreader,
            )
            fresh = jnp.dot(
                b_all[part].T.astype(bf16),
                (feed[part] * factors[:STRETCH]).astype(bf16),
                preferred_element_type=f32,
            )
            states_ref[index] = state
            sofar_exp_ref[index] = factors[STRETCH + 8 :]
            state = state * factors[STRETCH : STRETCH + 1] + fresh
            cum_ref[rows_of(index, STRETCH), :] = cum
            sofar = sofar + last
        state_ref[...] = state
        sofar_ref[...] = sofar
        return 0

    lax.fori_loop(0, chunks, project, 0)
    end_ref[0:STATE, :] = state_ref[...].astype(bf16)
    end_ref[STATE:, :] = log_rows(expand(sofar_ref[...], heads, spreader)[0:1])

    left = iota((STRETCH, 2 * HEAD_DIM), 1) < HEAD_DIM

    def within(block, _):
        rows = rows_of(block, STRETCH)
        cum = cum_ref[rows, :]
        cum_t = cum.T
        feed = feed_ref[rows, :]
        meet = lax.dot_general(
            c_ref[rows, :], b_ref[rows, :], (((1,), (1,)), ((), ())), preferred_element_type=f32
        )
        for pair in range(heads // 2):
            lanes = slice(pair * 2 * HEAD_DIM, (pair + 1) * 2 * HEAD_DIM)
            weights = []
            for h in (2 * pair, 2 * pair + 1):
                spread = jnp.where(lower, cum[:, h : h + 1] - cum_t[h : h + 1, :], -jnp.inf)
                weights.append((meet * jnp.exp(spread)).astype(bf16))
            fed = feed[:, lanes]
            nought = jnp.zeros_like(fed)
            stacked = jnp.concatenate(
                [jnp.where(left, fed, nought), jnp.where(left, nought, fed)], axis=0
            )
            inside = jnp.dot(
                jnp.concatenate(weights, axis=1), stacked, preferred_element_type=f32
            )
            y_ref[rows, lanes] = y_ref[rows, lanes] + inside
        return 0

    steps = len(partners)
    total_ref[...] = end_ref[:STATE, :].astype(f32)
    prefix_ref[...] = jnp.zeros_like(prefix_ref)
    total_log = log_of(end_ref[STATE:, :])
    prefix_log = jnp.zeros_like(total_log)
    sent = []
    done = 0
    for step, (partner, upper) in enumerate(zip(partners, uppers)):
        if step:
            send_ref[step - 1, :STATE, :] = total_ref[...].astype(bf16)
            send_ref[step - 1, STATE:, :] = log_rows(total_log)
        copy = remote(
            send_ref.at[step - 1] if step else end_ref, got_ref.at[step],
            ex_send.at[step], ex_recv.at[step], (partner, own),
        )
        copy.start()
        sent.append(copy)
        upto = blocks * (step + 1) // steps
        lax.fori_loop(done, upto, within, 0)
        done = upto
        copy.wait_recv()
        theirs = got_ref[step, :STATE, :].astype(f32)
        their_log = log_of(got_ref[step, STATE:, :])
        prefix = prefix_ref[...]
        prefix_ref[...] = jnp.where(upper, theirs * jnp.exp(prefix_log) + prefix, prefix)
        prefix_log = jnp.where(upper, prefix_log + their_log, prefix_log)
        if step + 1 < steps:
            mine = total_ref[...]
            first = jnp.where(upper, theirs, mine)
            then = jnp.where(upper, mine, theirs)
            total_ref[...] = first * jnp.exp(jnp.where(upper, total_log, their_log)) + then
            total_log = total_log + their_log
    if done < blocks:
        lax.fori_loop(done, blocks, within, 0)

    loads[2].wait()
    out_gain = out_gain_ref[layer : layer + 1, :]
    pair = 2 * HEAD_DIM
    one = iota((2 * pair, pair), 0) % pair // HEAD_DIM
    two = iota((2 * pair, pair), 1) // HEAD_DIM
    averager = jnp.where(one == two, 1.0 / HEAD_DIM, 0.0).astype(bf16)

    def columns(block):
        return pl.ds(pl.multiple_of(block * width, LANES), width)

    def near_part(side, k):
        rows = rows_of(k, ROWS)
        block = diagonal_id if side == 0 else near_id
        return remote(
            partial_ref.at[rows, columns(block)], near_ref.at[side, rows],
            near_send.at[side, k], near_recv.at[side, k], sibling,
        )

    def far_part(k):
        rows = rows_of(k, ROWS)
        return remote(
            sum_ref.at[rows], far_ref.at[rows], far_send.at[k], far_recv.at[k], across
        )

    def send_far(k):
        rows = rows_of(k, ROWS)
        near_part(0, k).wait_recv()
        sum_ref[rows, :] = (
            partial_ref[rows, columns(across_id)].astype(f32) + near_ref[0, rows, :].astype(f32)
        ).astype(bf16)
        far_part(k).start()

    def output(k, _):
        rows = rows_of(k, ROWS)
        grown = expand(jnp.exp(cum_ref[rows, :]), heads, spreader)
        carried = []
        for block in range(per):
            index = k * per + block
            state = states_ref[index] + prefix_ref[...] * sofar_exp_ref[index][0:1]
            carried.append(
                jnp.dot(
                    c_ref[rows_of(index, STRETCH), :], state.astype(bf16),
                    preferred_element_type=f32,
                )
            )
        gate = z_ref[rows, :].astype(f32)
        ssd = y_ref[rows, :] + jnp.concatenate(carried, axis=0) * grown
        gated = ssd * (gate * jax.nn.sigmoid(gate))
        square = gated * gated
        high = square.astype(bf16)
        low = (square - high.astype(f32)).astype(bf16)
        pieces = []
        for p in range(inner // pair):
            lanes = slice(p * pair, (p + 1) * pair)
            both = jnp.concatenate([high[:, lanes], low[:, lanes]], axis=1)
            mean = jnp.dot(both, averager, preferred_element_type=f32)
            pieces.append(
                (gated[:, lanes] * lax.rsqrt(mean + epsilon) * out_gain[:, lanes]).astype(bf16)
            )
        mixed_heads = jnp.concatenate(pieces, axis=1)
        partial_ref[rows, :] = jnp.dot(
            mixed_heads, wo_ref[...], preferred_element_type=f32
        ).astype(bf16)
        near_part(0, k).start()
        near_part(1, k).start()

        @pl.when(k > 0)
        def _():
            send_far(k - 1)

        return 0

    lax.fori_loop(0, chunks, output, 0)
    send_far(chunks - 1)

    def finish(k, _):
        rows = rows_of(k, ROWS)
        near_part(1, k).wait_recv()
        far_part(k).wait_recv()
        out_ref[rows, :] = (
            stream_ref[rows, :].astype(f32)
            + partial_ref[rows, columns(own)].astype(f32)
            + near_ref[1, rows, :].astype(f32)
            + far_ref[rows, :].astype(f32)
        ).astype(bf16)
        return 0

    lax.fori_loop(0, chunks, finish, 0)

    if with_orders:
        orders_ref[seq] = order_ref[...]
        for d in range(1, count):
            order_copy(d).wait_recv()
            order_copy(d).wait_send()
        orders_out_ref[...] = orders_ref[...]
    else:
        orders_out_ref[...] = jnp.zeros_like(orders_out_ref)
    for t in range(members):
        halo_copy(t).wait_send()

    def drain(k, _):
        across_copy(k).wait_send()
        near_copy(k).wait_send()
        forward_copy(k).wait_send()
        near_part(0, k).wait_send()
        near_part(1, k).wait_send()
        far_part(k).wait_send()
        return 0

    lax.fori_loop(0, chunks, drain, 0)
    for copy in sent:
        copy.wait_send()


def run_layer(layer, stream, order, params, with_orders):
    in_gain, w_in, w_bc, w_dt, conv_x, conv_bc, small, out_gain, w_out = params
    count, members = lax.axis_size("seq"), lax.axis_size("tp")
    steps = count.bit_length() - 1
    length, width = stream.shape
    inner = w_out.shape[1]
    heads = inner // HEAD_DIM
    mixed = inner + 2 * STATE
    depth = w_in.shape[1]
    chunks = length // ROWS
    blocks = length // STRETCH
    peers = max(count - 1, 1)
    vmem = pl.BlockSpec(memory_space=pltpu.VMEM)
    hbm = pl.BlockSpec(memory_space=pl.ANY)
    dma = pltpu.SemaphoreType.DMA
    return pl.pallas_call(
        functools.partial(layer_kernel, layer, count, members, with_orders),
        in_specs=[vmem, vmem, vmem, hbm, hbm, vmem, vmem, vmem, vmem, vmem, hbm],
        out_specs=[vmem, vmem],
        out_shape=[
            jax.ShapeDtypeStruct(stream.shape, bf16),
            jax.ShapeDtypeStruct((count if with_orders else 1, 1, length), jnp.int32),
        ],
        scratch_shapes=[
            pltpu.VMEM((members, length, width), bf16),
            pltpu.VMEM((members, HALO, width), bf16),
            pltpu.VMEM((count, 1, length), jnp.int32),
            pltpu.VMEM((depth, 2, inner), bf16),
            pltpu.VMEM((depth, mixed + inner + LANES), bf16),
            pltpu.VMEM((inner, depth), bf16),
            pltpu.VMEM((ROWS + 8, mixed), f32),
            pltpu.VMEM((length, inner), f32),
            pltpu.VMEM((length, inner), bf16),
            pltpu.VMEM((length, inner), bf16),
            pltpu.VMEM((length, STATE), bf16),
            pltpu.VMEM((length, STATE), bf16),
            pltpu.VMEM((length, LANES), f32),
            pltpu.VMEM((blocks, STATE, inner), f32),
            pltpu.VMEM((blocks, 8, inner), f32),
            pltpu.VMEM((STATE, inner), f32),
            pltpu.VMEM((8, LANES), f32),
            pltpu.VMEM((STATE + HALO, inner), bf16),
            pltpu.VMEM((max(steps - 1, 1), STATE + HALO, inner), bf16),
            pltpu.VMEM((steps, STATE + HALO, inner), bf16),
            pltpu.VMEM((STATE, inner), f32),
            pltpu.VMEM((STATE, inner), f32),
            pltpu.VMEM((length, depth), bf16),
            pltpu.VMEM((2, length, width), bf16),
            pltpu.VMEM((length, width), bf16),
            pltpu.VMEM((length, width), bf16),
            dma((3,)), dma, dma((3, chunks)), dma((3, chunks)),
            dma((members,)), dma((members,)), dma((peers,)), dma((peers,)),
            dma((steps,)), dma((steps,)), dma((2, chunks)), dma((2, chunks)),
            dma((chunks,)), dma((chunks,)),
        ],
        compiler_params=pltpu.CompilerParams(
            collective_id=layer, has_side_effects=True, vmem_limit_bytes=60 * 1024 * 1024
        ),
        name="mixer_layer_" + str(layer),
    )(stream, order, in_gain, w_in, w_bc, w_dt, conv_x, conv_bc, small, out_gain, w_out)


def plan_kernel(source_ref, local_ref, mine_ref, hand_ref, place_ref):
    own = lax.axis_index("seq")
    count, length = source_ref.shape
    share = length // count
    line = lax.broadcasted_iota(jnp.int32, (length, length), 0)
    lane = lax.broadcasted_iota(jnp.int32, (length, length), 1)
    upto = (line <= lane).astype(bf16)
    device = lax.broadcasted_iota(jnp.int32, (count, length), 0)

    def slots(member):
        ones = jnp.where(member, 1.0, 0.0)
        counted = jnp.dot(ones.astype(bf16), upto, preferred_element_type=f32)
        return jnp.where(member, counted.astype(jnp.int32) - 1, -1)

    slot = slots(source_ref[...] == own)
    short = lax.broadcasted_iota(jnp.int32, (share, length), 0)
    wide = lax.broadcasted_iota(jnp.int32, (share, length), 1)
    for d in range(count):
        chosen = slot[d : d + 1, :] == short
        local = jnp.where(chosen, local_ref[d : d + 1, :], 0).astype(f32)
        wanted = jnp.sum(local, axis=1, keepdims=True).astype(jnp.int32)
        hand_ref[d * share : (d + 1) * share, :] = jnp.where(wanted == wide, 1.0, 0.0).astype(bf16)
    from_each = mine_ref[...] == device
    arrived = jnp.where(from_each, slots(from_each) + share * device, 0).astype(f32)
    target = jnp.sum(arrived, axis=0, keepdims=True).astype(jnp.int32)
    place_ref[...] = jnp.where(line == target, 1.0, 0.0).astype(bf16)


def reorder_plans(col_order, orders):
    length = col_order.shape[0]
    vmem = pl.BlockSpec(memory_space=pltpu.VMEM)
    plan = jax.ShapeDtypeStruct((length, length), bf16)
    return pl.pallas_call(
        plan_kernel,
        in_specs=[vmem] * 3,
        out_specs=[vmem] * 2,
        out_shape=[plan, plan],
        compiler_params=pltpu.CompilerParams(vmem_limit_bytes=40 * 1024 * 1024),
        name="reorder_plans",
    )(orders // length, orders % length, (col_order // length)[None])


def pick(plan, rows):
    return jnp.dot(plan, rows, preferred_element_type=f32).astype(bf16)


def reorder_rows(stream, plans):
    hand, place = plans
    arrived = lax.all_to_all(pick(hand, stream), "seq", split_axis=0, concat_axis=0, tiled=True)
    return lax.dot_general(
        place, arrived, (((0,), (0,)), ((), ())), preferred_element_type=f32
    ).astype(bf16)


def body(
    tokens, col_order, in_gain, w_in, w_bc, w_dt, conv_x, conv_bc,
    dt_bias, a_log, d_skip, out_gain, w_out,
):
    small = jnp.stack([dt_bias, jnp.exp(a_log), d_skip], axis=1)
    small = jnp.pad(small, ((0, 0), (0, 0), (0, LANES - small.shape[2])))
    params = (
        in_gain, w_in, w_bc, jnp.swapaxes(w_dt, 1, 2), conv_x, conv_bc, small, out_gain, w_out
    )
    order = col_order[None]
    row_result, orders = run_layer(0, tokens, order, params, True)
    plans = reorder_plans(col_order, orders[:, 0])
    own_rows = reorder_rows(row_result, plans)
    return run_layer(1, own_rows, order, params, False)[0]


def solution(mesh):
    placed = (
        P("seq", "tp"),
        P("seq"),
        P(),
        P(None, None, None, "tp"),
        P(),
        P(None, None, "tp"),
        P(None, None, "tp"),
        P(),
        P(None, "tp"),
        P(None, "tp"),
        P(None, "tp"),
        P(None, "tp"),
        P(None, "tp", None),
    )
    return jax.shard_map(
        body, mesh=mesh, in_specs=placed, out_specs=P("seq", "tp"), check_vma=False
    )
```

time: 332 us -> 204 us (0.61)
  local copies, waits for them, and re-layouts: 50.2 us -> 2.94 us
  blocking collectives: 75.7 us -> 30.2 us
  waiting for transfers between devices: 23.9 us -> 0 us
  between operations: 13.7 us -> 0.04 us
  Pallas kernels: 151 us -> 162 us
  starting transfers between devices: 6.77 us -> 0 us
  other arithmetic: 6.5 us -> 2.79 us
    all_gather x3 -> x0, blocking collectives: 43.5 us -> none  [the longest x1 32.5 us: body(): orders = lax.all_gather(col_order, 'seq', axis=0)]
    all_gather x2 -> x0, waiting for transfers between devices: 22.4 us -> none  [spread_features(): return lax.all_gather(piece, 'tp', axis=1, tiled=True)]
    unnamed x59 -> x1, local copies, waits for them, and re-layouts: 24.5 us -> 2.26 us
    slice x6 -> x0, local copies, waits for them, and re-layouts: 14 us -> none  [the longest x1 11.8 us: layer(): w_in[which, :, 0]]
    pallas_call x8 -> x2, Pallas kernels: 148 us -> 160 us  [run_layer(): pl.pallas_call(functools.partial(layer_kernel, layer, count, members, wit...]
    squeeze x8 -> x0, local copies, waits for them, and re-layouts: 10.9 us -> none  [the longest x1 4.13 us: layer(): w_out[which]]
    ppermute x2 -> x0, starting transfers between devices: 6.73 us -> none  [halo_rows(): lax.ppermute(tail, 'seq', [(i, i + 1) for i in range(count - 1)])]
    concatenate x3 -> x0, other arithmetic: 5.78 us -> none  [the longest x2 5.77 us: layer(): jnp.concatenate([w_in[which, :, 0], w_bc[which], w_in[which, :, 1], jnp.p...]
  transfers between devices with their start and end apart: 4 -> 0, of which waited for: 2 -> 0; matrix products, arithmetic and copies ran while one was open for 10% -> 0% of each run, Pallas kernels for 1% -> 0%
where the time goes in v1:
time: 204 us; the launch traced here: 203 us
  Pallas kernels  162 us (79%)
  blocking collectives  30.2 us (15%)
  matrix products  4.71 us (2%)
  local copies, waits for them, and re-layouts  2.94 us (1%)
  other arithmetic  2.79 us (1%)
    pallas_call x2, Pallas kernels, run_layer(): pl.pallas_call(functools.partial(layer_kernel, layer, count, members, wit...  160 us
    all_to_all x1, blocking collectives, reorder_rows(): lax.all_to_all(pick(hand, stream), 'seq', split_axis=0, concat_axis=0, ti...  30.2 us

profile of v1, /device:TPU:0, one launch (start us, length us, event | category | flops | bytes accessed | tf_op | source)
XLA Modules:
  0.0 202.8 jit_solution(17663644348484558930)
XLA Ops:
  0.0 0.7 exp.3
  0.7 0.7 add_select_fusion.2
  1.4 1.3 select_maximum_fusion.small_ref
  2.7 82.1 %mixer_layer_0.1 = (bf16[1024,512]{1,0:T(8,128)(2,1)}, s32[8,1,1024]{2,1,0:T(1,128)}) custom-call(bf16[1024,512]{1,0:T(8,128)(2,1)} %stream_ref.1, s32[1,1024]{1,0:T(1,128)} %bitcast.49, f32[2,2048]{1,0:T(2,128)} %in_gain_ref.3, bf16[2,2048,2,512]{3,2,1,0:T(2,128)(2,1)} %w_in_ref.3, bf16[2,2048,256]{2,1,0:T(8,128)(2,1)} %w_bc_ref.3, ...), custom_call_target="tpu_custom_call" | custom-call | tf_op jit(solution)/shard_map/mixer_layer_0/pallas_call | solution.py:495
  84.8 0.8 add_select_fusion
  85.6 2.3 %reorder_plans.1 = (bf16[1024,1024]{1,0:T(8,128)(2,1)S(1)}, bf16[1024,1024]{1,0:T(8,128)(2,1)S(1)}) custom-call(s32[8,1024]{1,0:T(8,128)S(1)} %get-tuple-element.16.source_ref, s32[8,1024]{1,0:T(8,128)S(1)} %get-tuple-element.15.local_ref, s32[1,1024]{1,0:T(1,128)S(1)} %bitcast.44), custom_call_target="tpu_custom_call" | custom-call | tf_op jit(solution)/shard_map/reorder_plans/pallas_call | solution.py:574
  88.0 2.5 %convolution_convert_fusion.1 = bf16[1024,512]{1,0:T(8,128)(2,1)S(1)} fusion(bf16[1024,1024]{1,0:T(8,128)(2,1)S(1)} %get-tuple-element.12, bf16[1024,512]{1,0:T(8,128)(2,1)} %get-tuple-element.13), kind=kOutput, calls=%fused_computation.1 | convolution fusion | flops 1074266112 | bytes 4194304 | tf_op jit(solution)/shard_map/dot_general | solution.py:585
  90.4 30.2 %all_to_all.12 = bf16[8,128,512]{2,1,0:T(8,128)(2,1)S(1)} all-to-all(bf16[8,128,512]{2,1,0:T(8,128)(2,1)S(1)} %bitcast.46), channel_id=1, replica_groups=mesh['seq'=8,'tp'=4] {'seq'}, dimensions={0} | all-to-all | bytes 2097152 | tf_op jit(solution)/shard_map/all_to_all | solution.py:590
  120.6 2.2 %convolution_convert_fusion.stream_ref = bf16[1024,512]{1,0:T(8,128)(2,1)} fusion(bf16[1024,1024]{1,0:T(8,128)(2,1)S(1)} %get-tuple-element.11, bf16[1024,512]{1,0:T(8,128)(2,1)S(1)} %bitcast.45), kind=kOutput, calls=%fused_computation | convolution fusion | flops 1074266112 | bytes 4194304 | tf_op jit(solution)/shard_map/dot_general | solution.py:591
  122.9 77.7 %mixer_layer_1.1 = (bf16[1024,512]{1,0:T(8,128)(2,1)}, s32[1,1,1024]{2,1,0:T(1,128)}) custom-call(bf16[1024,512]{1,0:T(8,128)(2,1)} %convolution_convert_fusion.stream_ref, s32[1,1024]{1,0:T(1,128)} %bitcast.50, f32[2,2048]{1,0:T(2,128)} %in_gain_ref.3, bf16[2,2048,2,512]{3,2,1,0:T(2,128)(2,1)} %w_in_ref.3, bf16[2,2048,256]{2,1,0:T(8,128)(2,1)} %w_bc_ref.3, ...), custom_call_target="tpu_custom_call" | custom-call | tf_op jit(solution)/shard_map/mixer_layer_1/pallas_call | solution.py:495
  200.6 2.3 %copy.38 = bf16[1024,512]{1,0:T(8,128)(2,1)} copy(bf16[1024,512]{1,0:T(8,128)(2,1)} %get-tuple-element.14) | data formatting | bytes 2097152

commit v2 on v1

--- a/solution.py
+++ b/solution.py
@@ -13,6 +13,7 @@
 LANES = 128
 HALO = 16
 ROWS = 256
+COLUMNS = 128
 
 epsilon = 1e-05
 f32 = jnp.float32
@@ -82,16 +83,18 @@
 
 
 def layer_kernel(
-    layer, count, members, with_orders,
+    layer, count, members, reorder,
     stream_ref, order_ref, in_gain_ref, w_in_ref, w_bc_ref, w_dt_ref, conv_x_ref, conv_bc_ref,
     small_ref, out_gain_ref, w_out_ref,
-    out_ref, orders_out_ref,
+    out_ref,
     full_ref, halo_ref, orders_ref, raw_ref, w_ref, wo_ref, ext_ref, y_ref, z_ref, feed_ref,
     b_ref, c_ref, cum_ref, states_ref, sofar_exp_ref, state_ref, sofar_ref,
     end_ref, send_ref, got_ref, total_ref, prefix_ref,
     partial_ref, near_ref, sum_ref, far_ref,
+    mixed_ref, hand_ref, place_ref, leaving_ref, arrived_ref,
     load_sem, self_sem, ag_send, ag_recv, halo_send, halo_recv, order_send, order_recv,
     ex_send, ex_recv, near_send, near_recv, far_send, far_recv,
+    move_send, move_recv,
 ):
     seq = lax.axis_index("seq")
     own = lax.axis_index("tp")
@@ -115,7 +118,7 @@
     greeted = [sibling, across]
     greeted += [(before, t) for t in range(members)]
     greeted += [(partner, own) for partner in partners]
-    if with_orders:
+    if reorder:
         greeted += [((seq + d) % count, own) for d in range(1, count)]
     barrier = pltpu.get_barrier_semaphore()
     for device in greeted:
@@ -126,9 +129,22 @@
         pltpu.make_async_copy(
             w_bc_ref.at[layer], w_ref.at[:, inner:mixed], load_sem.at[1]
         ),
-        pltpu.make_async_copy(w_out_ref.at[layer], wo_ref, load_sem.at[2]),
         pltpu.make_async_copy(stream_ref, full_ref.at[own], self_sem),
     ]
+    if reorder:
+        pieces = width // COLUMNS
+        for j in range(pieces):
+            for t in range(members):
+                first = t * width + j * COLUMNS
+                loads.append(
+                    pltpu.make_async_copy(
+                        w_out_ref.at[layer, :, first : first + COLUMNS],
+                        wo_ref.at[:, (j * members + t) * COLUMNS : (j * members + t + 1) * COLUMNS],
+                        load_sem.at[2 + j * members + t],
+                    )
+                )
+    else:
+        loads.append(pltpu.make_async_copy(w_out_ref.at[layer], wo_ref, load_sem.at[2]))
     for copy in loads:
         copy.start()
 
@@ -180,7 +196,7 @@
     for k in range(chunks):
         across_copy(k).start()
         near_copy(k).start()
-    if with_orders:
+    if reorder:
         for d in range(1, count):
             order_copy(d).start()
 
@@ -203,7 +219,7 @@
 
     lax.fori_loop(0, depth // LANES, split_halves, 0)
     loads[1].wait()
-    loads[3].wait()
+    loads[2].wait()
 
     gain = in_gain_ref[layer : layer + 1, :]
 
@@ -363,39 +379,15 @@
     if done < blocks:
         lax.fori_loop(done, blocks, within, 0)
 
-    loads[2].wait()
+    for copy in loads[3:]:
+        copy.wait()
     out_gain = out_gain_ref[layer : layer + 1, :]
     pair = 2 * HEAD_DIM
     one = iota((2 * pair, pair), 0) % pair // HEAD_DIM
     two = iota((2 * pair, pair), 1) // HEAD_DIM
     averager = jnp.where(one == two, 1.0 / HEAD_DIM, 0.0).astype(bf16)
 
-    def columns(block):
-        return pl.ds(pl.multiple_of(block * width, LANES), width)
-
-    def near_part(side, k):
-        rows = rows_of(k, ROWS)
-        block = diagonal_id if side == 0 else near_id
-        return remote(
-            partial_ref.at[rows, columns(block)], near_ref.at[side, rows],
-            near_send.at[side, k], near_recv.at[side, k], sibling,
-        )
-
-    def far_part(k):
-        rows = rows_of(k, ROWS)
-        return remote(
-            sum_ref.at[rows], far_ref.at[rows], far_send.at[k], far_recv.at[k], across
-        )
-
-    def send_far(k):
-        rows = rows_of(k, ROWS)
-        near_part(0, k).wait_recv()
-        sum_ref[rows, :] = (
-            partial_ref[rows, columns(across_id)].astype(f32) + near_ref[0, rows, :].astype(f32)
-        ).astype(bf16)
-        far_part(k).start()
-
-    def output(k, _):
+    def mixed_of(k):
         rows = rows_of(k, ROWS)
         grown = expand(jnp.exp(cum_ref[rows, :]), heads, spreader)
         carried = []
@@ -422,10 +414,47 @@
             pieces.append(
                 (gated[:, lanes] * lax.rsqrt(mean + epsilon) * out_gain[:, lanes]).astype(bf16)
             )
-        mixed_heads = jnp.concatenate(pieces, axis=1)
-        partial_ref[rows, :] = jnp.dot(
-            mixed_heads, wo_ref[...], preferred_element_type=f32
+        return jnp.concatenate(pieces, axis=1)
+
+    size, wide = (length, COLUMNS) if reorder else (ROWS, width)
+    parts = (length // size) * (width // wide)
+
+    def columns(k, block):
+        place = (k * members + block) if reorder else block
+        return pl.ds(pl.multiple_of(place * wide, LANES), wide)
+
+    def rows_in(k):
+        return pl.ds(0, length) if reorder else rows_of(k, ROWS)
+
+    def near_part(side, k):
+        block = diagonal_id if side == 0 else near_id
+        return remote(
+            partial_ref.at[rows_in(k), columns(k, block)], near_ref.at[side, k],
+            near_send.at[side, k], near_recv.at[side, k], sibling,
+        )
+
+    def far_part(k):
+        return remote(sum_ref.at[k], far_ref.at[k], far_send.at[k], far_recv.at[k], across)
+
+    def send_far(k):
+        near_part(0, k).wait_recv()
+        sum_ref[k] = (
+            partial_ref[rows_in(k), columns(k, across_id)].astype(f32)
+            + near_ref[0, k].astype(f32)
         ).astype(bf16)
+        far_part(k).start()
+
+    def summed(k, stream):
+        near_part(1, k).wait_recv()
+        far_part(k).wait_recv()
+        return (
+            stream.astype(f32)
+            + partial_ref[rows_in(k), columns(k, own)].astype(f32)
+            + near_ref[1, k].astype(f32)
+            + far_ref[k].astype(f32)
+        ).astype(bf16)
+
+    def send_near(k):
         near_part(0, k).start()
         near_part(1, k).start()
 
@@ -433,33 +462,145 @@
         def _():
             send_far(k - 1)
 
-        return 0
-
-    lax.fori_loop(0, chunks, output, 0)
-    send_far(chunks - 1)
-
-    def finish(k, _):
-        rows = rows_of(k, ROWS)
-        near_part(1, k).wait_recv()
-        far_part(k).wait_recv()
-        out_ref[rows, :] = (
-            stream_ref[rows, :].astype(f32)
-            + partial_ref[rows, columns(own)].astype(f32)
-            + near_ref[1, rows, :].astype(f32)
-            + far_ref[rows, :].astype(f32)
-        ).astype(bf16)
-        return 0
-
-    lax.fori_loop(0, chunks, finish, 0)
-
-    if with_orders:
-        orders_ref[seq] = order_ref[...]
+    if reorder:
+
+        def mix(k, _):
+            mixed_ref[rows_of(k, ROWS), :] = mixed_of(k)
+            return 0
+
+        lax.fori_loop(0, chunks, mix, 0)
+
+        def output(j, _):
+            lanes = pl.ds(pl.multiple_of(j * members * wide, LANES), members * wide)
+
+            def product(k, _):
+                rows = rows_of(k, ROWS)
+                partial_ref[rows, lanes] = jnp.dot(
+                    mixed_ref[rows, :], wo_ref[:, lanes], preferred_element_type=f32
+                ).astype(bf16)
+                return 0
+
+            lax.fori_loop(0, chunks, product, 0)
+            send_near(j)
+            return 0
+
+        lax.fori_loop(0, parts, output, 0)
+        send_far(parts - 1)
+
+        share = length // count
+        shift = length.bit_length() - 1
         for d in range(1, count):
             order_copy(d).wait_recv()
+        orders_ref[seq] = order_ref[...]
+        orders = jnp.concatenate([orders_ref[d] for d in range(count)], axis=0)
+
+        def count_up(r, _):
+            first = iota((LANES, length), 0) + r * LANES
+            place_ref[rows_of(r, LANES), :] = jnp.where(
+                first <= iota((LANES, length), 1), 1.0, 0.0
+            ).astype(bf16)
+            return 0
+
+        lax.fori_loop(0, length // LANES, count_up, 0)
+        device = iota((count, length), 0)
+        wanted_here = jnp.right_shift(orders, shift) == seq
+        from_each = jnp.right_shift(order_ref[...], shift) == device
+        ones = jnp.concatenate(
+            [jnp.where(wanted_here, 1.0, 0.0), jnp.where(from_each, 1.0, 0.0)], axis=0
+        ).astype(bf16)
+        counted = jnp.dot(ones, place_ref[...], preferred_element_type=f32).astype(jnp.int32) - 1
+        slot = jnp.where(wanted_here, counted[:count], -1)
+        local = jnp.bitwise_and(orders, length - 1)
+        short = iota((share, length), 0)
+        long = iota((share, length), 1)
+        for d in range(count):
+            chosen = slot[d : d + 1, :] == short
+            found = jnp.where(chosen, local[d : d + 1, :], 0).astype(f32)
+            wanted = jnp.sum(found, axis=1, keepdims=True).astype(jnp.int32)
+            hand_ref[d * share : (d + 1) * share, :] = jnp.where(
+                wanted == long, 1.0, 0.0
+            ).astype(bf16)
+        target = jnp.where(from_each, counted[count:] + share * device, 0).astype(f32)
+        target = jnp.sum(target, axis=0, keepdims=True)
+        target = jnp.broadcast_to(target, (LANES, length)).T.astype(jnp.int32)
+        for c in range(length // LANES):
+            place_ref[:, c * LANES : (c + 1) * LANES] = jnp.where(
+                target == iota((length, LANES), 1) + c * LANES, 1.0, 0.0
+            ).astype(bf16)
+
+        def move_copy(j, d):
+            other = (seq + d) % count
+            return remote(
+                leaving_ref.at[j, rows_of(other, share)], arrived_ref.at[j, rows_of(seq, share)],
+                move_send.at[j, d - 1], move_recv.at[j, d - 1], (other, own),
+            )
+
+        def move_arrival(j, d):
+            other = (seq + count - d) % count
+            return remote(
+                leaving_ref.at[j, rows_of(other, share)], arrived_ref.at[j, rows_of(other, share)],
+                move_send.at[j, d - 1], move_recv.at[j, d - 1], ((seq + d) % count, own),
+            )
+
+        def hand_over(j):
+            lanes = slice(j * wide, (j + 1) * wide)
+            held = summed(j, stream_ref[:, lanes])
+            leaving_ref[j] = jnp.dot(
+                hand_ref[...], held, preferred_element_type=f32
+            ).astype(bf16)
+
+            def send(d, _):
+                move_copy(j, d).start()
+                return 0
+
+            lax.fori_loop(1, count, send, 0)
+            arrived_ref[j, rows_of(seq, share), :] = leaving_ref[j, rows_of(seq, share), :]
+
+        def put(j):
+            lanes = slice(j * wide, (j + 1) * wide)
+
+            def arrive(d, _):
+                move_arrival(j, d).wait_recv()
+                return 0
+
+            lax.fori_loop(1, count, arrive, 0)
+            out_ref[:, lanes] = jnp.dot(
+                place_ref[...], arrived_ref[j], preferred_element_type=f32
+            ).astype(bf16)
+
+        for j in range(parts):
+            hand_over(j)
+            if j:
+                put(j - 1)
+        put(parts - 1)
+
+        def moved(d, _):
+            for j in range(parts):
+                move_copy(j, d).wait_send()
+            return 0
+
+        lax.fori_loop(1, count, moved, 0)
+        for d in range(1, count):
             order_copy(d).wait_send()
-        orders_out_ref[...] = orders_ref[...]
     else:
-        orders_out_ref[...] = jnp.zeros_like(orders_out_ref)
+
+        def output(k, _):
+            partial_ref[rows_of(k, ROWS), :] = jnp.dot(
+                mixed_of(k), wo_ref[...], preferred_element_type=f32
+            ).astype(bf16)
+            send_near(k)
+            return 0
+
+        lax.fori_loop(0, parts, output, 0)
+        send_far(parts - 1)
+
+        def finish(k, _):
+            rows = rows_of(k, ROWS)
+            out_ref[rows, :] = summed(k, stream_ref[rows, :])
+            return 0
+
+        lax.fori_loop(0, parts, finish, 0)
+
     for t in range(members):
         halo_copy(t).wait_send()
 
@@ -467,17 +608,22 @@
         across_copy(k).wait_send()
         near_copy(k).wait_send()
         forward_copy(k).wait_send()
+        return 0
+
+    lax.fori_loop(0, chunks, drain, 0)
+
+    def drain_sums(k, _):
         near_part(0, k).wait_send()
         near_part(1, k).wait_send()
         far_part(k).wait_send()
         return 0
 
-    lax.fori_loop(0, chunks, drain, 0)
+    lax.fori_loop(0, parts, drain_sums, 0)
     for copy in sent:
         copy.wait_send()
 
 
-def run_layer(layer, stream, order, params, with_orders):
+def run_layer(layer, stream, order, params, reorder):
     in_gain, w_in, w_bc, w_dt, conv_x, conv_bc, small, out_gain, w_out = params
     count, members = lax.axis_size("seq"), lax.axis_size("tp")
     steps = count.bit_length() - 1
@@ -489,17 +635,18 @@
     chunks = length // ROWS
     blocks = length // STRETCH
     peers = max(count - 1, 1)
+    size, wide = (length, COLUMNS) if reorder else (ROWS, width)
+    parts = (length // size) * (width // wide)
+    plan = (length, length) if reorder else (16, LANES)
+    moving = (parts, length, wide) if reorder else (1, 16, LANES)
     vmem = pl.BlockSpec(memory_space=pltpu.VMEM)
     hbm = pl.BlockSpec(memory_space=pl.ANY)
     dma = pltpu.SemaphoreType.DMA
     return pl.pallas_call(
-        functools.partial(layer_kernel, layer, count, members, with_orders),
+        functools.partial(layer_kernel, layer, count, members, reorder),
         in_specs=[vmem, vmem, vmem, hbm, hbm, vmem, vmem, vmem, vmem, vmem, hbm],
-        out_specs=[vmem, vmem],
-        out_shape=[
-            jax.ShapeDtypeStruct(stream.shape, bf16),
-            jax.ShapeDtypeStruct((count if with_orders else 1, 1, length), jnp.int32),
-        ],
+        out_specs=vmem,
+        out_shape=jax.ShapeDtypeStruct(stream.shape, bf16),
         scratch_shapes=[
             pltpu.VMEM((members, length, width), bf16),
             pltpu.VMEM((members, HALO, width), bf16),
@@ -524,73 +671,22 @@
             pltpu.VMEM((STATE, inner), f32),
             pltpu.VMEM((STATE, inner), f32),
             pltpu.VMEM((length, depth), bf16),
-            pltpu.VMEM((2, length, width), bf16),
-            pltpu.VMEM((length, width), bf16),
-            pltpu.VMEM((length, width), bf16),
-            dma((3,)), dma, dma((3, chunks)), dma((3, chunks)),
+            pltpu.VMEM((2, parts, size, wide), bf16),
+            pltpu.VMEM((parts, size, wide), bf16),
+            pltpu.VMEM((parts, size, wide), bf16),
+            pltpu.VMEM((length, inner) if reorder else (16, LANES), bf16),
+            pltpu.VMEM(plan, bf16), pltpu.VMEM(plan, bf16),
+            pltpu.VMEM(moving, bf16), pltpu.VMEM(moving, bf16),
+            dma((2 + (parts * members if reorder else 1),)), dma, dma((3, chunks)), dma((3, chunks)),
             dma((members,)), dma((members,)), dma((peers,)), dma((peers,)),
-            dma((steps,)), dma((steps,)), dma((2, chunks)), dma((2, chunks)),
-            dma((chunks,)), dma((chunks,)),
+            dma((steps,)), dma((steps,)), dma((2, parts)), dma((2, parts)),
+            dma((parts,)), dma((parts,)), dma((parts, peers)), dma((parts, peers)),
         ],
         compiler_params=pltpu.CompilerParams(
             collective_id=layer, has_side_effects=True, vmem_limit_bytes=60 * 1024 * 1024
         ),
         name="mixer_layer_" + str(layer),
     )(stream, order, in_gain, w_in, w_bc, w_dt, conv_x, conv_bc, small, out_gain, w_out)
-
-
-def plan_kernel(source_ref, local_ref, mine_ref, hand_ref, place_ref):
-    own = lax.axis_index("seq")
-    count, length = source_ref.shape
-    share = length // count
-    line = lax.broadcasted_iota(jnp.int32, (length, length), 0)
-    lane = lax.broadcasted_iota(jnp.int32, (length, length), 1)
-    upto = (line <= lane).astype(bf16)
-    device = lax.broadcasted_iota(jnp.int32, (count, length), 0)
-
-    def slots(member):
-        ones = jnp.where(member, 1.0, 0.0)
-        counted = jnp.dot(ones.astype(bf16), upto, preferred_element_type=f32)
-        return jnp.where(member, counted.astype(jnp.int32) - 1, -1)
-
-    slot = slots(source_ref[...] == own)
-    short = lax.broadcasted_iota(jnp.int32, (share, length), 0)
-    wide = lax.broadcasted_iota(jnp.int32, (share, length), 1)
-    for d in range(count):
-        chosen = slot[d : d + 1, :] == short
-        local = jnp.where(chosen, local_ref[d : d + 1, :], 0).astype(f32)
-        wanted = jnp.sum(local, axis=1, keepdims=True).astype(jnp.int32)
-        hand_ref[d * share : (d + 1) * share, :] = jnp.where(wanted == wide, 1.0, 0.0).astype(bf16)
-    from_each = mine_ref[...] == device
-    arrived = jnp.where(from_each, slots(from_each) + share * device, 0).astype(f32)
-    target = jnp.sum(arrived, axis=0, keepdims=True).astype(jnp.int32)
-    place_ref[...] = jnp.where(line == target, 1.0, 0.0).astype(bf16)
-
-
-def reorder_plans(col_order, orders):
-    length = col_order.shape[0]
-    vmem = pl.BlockSpec(memory_space=pltpu.VMEM)
-    plan = jax.ShapeDtypeStruct((length, length), bf16)
-    return pl.pallas_call(
-        plan_kernel,
-        in_specs=[vmem] * 3,
-        out_specs=[vmem] * 2,
-        out_shape=[plan, plan],
-        compiler_params=pltpu.CompilerParams(vmem_limit_bytes=40 * 1024 * 1024),
-        name="reorder_plans",
-    )(orders // length, orders % length, (col_order // length)[None])
-
-
-def pick(plan, rows):
-    return jnp.dot(plan, rows, preferred_element_type=f32).astype(bf16)
-
-
-def reorder_rows(stream, plans):
-    hand, place = plans
-    arrived = lax.all_to_all(pick(hand, stream), "seq", split_axis=0, concat_axis=0, tiled=True)
-    return lax.dot_general(
-        place, arrived, (((0,), (0,)), ((), ())), preferred_element_type=f32
-    ).astype(bf16)
 
 
 def body(
@@ -603,10 +699,8 @@
         in_gain, w_in, w_bc, jnp.swapaxes(w_dt, 1, 2), conv_x, conv_bc, small, out_gain, w_out
     )
     order = col_order[None]
-    row_result, orders = run_layer(0, tokens, order, params, True)
-    plans = reorder_plans(col_order, orders[:, 0])
-    own_rows = reorder_rows(row_result, plans)
-    return run_layer(1, own_rows, order, params, False)[0]
+    own_rows = run_layer(0, tokens, order, params, True)
+    return run_layer(1, own_rows, order, params, False)
 
 
 def solution(mesh):

time: 204 us -> 179 us (0.88)
  blocking collectives: 30.2 us -> 0 us
  Pallas kernels: 162 us -> 175 us
  matrix products: 4.71 us -> 0 us
    all_to_all x1 -> x0, blocking collectives: 30.2 us -> none  [reorder_rows(): lax.all_to_all(pick(hand, stream), 'seq', split_axis=0, concat_axis=0, ti...]
    pallas_call x3 -> x2, Pallas kernels: 162 us -> 175 us  [run_layer(): pl.pallas_call(functools.partial(layer_kernel, layer, count, members, reo...]
    dot_general x2 -> x0, matrix products: 4.71 us -> none  [the longest x1 2.46 us: pick(): return jnp.dot(plan, rows, preferred_element_type=f32).astype(bf16)]
where the time goes in v2:
time: 179 us
  Pallas kernels  175 us (98%)
  local copies, waits for them, and re-layouts  2.94 us (2%)
    pallas_call x2, Pallas kernels, run_layer(): pl.pallas_call(functools.partial(layer_kernel, layer, count, members, reo...  175 us

profile of v2, /device:TPU:0, one launch (start us, length us, event | category | flops | bytes accessed | tf_op | source)
XLA Modules:
  0.0 178.9 jit_solution(4682566571954687103)
XLA Ops:
  0.0 0.7 exp.3
  0.7 1.3 select_maximum_fusion.small_ref
  2.0 94.6 %mixer_layer_0.1.stream_ref = bf16[1024,512]{1,0:T(8,128)(2,1)} custom-call(bf16[1024,512]{1,0:T(8,128)(2,1)} %stream_ref.1, s32[1,1024]{1,0:T(1,128)} %bitcast.13, f32[2,2048]{1,0:T(2,128)} %in_gain_ref.3, bf16[2,2048,2,512]{3,2,1,0:T(2,128)(2,1)} %w_in_ref.3, bf16[2,2048,256]{2,1,0:T(8,128)(2,1)} %w_bc_ref.3, bf16[2,8,2048]{2,1,0:T(8,128)(2,1)} %bitcast.11, ...), custom_call_target="tpu_custom_call" | custom-call | tf_op jit(solution)/shard_map/mixer_layer_0/pallas_call | solution.py:645
  96.6 80.0 %mixer_layer_1.1 = bf16[1024,512]{1,0:T(8,128)(2,1)} custom-call(bf16[1024,512]{1,0:T(8,128)(2,1)} %mixer_layer_0.1.stream_ref, s32[1,1024]{1,0:T(1,128)} %bitcast.14, f32[2,2048]{1,0:T(2,128)} %in_gain_ref.3, bf16[2,2048,2,512]{3,2,1,0:T(2,128)(2,1)} %w_in_ref.3, bf16[2,2048,256]{2,1,0:T(8,128)(2,1)} %w_bc_ref.3, bf16[2,8,2048]{2,1,0:T(8,128)(2,1)} %bitcast.12, ...), custom_call_target="tpu_custom_call" | custom-call | tf_op jit(solution)/shard_map/mixer_layer_1/pallas_call | solution.py:645
  176.6 2.3 %copy.18 = bf16[1024,512]{1,0:T(8,128)(2,1)} copy(bf16[1024,512]{1,0:T(8,128)(2,1)} %mixer_layer_1.1) | data formatting | bytes 2097152

commit v3 on v2

v3 whole, which is shorter than its diff:
```python
import functools

import jax
import jax.numpy as jnp
from jax import lax
from jax.experimental import pallas as pl
from jax.experimental.pallas import tpu as pltpu
from jax.sharding import PartitionSpec as P

HEAD_DIM = 64
STATE = 128
STRETCH = 128
LANES = 128
HALO = 16
ROWS = 256
COLUMNS = 128

epsilon = 1e-05
f32 = jnp.float32
bf16 = jnp.bfloat16
MESH = pl.DeviceIdType.MESH


def iota(shape, axis):
    return lax.broadcasted_iota(jnp.int32, shape, axis)


def spreader_of(heads, inner):
    row = iota((LANES, inner), 0)
    channel = iota((LANES, inner), 1)
    chosen = (row % heads == channel // HEAD_DIM) & (row < 3 * heads)
    return jnp.where(chosen, 1.0, 0.0).astype(bf16)


def pack_pieces(values, heads):
    values = jnp.where(iota(values.shape, 1) < heads, values, 0.0)
    high = values.astype(bf16).astype(f32)
    rest = values - high
    middle = rest.astype(bf16).astype(f32)
    low = rest - middle
    packed = high + pltpu.roll(middle, heads, 1) + pltpu.roll(low, 2 * heads, 1)
    return packed.astype(bf16)


def expand(values, heads, spreader):
    return jnp.dot(pack_pieces(values, heads), spreader, preferred_element_type=f32)


def running_sum(tri, logs, heads):
    parts = jnp.dot(tri, pack_pieces(logs, heads), preferred_element_type=f32)
    total = parts + pltpu.roll(parts, LANES - heads, 1) + pltpu.roll(parts, LANES - 2 * heads, 1)
    return jnp.where(iota(total.shape, 1) < heads, total, 0.0)


def rows_of(k, size):
    return pl.ds(pl.multiple_of(k * size, size), size)


def lanes_of(k, size):
    return pl.ds(pl.multiple_of(k * size, LANES), size)


def pad_row(row):
    return jnp.concatenate([row, jnp.zeros((1, LANES - row.shape[1]), f32)], axis=1)


def layers_kernel(
    count, members,
    stream_ref, order_ref, in_gain_ref, w_in_ref, w_bc_ref, w_dt_ref, conv_x_ref, conv_bc_ref,
    bias_ref, a_log_ref, d_skip_ref, out_gain_ref, w_out_ref,
    out_ref,
    full_ref, tail_ref, halo_ref, orders_ref, raw_ref, raw_bc_ref, w_ref, wz_ref, wo_col_ref, wo_ref,
    ext_ref, y_ref, z_ref, feed_ref, b_ref, c_ref, cum_ref, scale_ref, states_ref, sofar_exp_ref,
    state_ref, sofar_ref,
    end_ref, log_ref, got_ref, logs_ref, give_ref, arriving_ref, prefix_ref,
    partial_ref, near_col_ref, sum_col_ref, far_col_ref, near_row_ref, sum_row_ref, far_row_ref,
    mixed_ref, hand_ref, place_ref, leaving_ref, arrived_ref,
    load_sem, wo_sem, self_sem, ag_send, ag_recv, halo_send, halo_recv, order_send, order_recv,
    end_send, end_recv, log_send, log_recv, give_send, give_recv,
    near_send, near_recv, far_send, far_recv, move_send, move_recv,
):
    seq = lax.axis_index("seq")
    own = lax.axis_index("tp")
    chip, core = own // 2, own % 2
    near_id = chip * 2 + 1 - core
    across_id = (1 - chip) * 2 + core
    diagonal_id = (1 - chip) * 2 + 1 - core
    sibling = (seq, near_id)
    across = (seq, across_id)
    length, width = stream_ref.shape
    depth = w_ref.shape[0]
    inner = y_ref.shape[1]
    mixed = inner + 2 * STATE
    heads = inner // HEAD_DIM
    chunks = length // ROWS
    per = ROWS // STRETCH
    blocks = length // STRETCH
    pieces = width // COLUMNS
    share = length // count
    state_rows = STATE // count
    following = (seq + 1) % count
    before = (seq + count - 1) % count

    def remote(src, dst, send, recv, device):
        return pltpu.make_async_remote_copy(
            src_ref=src, dst_ref=dst, send_sem=send, recv_sem=recv,
            device_id=device, device_id_type=MESH,
        )

    def each(first, last, act):
        def step(i, _):
            act(i)
            return 0

        lax.fori_loop(first, last, step, 0)

    greeted = [sibling, across]
    greeted += [(before, t) for t in range(members)]
    greeted += [((seq + d) % count, own) for d in range(1, count)]
    barrier = pltpu.get_barrier_semaphore()
    for device in greeted:
        pl.semaphore_signal(barrier, inc=1, device_id=device, device_id_type=MESH)

    def weight_loads(layer):
        return [
            pltpu.make_async_copy(w_in_ref.at[layer], raw_ref, load_sem.at[layer, 0]),
            pltpu.make_async_copy(w_bc_ref.at[layer], raw_bc_ref, load_sem.at[layer, 1]),
        ]

    own_lanes = lanes_of(own, COLUMNS)
    self_loads, wo_loads = [], []
    for j in range(pieces):
        self_loads.append(
            pltpu.make_async_copy(
                stream_ref.at[:, j * COLUMNS : (j + 1) * COLUMNS],
                full_ref.at[j, :, own_lanes], self_sem.at[j],
            )
        )
        for t in range(members):
            first = t * width + j * COLUMNS
            place = j * members + t
            wo_loads.append(
                pltpu.make_async_copy(
                    w_out_ref.at[0, :, first : first + COLUMNS],
                    wo_col_ref.at[:, place * COLUMNS : (place + 1) * COLUMNS],
                    wo_sem.at[place],
                )
            )
    wo_loads.append(pltpu.make_async_copy(w_out_ref.at[1], wo_ref, wo_sem.at[pieces * members]))
    for copy in weight_loads(0) + self_loads + wo_loads:
        copy.start()

    pl.semaphore_wait(barrier, len(greeted))

    def piece_of(j, k, t):
        return full_ref.at[j, rows_of(k, ROWS), lanes_of(t, COLUMNS)]

    def gather_copy(layer, kind, j, k, owner):
        src = piece_of(j, k, owner)
        if layer == 0 and kind < 2:
            src = stream_ref.at[rows_of(k, ROWS), lanes_of(j, COLUMNS)]
        return remote(
            src, piece_of(j, k, owner), ag_send.at[layer, kind, j, k],
            ag_recv.at[layer, kind, j, k], across if kind == 0 else sibling,
        )

    def send_piece(layer, j, k):
        gather_copy(layer, 0, j, k, own).start()
        gather_copy(layer, 1, j, k, own).start()

    def forward_piece(layer, j, k):
        gather_copy(layer, 0, j, k, across_id).wait_recv()
        gather_copy(layer, 2, j, k, across_id).start()

    def rest_of_piece(layer, j, k):
        gather_copy(layer, 1, j, k, near_id).wait_recv()
        gather_copy(layer, 2, j, k, diagonal_id).wait_recv()

    def gathered(layer):
        def drain(k):
            for j in range(pieces):
                gather_copy(layer, 0, j, k, own).wait_send()
                gather_copy(layer, 1, j, k, own).wait_send()
                gather_copy(layer, 2, j, k, across_id).wait_send()

        each(0, chunks, drain)

    def tail_of(layer):
        return tail_ref if layer else stream_ref.at[pl.ds(length - HALO, HALO)]

    def halo_copy(layer, t, source):
        return remote(
            tail_of(layer), halo_ref.at[layer, source],
            halo_send.at[layer, t], halo_recv.at[layer, source], (following, t),
        )

    def order_copy(d):
        return remote(
            order_ref, orders_ref.at[seq], order_send.at[d - 1], order_recv.at[d - 1],
            ((seq + d) % count, own),
        )

    for t in range(members):
        halo_copy(0, t, own).start()

    def send_rows(k):
        for j in range(pieces):
            send_piece(0, j, k)

    each(0, chunks, send_rows)
    each(1, count, lambda d: order_copy(d).start())

    row = iota((2 * LANES, 2 * LANES), 0)
    col = iota((2 * LANES, 2 * LANES), 1)
    apart = jnp.where(col == 2 * (row % LANES) + row // LANES, 1.0, 0.0).astype(bf16)

    def prepare(layer, j):
        def block(t):
            i = t * pieces + j
            rows = rows_of(i, LANES)
            to = rows_of(j * members + t, LANES)
            gain = in_gain_ref[layer : layer + 1, lanes_of(i, LANES)]
            gain = jnp.broadcast_to(gain, (LANES, LANES)).T
            both = raw_ref[rows].reshape(2 * LANES, inner)
            halves = jnp.dot(apart, both, preferred_element_type=f32)
            for p in range(inner // LANES):
                lanes = slice(p * LANES, (p + 1) * LANES)
                w_ref[to, lanes] = (halves[:LANES, lanes] * gain).astype(bf16)
                wz_ref[to, lanes] = (halves[LANES:, lanes] * gain).astype(bf16)
            for p in range(2 * STATE // LANES):
                lanes = slice(p * LANES, (p + 1) * LANES)
                w_ref[to, inner + p * LANES : inner + (p + 1) * LANES] = (
                    raw_bc_ref[rows, lanes].astype(f32) * gain
                ).astype(bf16)
            dt = w_dt_ref[layer, :, lanes_of(i, LANES)].astype(f32)
            dt = jnp.concatenate([dt, jnp.zeros((LANES - heads, LANES), f32)], axis=0)
            w_ref[to, mixed:] = (dt.T * gain).astype(bf16)

        each(0, members, block)

    spreader = spreader_of(heads, inner)
    line = iota((STRETCH, STRETCH), 0)
    lane = iota((STRETCH, STRETCH), 1)
    lower = line >= lane
    tri = jnp.where(lower, 1.0, 0.0).astype(bf16)
    left = iota((STRETCH, 2 * HEAD_DIM), 1) < HEAD_DIM

    def scale_of(v):
        wide = v.astype(f32)
        return lax.rsqrt(jnp.mean(wide * wide, axis=-1, keepdims=True) + epsilon)

    def scan(layer, arrive):
        for t in range(members):
            halo_copy(layer, t, t).wait_recv()
        ahead = jnp.concatenate(
            [
                halo_ref[layer, t, :, j * COLUMNS : (j + 1) * COLUMNS]
                for j in range(pieces) for t in range(members)
            ],
            axis=1,
        )
        ahead = jnp.dot(ahead, w_ref[:, :mixed], preferred_element_type=f32) * scale_of(ahead)
        ahead = ahead[HALO - 8 :, :].astype(bf16).astype(f32)
        ext_ref[0:8, :] = jnp.where(seq > 0, ahead, 0.0)
        state_ref[...] = jnp.zeros_like(state_ref)
        sofar_ref[...] = jnp.zeros_like(sofar_ref)
        bias = pad_row(bias_ref[layer : layer + 1, :])
        rate = pad_row(jnp.exp(a_log_ref[layer : layer + 1, :]))
        skip = pad_row(d_skip_ref[layer : layer + 1, :])
        skip = expand(jnp.broadcast_to(skip, (8, LANES)), heads, spreader)[0:1]
        taps = jnp.concatenate([conv_x_ref[layer], conv_bc_ref[layer]], axis=1)
        tap_count = taps.shape[0]

        def project(k):
            rows = rows_of(k, ROWS)
            arrive(k)
            tokens = jnp.concatenate([full_ref[j, rows, :] for j in range(pieces)], axis=1)
            scale = scale_of(tokens)
            scale_ref[rows, :] = jnp.broadcast_to(scale, (ROWS, LANES))
            projected = jnp.dot(tokens, w_ref[...], preferred_element_type=f32) * scale
            ext_ref[8 : 8 + ROWS, :] = projected[:, :mixed].astype(bf16).astype(f32)
            conv = jnp.zeros((ROWS, mixed), f32)
            for tap in range(tap_count):
                first = 9 - tap_count + tap
                conv = conv + taps[tap : tap + 1, :] * ext_ref[first : first + ROWS, :]
            conv = conv * jax.nn.sigmoid(conv)
            ext_ref[0:8, :] = ext_ref[ROWS : ROWS + 8, :]
            raw = projected[:, mixed:] + bias
            step = jnp.maximum(raw, 0.0) + jnp.log1p(jnp.exp(-jnp.abs(raw)))
            logs = -step * rate
            x = conv[:, :inner]
            b_all = conv[:, inner : inner + STATE]
            b_ref[rows, :] = b_all.astype(bf16)
            c_ref[rows, :] = conv[:, inner + STATE :].astype(bf16)
            feed = x * expand(step, heads, spreader)
            feed_ref[rows, :] = feed.astype(bf16)
            y_ref[rows, :] = skip * x
            state = state_ref[...]
            sofar = sofar_ref[...]
            for block in range(per):
                part = slice(block * STRETCH, (block + 1) * STRETCH)
                index = k * per + block
                cum = running_sum(tri, logs[part], heads)
                last = cum[STRETCH - 1 : STRETCH, :]
                factors = expand(
                    jnp.concatenate(
                        [
                            jnp.exp(last - cum),
                            jnp.exp(jnp.broadcast_to(last, (8, LANES))),
                            jnp.exp(sofar),
                        ],
                        axis=0,
                    ),
                    heads, spreader,
                )
                fresh = jnp.dot(
                    b_all[part].T.astype(bf16),
                    (feed[part] * factors[:STRETCH]).astype(bf16),
                    preferred_element_type=f32,
                )
                states_ref[index] = state
                sofar_exp_ref[index] = factors[STRETCH + 8 :]
                state = state * factors[STRETCH : STRETCH + 1] + fresh
                cum_ref[rows_of(index, STRETCH), :] = cum
                sofar = sofar + last
            state_ref[...] = state
            sofar_ref[...] = sofar

        each(0, chunks, project)

    def within(k):
        rows = rows_of(k, ROWS)
        tokens = jnp.concatenate([full_ref[j, rows, :] for j in range(pieces)], axis=1)
        gate = jnp.dot(tokens, wz_ref[...], preferred_element_type=f32)
        z_ref[rows, :] = (gate * scale_ref[rows, 0:1]).astype(bf16)

        def block(b):
            rows = rows_of(k * per + b, STRETCH)
            cum = cum_ref[rows, :]
            cum_t = cum.T
            feed = feed_ref[rows, :]
            meet = lax.dot_general(
                c_ref[rows, :], b_ref[rows, :], (((1,), (1,)), ((), ())),
                preferred_element_type=f32,
            )
            for pair in range(heads // 2):
                lanes = slice(pair * 2 * HEAD_DIM, (pair + 1) * 2 * HEAD_DIM)
                weights = []
                for h in (2 * pair, 2 * pair + 1):
                    spread = jnp.where(lower, cum[:, h : h + 1] - cum_t[h : h + 1, :], -jnp.inf)
                    weights.append((meet * jnp.exp(spread)).astype(bf16))
                fed = feed[:, lanes]
                nought = jnp.zeros_like(fed)
                stacked = jnp.concatenate(
                    [jnp.where(left, fed, nought), jnp.where(left, nought, fed)], axis=0
                )
                inside = jnp.dot(
                    jnp.concatenate(weights, axis=1), stacked, preferred_element_type=f32
                )
                y_ref[rows, lanes] = y_ref[rows, lanes] + inside

        each(0, per, block)

    def exchange(layer):
        def end_copy(d, place):
            other = (seq + d) % count
            return remote(
                end_ref.at[layer, other], got_ref.at[layer, place],
                end_send.at[layer, d - 1], end_recv.at[layer, d - 1], (other, own),
            )

        def log_copy(d, place):
            return remote(
                log_ref.at[layer], logs_ref.at[layer, place],
                log_send.at[layer, d - 1], log_recv.at[layer, d - 1], ((seq + d) % count, own),
            )

        def give_copy(d, place):
            other = (seq + d) % count
            return remote(
                give_ref.at[layer, other], arriving_ref.at[layer, place],
                give_send.at[layer, d - 1], give_recv.at[layer, d - 1], (other, own),
            )

        def sender(d):
            return (seq + count - d) % count

        state = state_ref[...]
        for d in range(count):
            end_ref[layer, d] = state[d * state_rows : (d + 1) * state_rows].astype(bf16)
        log_ref[layer] = sofar_ref[...]

        def send(d):
            log_copy(d, seq).start()
            end_copy(d, seq).start()

        each(1, count, send)
        each(0, chunks // 2, within)

        def receive(d):
            log_copy(d, sender(d)).wait_recv()
            end_copy(d, sender(d)).wait_recv()

        each(1, count, receive)
        got_ref[layer, seq] = end_ref[layer, seq]
        logs_ref[layer, seq] = log_ref[layer]
        logs = jnp.concatenate([logs_ref[layer, d, 0:1] for d in range(count)], axis=0)
        factors = expand(jnp.exp(logs), heads, spreader)
        prefix = jnp.zeros((state_rows, inner), f32)
        for d in range(count):
            give_ref[layer, d] = prefix.astype(bf16)
            if d + 1 < count:
                prefix = prefix * factors[d : d + 1] + got_ref[layer, d].astype(f32)
        each(1, count, lambda d: give_copy(d, seq).start())
        each(chunks // 2, chunks, within)
        each(1, count, lambda d: give_copy(d, sender(d)).wait_recv())
        arriving_ref[layer, seq] = give_ref[layer, seq]
        prefix_ref[...] = jnp.concatenate(
            [arriving_ref[layer, d].astype(f32) for d in range(count)], axis=0
        )

        def drain(d):
            log_copy(d, seq).wait_send()
            end_copy(d, seq).wait_send()
            give_copy(d, seq).wait_send()

        each(1, count, drain)

    pair = 2 * HEAD_DIM
    one = iota((2 * pair, pair), 0) % pair // HEAD_DIM
    two = iota((2 * pair, pair), 1) // HEAD_DIM
    averager = jnp.where(one == two, 1.0 / HEAD_DIM, 0.0).astype(bf16)

    def mixed_of(layer, k):
        rows = rows_of(k, ROWS)
        grown = expand(jnp.exp(cum_ref[rows, :]), heads, spreader)
        carried = []
        for block in range(per):
            index = k * per + block
            state = states_ref[index] + prefix_ref[...] * sofar_exp_ref[index][0:1]
            carried.append(
                jnp.dot(
                    c_ref[rows_of(index, STRETCH), :], state.astype(bf16),
                    preferred_element_type=f32,
                )
            )
        gate = z_ref[rows, :].astype(f32)
        ssd = y_ref[rows, :] + jnp.concatenate(carried, axis=0) * grown
        gated = ssd * (gate * jax.nn.sigmoid(gate))
        square = gated * gated
        high = square.astype(bf16)
        low = (square - high.astype(f32)).astype(bf16)
        results = []
        for p in range(inner // pair):
            lanes = slice(p * pair, (p + 1) * pair)
            both = jnp.concatenate([high[:, lanes], low[:, lanes]], axis=1)
            mean = jnp.dot(both, averager, preferred_element_type=f32)
            scaled = gated[:, lanes] * lax.rsqrt(mean + epsilon)
            results.append((scaled * out_gain_ref[layer : layer + 1, lanes]).astype(bf16))
        return jnp.concatenate(results, axis=1)

    sums = (
        (near_col_ref, sum_col_ref, far_col_ref, pieces),
        (near_row_ref, sum_row_ref, far_row_ref, chunks),
    )

    def part_of(layer, k, block):
        if layer == 0:
            return pl.ds(0, length), lanes_of(k * members + block, COLUMNS)
        return rows_of(k, ROWS), lanes_of(block, width)

    def near_part(layer, side, k):
        block = diagonal_id if side == 0 else near_id
        rows, lanes = part_of(layer, k, block)
        return remote(
            partial_ref.at[rows, lanes], sums[layer][0].at[side, k],
            near_send.at[layer, side, k], near_recv.at[layer, side, k], sibling,
        )

    def far_part(layer, k):
        return remote(
            sums[layer][1].at[k], sums[layer][2].at[k],
            far_send.at[layer, k], far_recv.at[layer, k], across,
        )

    def send_far(layer, k):
        near_ref, sum_ref = sums[layer][:2]
        near_part(layer, 0, k).wait_recv()
        rows, lanes = part_of(layer, k, across_id)
        sum_ref[k] = (
            partial_ref[rows, lanes].astype(f32) + near_ref[0, k].astype(f32)
        ).astype(bf16)
        far_part(layer, k).start()

    def send_near(layer, k):
        near_part(layer, 0, k).start()
        near_part(layer, 1, k).start()

        @pl.when(k > 0)
        def _():
            send_far(layer, k - 1)

    def summed(layer, k, stream):
        near_ref, far_ref = sums[layer][0], sums[layer][2]
        near_part(layer, 1, k).wait_recv()
        far_part(layer, k).wait_recv()
        rows, lanes = part_of(layer, k, own)
        return (
            stream.astype(f32)
            + partial_ref[rows, lanes].astype(f32)
            + near_ref[1, k].astype(f32)
            + far_ref[k].astype(f32)
        ).astype(bf16)

    def drain_sums(layer):
        def drain(k):
            near_part(layer, 0, k).wait_send()
            near_part(layer, 1, k).wait_send()
            far_part(layer, k).wait_send()

        each(0, sums[layer][3], drain)

    def plan():
        shift = length.bit_length() - 1
        each(1, count, lambda d: order_copy(d).wait_recv())
        orders_ref[seq] = order_ref[...]
        orders = jnp.concatenate([orders_ref[d] for d in range(count)], axis=0)

        def count_up(r):
            first = iota((LANES, length), 0) + r * LANES
            place_ref[rows_of(r, LANES), :] = jnp.where(
                first <= iota((LANES, length), 1), 1.0, 0.0
            ).astype(bf16)

        each(0, length // LANES, count_up)
        device = iota((count, length), 0)
        wanted_here = jnp.right_shift(orders, shift) == seq
        from_each = jnp.right_shift(order_ref[...], shift) == device
        ones = jnp.concatenate(
            [jnp.where(wanted_here, 1.0, 0.0), jnp.where(from_each, 1.0, 0.0)], axis=0
        ).astype(bf16)
        counted = jnp.dot(ones, place_ref[...], preferred_element_type=f32).astype(jnp.int32) - 1
        slot = jnp.where(wanted_here, counted[:count], -1)
        local = jnp.bitwise_and(orders, length - 1)
        short = iota((share, length), 0)
        long = iota((share, length), 1)
        for d in range(count):
            chosen = slot[d : d + 1, :] == short
            found = jnp.where(chosen, local[d : d + 1, :], 0).astype(f32)
            wanted = jnp.sum(found, axis=1, keepdims=True).astype(jnp.int32)
            hand_ref[d * share : (d + 1) * share, :] = jnp.where(
                wanted == long, 1.0, 0.0
            ).astype(bf16)
        target = jnp.where(from_each, counted[count:] + share * device, 0).astype(f32)
        target = jnp.sum(target, axis=0, keepdims=True)
        target = jnp.broadcast_to(target, (LANES, length)).T.astype(jnp.int32)
        for c in range(length // LANES):
            place_ref[:, c * LANES : (c + 1) * LANES] = jnp.where(
                target == iota((length, LANES), 1) + c * LANES, 1.0, 0.0
            ).astype(bf16)

    def move_copy(j, d):
        other = (seq + d) % count
        return remote(
            leaving_ref.at[j, rows_of(other, share)], arrived_ref.at[j, rows_of(seq, share)],
            move_send.at[j, d - 1], move_recv.at[j, d - 1], (other, own),
        )

    def move_arrival(j, d):
        other = (seq + count - d) % count
        return remote(
            leaving_ref.at[j, rows_of(other, share)], arrived_ref.at[j, rows_of(other, share)],
            move_send.at[j, d - 1], move_recv.at[j, d - 1], ((seq + d) % count, own),
        )

    def hand_over(j):
        held = summed(0, j, stream_ref[:, j * COLUMNS : (j + 1) * COLUMNS])
        leaving_ref[j] = jnp.dot(hand_ref[...], held, preferred_element_type=f32).astype(bf16)
        each(1, count, lambda d: move_copy(j, d).start())
        arrived_ref[j, rows_of(seq, share), :] = leaving_ref[j, rows_of(seq, share), :]

    def put(j):
        lanes = slice(j * COLUMNS, (j + 1) * COLUMNS)
        each(1, count, lambda d: move_arrival(j, d).wait_recv())
        rows = jnp.dot(place_ref[...], arrived_ref[j], preferred_element_type=f32).astype(bf16)
        out_ref[:, lanes] = rows
        full_ref[j, :, own_lanes] = rows
        tail_ref[:, lanes] = rows[length - HALO :]
        each(0, chunks, lambda k: send_piece(1, j, k))

    for copy in weight_loads(0):
        copy.wait()
    for j in range(pieces):
        prepare(0, j)
    for copy in weight_loads(1):
        copy.start()
    for copy in self_loads:
        copy.wait()

    def arrive_first(k):
        for j in range(pieces):
            forward_piece(0, j, k)
        for j in range(pieces):
            rest_of_piece(0, j, k)

    scan(0, arrive_first)
    exchange(0)
    gathered(0)
    for copy in wo_loads:
        copy.wait()

    def mix(k):
        mixed_ref[rows_of(k, ROWS), :] = mixed_of(0, k)

    each(0, chunks, mix)

    def output_columns(j):
        lanes = lanes_of(j, members * COLUMNS)

        def product(k):
            rows = rows_of(k, ROWS)
            partial_ref[rows, lanes] = jnp.dot(
                mixed_ref[rows, :], wo_col_ref[:, lanes], preferred_element_type=f32
            ).astype(bf16)

        each(0, chunks, product)
        send_near(0, j)

    each(0, pieces, output_columns)
    send_far(0, pieces - 1)
    plan()
    for copy in weight_loads(1):
        copy.wait()

    for j in range(pieces):
        hand_over(j)
        if j:
            put(j - 1)
        prepare(1, j)
    put(pieces - 1)
    for t in range(members):
        halo_copy(1, t, own).start()
    drain_sums(0)

    for j in range(pieces - 1):
        each(0, chunks, lambda k: forward_piece(1, j, k))

    def arrive_second(k):
        forward_piece(1, pieces - 1, k)
        for j in range(pieces):
            rest_of_piece(1, j, k)

    scan(1, arrive_second)
    exchange(1)

    def output_rows(k):
        partial_ref[rows_of(k, ROWS), :] = jnp.dot(
            mixed_of(1, k), wo_ref[...], preferred_element_type=f32
        ).astype(bf16)
        send_near(1, k)

    each(0, chunks, output_rows)
    send_far(1, chunks - 1)

    def finish(k):
        rows = rows_of(k, ROWS)
        out_ref[rows, :] = summed(1, k, out_ref[rows, :])

    each(0, chunks, finish)
    gathered(1)
    drain_sums(1)
    for layer in range(2):
        for t in range(members):
            halo_copy(layer, t, own).wait_send()

    def moved(d):
        order_copy(d).wait_send()
        for j in range(pieces):
            move_copy(j, d).wait_send()

    each(1, count, moved)


def body(
    tokens, col_order, in_gain, w_in, w_bc, w_dt, conv_x, conv_bc,
    dt_bias, a_log, d_skip, out_gain, w_out,
):
    count, members = lax.axis_size("seq"), lax.axis_size("tp")
    length, width = tokens.shape
    inner = w_out.shape[1]
    heads = inner // HEAD_DIM
    mixed = inner + 2 * STATE
    depth = w_in.shape[1]
    chunks = length // ROWS
    blocks = length // STRETCH
    pieces = width // COLUMNS
    peers = count - 1
    state_rows = STATE // count
    vmem = pl.BlockSpec(memory_space=pltpu.VMEM)
    hbm = pl.BlockSpec(memory_space=pl.ANY)
    dma = pltpu.SemaphoreType.DMA
    return pl.pallas_call(
        functools.partial(layers_kernel, count, members),
        in_specs=[vmem, vmem, vmem, hbm, hbm] + [vmem] * 7 + [hbm],
        out_specs=vmem,
        out_shape=jax.ShapeDtypeStruct(tokens.shape, bf16),
        scratch_shapes=[
            pltpu.VMEM((pieces, length, members * COLUMNS), bf16),
            pltpu.VMEM((HALO, width), bf16),
            pltpu.VMEM((2, members, HALO, width), bf16),
            pltpu.VMEM((count, 1, length), jnp.int32),
            pltpu.VMEM((depth, 2, inner), bf16),
            pltpu.VMEM((depth, 2 * STATE), bf16),
            pltpu.VMEM((depth, mixed + LANES), bf16),
            pltpu.VMEM((depth, inner), bf16),
            pltpu.VMEM((inner, depth), bf16),
            pltpu.VMEM((inner, depth), bf16),
            pltpu.VMEM((ROWS + 8, mixed), f32),
            pltpu.VMEM((length, inner), f32),
            pltpu.VMEM((length, inner), bf16),
            pltpu.VMEM((length, inner), bf16),
            pltpu.VMEM((length, STATE), bf16),
            pltpu.VMEM((length, STATE), bf16),
            pltpu.VMEM((length, LANES), f32),
            pltpu.VMEM((length, LANES), f32),
            pltpu.VMEM((blocks, STATE, inner), f32),
            pltpu.VMEM((blocks, 8, inner), f32),
            pltpu.VMEM((STATE, inner), f32),
            pltpu.VMEM((8, LANES), f32),
            pltpu.VMEM((2, count, state_rows, inner), bf16),
            pltpu.VMEM((2, 8, LANES), f32),
            pltpu.VMEM((2, count, state_rows, inner), bf16),
            pltpu.VMEM((2, count, 8, LANES), f32),
            pltpu.VMEM((2, count, state_rows, inner), bf16),
            pltpu.VMEM((2, count, state_rows, inner), bf16),
            pltpu.VMEM((STATE, inner), f32),
            pltpu.VMEM((length, depth), bf16),
            pltpu.VMEM((2, pieces, length, COLUMNS), bf16),
            pltpu.VMEM((pieces, length, COLUMNS), bf16),
            pltpu.VMEM((pieces, length, COLUMNS), bf16),
            pltpu.VMEM((2, chunks, ROWS, width), bf16),
            pltpu.VMEM((chunks, ROWS, width), bf16),
            pltpu.VMEM((chunks, ROWS, width), bf16),
            pltpu.VMEM((length, inner), bf16),
            pltpu.VMEM((length, length), bf16),
            pltpu.VMEM((length, length), bf16),
            pltpu.VMEM((pieces, length, COLUMNS), bf16),
            pltpu.VMEM((pieces, length, COLUMNS), bf16),
            dma((2, 2)), dma((pieces * members + 1,)), dma((pieces,)),
            dma((2, 3, pieces, chunks)), dma((2, 3, pieces, chunks)),
            dma((2, members)), dma((2, members)), dma((peers,)), dma((peers,)),
            dma((2, peers)), dma((2, peers)), dma((2, peers)), dma((2, peers)),
            dma((2, peers)), dma((2, peers)),
            dma((2, 2, max(pieces, chunks))), dma((2, 2, max(pieces, chunks))),
            dma((2, max(pieces, chunks))), dma((2, max(pieces, chunks))),
            dma((pieces, peers)), dma((pieces, peers)),
        ],
        compiler_params=pltpu.CompilerParams(
            collective_id=0, has_side_effects=True, vmem_limit_bytes=63 * 1024 * 1024
        ),
        name="mixer_layers",
    )(
        tokens, col_order[None], in_gain, w_in, w_bc, jnp.swapaxes(w_dt, 1, 2), conv_x, conv_bc,
        dt_bias, a_log, d_skip, out_gain, w_out,
    )


def solution(mesh):
    placed = (
        P("seq", "tp"),
        P("seq"),
        P(),
        P(None, None, None, "tp"),
        P(),
        P(None, None, "tp"),
        P(None, None, "tp"),
        P(),
        P(None, "tp"),
        P(None, "tp"),
        P(None, "tp"),
        P(None, "tp"),
        P(None, "tp", None),
    )
    return jax.shard_map(
        body, mesh=mesh, in_specs=placed, out_specs=P("seq", "tp"), check_vma=False
    )
```

time: 179 us -> 162 us (0.905)
  Pallas kernels: 175 us -> 159 us
    pallas_call x2 -> x1, Pallas kernels: 175 us -> 159 us  [body(): pl.pallas_call(functools.partial(layers_kernel, count, members), in_specs...]
where the time goes in v3:
time: 162 us
  Pallas kernels  159 us (98%)
  local copies, waits for them, and re-layouts  2.26 us (1%)
    pallas_call x1, Pallas kernels, body(): pl.pallas_call(functools.partial(layers_kernel, count, members), in_specs...  159 us

profile of v3, /device:TPU:0, one launch (start us, length us, event | category | flops | bytes accessed | tf_op | source)
XLA Modules:
  0.0 161.8 jit_solution(2891316106577522351)
XLA Ops:
  0.0 159.5 %mixer_layers.1 = bf16[1024,512]{1,0:T(8,128)(2,1)} custom-call(bf16[1024,512]{1,0:T(8,128)(2,1)} %stream_ref.1, s32[1,1024]{1,0:T(1,128)} %bitcast.3, f32[2,2048]{1,0:T(2,128)} %in_gain_ref.1, bf16[2,2048,2,512]{3,2,1,0:T(2,128)(2,1)} %w_in_ref.1, bf16[2,2048,256]{2,1,0:T(8,128)(2,1)} %w_bc_ref.1, bf16[2,8,2048]{2,1,0:T(8,128)(2,1)} %bitcast.2, ...), custom_call_target="tpu_custom_call" | custom-call | tf_op jit(solution)/shard_map/mixer_layers/pallas_call | solution.py:702
  159.5 2.3 %copy.15 = bf16[1024,512]{1,0:T(8,128)(2,1)} copy(bf16[1024,512]{1,0:T(8,128)(2,1)} %mixer_layers.1) | data formatting | bytes 2097152

commit v4 on v3

--- a/solution.py
+++ b/solution.py
@@ -74,7 +74,7 @@
     state_ref, sofar_ref,
     end_ref, log_ref, got_ref, logs_ref, give_ref, arriving_ref, prefix_ref,
     partial_ref, near_col_ref, sum_col_ref, far_col_ref, near_row_ref, sum_row_ref, far_row_ref,
-    mixed_ref, hand_ref, place_ref, leaving_ref, arrived_ref,
+    mixed_ref, hand_ref, place_ref, leaving_ref, arrived_ref, held_ref, acc_ref,
     load_sem, wo_sem, self_sem, ag_send, ag_recv, halo_send, halo_recv, order_send, order_recv,
     end_send, end_recv, log_send, log_recv, give_send, give_recv,
     near_send, near_recv, far_send, far_recv, move_send, move_recv,
@@ -152,60 +152,74 @@
 
     pl.semaphore_wait(barrier, len(greeted))
 
-    def piece_of(j, k, t):
-        return full_ref.at[j, rows_of(k, ROWS), lanes_of(t, COLUMNS)]
-
-    def gather_copy(layer, kind, j, k, owner):
-        src = piece_of(j, k, owner)
-        if layer == 0 and kind < 2:
-            src = stream_ref.at[rows_of(k, ROWS), lanes_of(j, COLUMNS)]
+    last_piece = pieces - 1
+
+    def block_of(layer, i, owner):
+        lanes = lanes_of(owner, COLUMNS)
+        if layer == 0:
+            return full_ref.at[:, rows_of(i, ROWS), lanes], i
+        if isinstance(i, int):
+            return full_ref.at[i, :, lanes], chunks + i
+        return full_ref.at[last_piece, rows_of(i[0], ROWS), lanes], chunks + last_piece + i[0]
+
+    def gather_copy(layer, kind, i, owner):
+        block, slot = block_of(layer, i, owner)
         return remote(
-            src, piece_of(j, k, owner), ag_send.at[layer, kind, j, k],
-            ag_recv.at[layer, kind, j, k], across if kind == 0 else sibling,
-        )
-
-    def send_piece(layer, j, k):
-        gather_copy(layer, 0, j, k, own).start()
-        gather_copy(layer, 1, j, k, own).start()
-
-    def forward_piece(layer, j, k):
-        gather_copy(layer, 0, j, k, across_id).wait_recv()
-        gather_copy(layer, 2, j, k, across_id).start()
-
-    def rest_of_piece(layer, j, k):
-        gather_copy(layer, 1, j, k, near_id).wait_recv()
-        gather_copy(layer, 2, j, k, diagonal_id).wait_recv()
-
-    def gathered(layer):
-        def drain(k):
+            block, block, ag_send.at[kind, slot], ag_recv.at[kind, slot],
+            across if kind == 0 else sibling,
+        )
+
+    def send_rows(k):
+        rows = rows_of(k, ROWS)
+        for kind, device in ((0, across), (1, sibling)):
             for j in range(pieces):
-                gather_copy(layer, 0, j, k, own).wait_send()
-                gather_copy(layer, 1, j, k, own).wait_send()
-                gather_copy(layer, 2, j, k, across_id).wait_send()
-
-        each(0, chunks, drain)
-
-    def tail_of(layer):
-        return tail_ref if layer else stream_ref.at[pl.ds(length - HALO, HALO)]
+                remote(
+                    stream_ref.at[rows, lanes_of(j, COLUMNS)], full_ref.at[j, rows, own_lanes],
+                    ag_send.at[kind, k], ag_recv.at[kind, k], device,
+                ).start()
+
+    def send_block(layer, i):
+        gather_copy(layer, 0, i, own).start()
+        gather_copy(layer, 1, i, own).start()
+
+    def forward_block(layer, i):
+        gather_copy(layer, 0, i, across_id).wait_recv()
+        gather_copy(layer, 2, i, across_id).start()
+
+    def rest_of_block(layer, i):
+        gather_copy(layer, 1, i, near_id).wait_recv()
+        gather_copy(layer, 2, i, diagonal_id).wait_recv()
+
+    def drain_block(layer, i):
+        gather_copy(layer, 0, i, own).wait_send()
+        gather_copy(layer, 1, i, own).wait_send()
+        gather_copy(layer, 2, i, across_id).wait_send()
 
     def halo_copy(layer, t, source):
+        tail = tail_ref if layer else stream_ref.at[pl.ds(length - HALO, HALO)]
         return remote(
-            tail_of(layer), halo_ref.at[layer, source],
+            tail, halo_ref.at[layer, source],
             halo_send.at[layer, t], halo_recv.at[layer, source], (following, t),
+        )
+
+    def halo_piece(j, t):
+        lanes = lanes_of(j, COLUMNS)
+        return remote(
+            tail_ref.at[:, lanes], halo_ref.at[1, own, :, lanes],
+            halo_send.at[1, t], halo_recv.at[1, own], (following, t),
         )
 
     def order_copy(d):
         return remote(
-            order_ref, orders_ref.at[seq], order_send.at[d - 1], order_recv.at[d - 1],
-            ((seq + d) % count, own),
-        )
+            order_ref, orders_ref.at[seq], order_send, order_recv, ((seq + d) % count, own)
+        )
+
+    def all_orders():
+        others = orders_ref.at[pl.ds(0, count - 1)]
+        return remote(others, others, order_send, order_recv, (following, own))
 
     for t in range(members):
         halo_copy(0, t, own).start()
-
-    def send_rows(k):
-        for j in range(pieces):
-            send_piece(0, j, k)
 
     each(0, chunks, send_rows)
     each(1, count, lambda d: order_copy(d).start())
@@ -277,7 +291,14 @@
             tokens = jnp.concatenate([full_ref[j, rows, :] for j in range(pieces)], axis=1)
             scale = scale_of(tokens)
             scale_ref[rows, :] = jnp.broadcast_to(scale, (ROWS, LANES))
-            projected = jnp.dot(tokens, w_ref[...], preferred_element_type=f32) * scale
+            if layer == 0:
+                projected = jnp.dot(tokens, w_ref[...], preferred_element_type=f32)
+            else:
+                projected = acc_ref[rows, :] + jnp.dot(
+                    full_ref[last_piece, rows, :], w_ref[last_piece * width :, :],
+                    preferred_element_type=f32,
+                )
+            projected = projected * scale
             ext_ref[8 : 8 + ROWS, :] = projected[:, :mixed].astype(bf16).astype(f32)
             conv = jnp.zeros((ROWS, mixed), f32)
             for tap in range(tap_count):
@@ -362,28 +383,35 @@
         each(0, per, block)
 
     def exchange(layer):
-        def end_copy(d, place):
+        def end_copy(d):
             other = (seq + d) % count
             return remote(
-                end_ref.at[layer, other], got_ref.at[layer, place],
-                end_send.at[layer, d - 1], end_recv.at[layer, d - 1], (other, own),
+                end_ref.at[layer, other], got_ref.at[layer, seq],
+                end_send.at[layer], end_recv.at[layer], (other, own),
             )
 
-        def log_copy(d, place):
+        def log_copy(d):
             return remote(
-                log_ref.at[layer], logs_ref.at[layer, place],
-                log_send.at[layer, d - 1], log_recv.at[layer, d - 1], ((seq + d) % count, own),
+                log_ref.at[layer], logs_ref.at[layer, seq],
+                log_send.at[layer], log_recv.at[layer], ((seq + d) % count, own),
             )
 
-        def give_copy(d, place):
+        def give_copy(d):
             other = (seq + d) % count
             return remote(
-                give_ref.at[layer, other], arriving_ref.at[layer, place],
-                give_send.at[layer, d - 1], give_recv.at[layer, d - 1], (other, own),
+                give_ref.at[layer, other], arriving_ref.at[layer, seq],
+                give_send.at[layer], give_recv.at[layer], (other, own),
             )
 
-        def sender(d):
-            return (seq + count - d) % count
+        others = pl.ds(0, count - 1)
+
+        def all_of(ref, send, recv):
+            block = ref.at[layer, others]
+            return remote(block, block, send.at[layer], recv.at[layer], (following, own))
+
+        all_ends = all_of(got_ref, end_send, end_recv)
+        all_logs = all_of(logs_ref, log_send, log_recv)
+        all_given = all_of(arriving_ref, give_send, give_recv)
 
         state = state_ref[...]
         for d in range(count):
@@ -391,17 +419,13 @@
         log_ref[layer] = sofar_ref[...]
 
         def send(d):
-            log_copy(d, seq).start()
-            end_copy(d, seq).start()
+            log_copy(d).start()
+            end_copy(d).start()
 
         each(1, count, send)
         each(0, chunks // 2, within)
-
-        def receive(d):
-            log_copy(d, sender(d)).wait_recv()
-            end_copy(d, sender(d)).wait_recv()
-
-        each(1, count, receive)
+        all_logs.wait_recv()
+        all_ends.wait_recv()
         got_ref[layer, seq] = end_ref[layer, seq]
         logs_ref[layer, seq] = log_ref[layer]
         logs = jnp.concatenate([logs_ref[layer, d, 0:1] for d in range(count)], axis=0)
@@ -411,20 +435,17 @@
             give_ref[layer, d] = prefix.astype(bf16)
             if d + 1 < count:
                 prefix = prefix * factors[d : d + 1] + got_ref[layer, d].astype(f32)
-        each(1, count, lambda d: give_copy(d, seq).start())
+        each(1, count, lambda d: give_copy(d).start())
         each(chunks // 2, chunks, within)
-        each(1, count, lambda d: give_copy(d, sender(d)).wait_recv())
+        all_given.wait_recv()
         arriving_ref[layer, seq] = give_ref[layer, seq]
         prefix_ref[...] = jnp.concatenate(
             [arriving_ref[layer, d].astype(f32) for d in range(count)], axis=0
         )
 
-        def drain(d):
-            log_copy(d, seq).wait_send()
-            end_copy(d, seq).wait_send()
-            give_copy(d, seq).wait_send()
-
-        each(1, count, drain)
+        all_logs.wait_send()
+        all_ends.wait_send()
+        all_given.wait_send()
 
     pair = 2 * HEAD_DIM
     one = iota((2 * pair, pair), 0) % pair // HEAD_DIM
@@ -459,70 +480,63 @@
             results.append((scaled * out_gain_ref[layer : layer + 1, lanes]).astype(bf16))
         return jnp.concatenate(results, axis=1)
 
-    sums = (
-        (near_col_ref, sum_col_ref, far_col_ref, pieces),
-        (near_row_ref, sum_row_ref, far_row_ref, chunks),
-    )
-
-    def part_of(layer, k, block):
-        if layer == 0:
-            return pl.ds(0, length), lanes_of(k * members + block, COLUMNS)
-        return rows_of(k, ROWS), lanes_of(block, width)
-
-    def near_part(layer, side, k):
+    def part_of(layer, i):
+        if layer == 1:
+            rows = rows_of(i, ROWS)
+            blocks_of = [ref.at[rows] for ref in (sum_row_ref, far_row_ref)]
+            nears = [near_row_ref.at[side, rows] for side in range(2)]
+            return rows, lambda t: lanes_of(t, width), nears, blocks_of, i
+        if isinstance(i, int):
+            rows, j, slot = pl.ds(0, length), i, chunks + i - 1
+        else:
+            rows, j, slot = rows_of(i[0], ROWS), 0, i[0]
+        blocks_of = [ref.at[j, rows] for ref in (sum_col_ref, far_col_ref)]
+        nears = [near_col_ref.at[side, j, rows] for side in range(2)]
+        return rows, lambda t: lanes_of(j * members + t, COLUMNS), nears, blocks_of, slot
+
+    def near_part(layer, side, i):
+        rows, lanes, nears, _, slot = part_of(layer, i)
         block = diagonal_id if side == 0 else near_id
-        rows, lanes = part_of(layer, k, block)
         return remote(
-            partial_ref.at[rows, lanes], sums[layer][0].at[side, k],
-            near_send.at[layer, side, k], near_recv.at[layer, side, k], sibling,
-        )
-
-    def far_part(layer, k):
-        return remote(
-            sums[layer][1].at[k], sums[layer][2].at[k],
-            far_send.at[layer, k], far_recv.at[layer, k], across,
-        )
-
-    def send_far(layer, k):
-        near_ref, sum_ref = sums[layer][:2]
-        near_part(layer, 0, k).wait_recv()
-        rows, lanes = part_of(layer, k, across_id)
-        sum_ref[k] = (
-            partial_ref[rows, lanes].astype(f32) + near_ref[0, k].astype(f32)
+            partial_ref.at[rows, lanes(block)], nears[side],
+            near_send.at[layer, side, slot], near_recv.at[layer, side, slot], sibling,
+        )
+
+    def far_part(layer, i):
+        _, _, _, (summing, far), slot = part_of(layer, i)
+        return remote(summing, far, far_send.at[layer, slot], far_recv.at[layer, slot], across)
+
+    def send_near(layer, i):
+        near_part(layer, 0, i).start()
+        near_part(layer, 1, i).start()
+
+    def send_far(layer, i):
+        rows, lanes, nears, (summing, _), _ = part_of(layer, i)
+        near_part(layer, 0, i).wait_recv()
+        summing[...] = (
+            partial_ref[rows, lanes(across_id)].astype(f32) + nears[0][...].astype(f32)
         ).astype(bf16)
-        far_part(layer, k).start()
-
-    def send_near(layer, k):
-        near_part(layer, 0, k).start()
-        near_part(layer, 1, k).start()
-
-        @pl.when(k > 0)
-        def _():
-            send_far(layer, k - 1)
-
-    def summed(layer, k, stream):
-        near_ref, far_ref = sums[layer][0], sums[layer][2]
-        near_part(layer, 1, k).wait_recv()
-        far_part(layer, k).wait_recv()
-        rows, lanes = part_of(layer, k, own)
+        far_part(layer, i).start()
+
+    def summed(layer, i, stream):
+        rows, lanes, nears, (_, far), _ = part_of(layer, i)
+        near_part(layer, 1, i).wait_recv()
+        far_part(layer, i).wait_recv()
         return (
             stream.astype(f32)
-            + partial_ref[rows, lanes].astype(f32)
-            + near_ref[1, k].astype(f32)
-            + far_ref[k].astype(f32)
+            + partial_ref[rows, lanes(own)].astype(f32)
+            + nears[1][...].astype(f32)
+            + far[...].astype(f32)
         ).astype(bf16)
 
-    def drain_sums(layer):
-        def drain(k):
-            near_part(layer, 0, k).wait_send()
-            near_part(layer, 1, k).wait_send()
-            far_part(layer, k).wait_send()
-
-        each(0, sums[layer][3], drain)
+    def drain_part(layer, i):
+        near_part(layer, 0, i).wait_send()
+        near_part(layer, 1, i).wait_send()
+        far_part(layer, i).wait_send()
 
     def plan():
         shift = length.bit_length() - 1
-        each(1, count, lambda d: order_copy(d).wait_recv())
+        all_orders().wait_recv()
         orders_ref[seq] = order_ref[...]
         orders = jnp.concatenate([orders_ref[d] for d in range(count)], axis=0)
 
@@ -563,30 +577,53 @@
         other = (seq + d) % count
         return remote(
             leaving_ref.at[j, rows_of(other, share)], arrived_ref.at[j, rows_of(seq, share)],
-            move_send.at[j, d - 1], move_recv.at[j, d - 1], (other, own),
-        )
-
-    def move_arrival(j, d):
-        other = (seq + count - d) % count
-        return remote(
-            leaving_ref.at[j, rows_of(other, share)], arrived_ref.at[j, rows_of(other, share)],
-            move_send.at[j, d - 1], move_recv.at[j, d - 1], ((seq + d) % count, own),
-        )
+            move_send.at[j], move_recv.at[j], (other, own),
+        )
+
+    def all_moves(j):
+        others = arrived_ref.at[j, pl.ds(0, length - share)]
+        return remote(others, others, move_send.at[j], move_recv.at[j], (following, own))
 
     def hand_over(j):
-        held = summed(0, j, stream_ref[:, j * COLUMNS : (j + 1) * COLUMNS])
+        if j:
+            held = summed(0, j, stream_ref[:, j * COLUMNS : (j + 1) * COLUMNS])
+        else:
+
+            def first(k):
+                rows = rows_of(k, ROWS)
+                held_ref[rows, :] = summed(0, (k,), stream_ref[rows, :COLUMNS])
+
+            each(0, chunks, first)
+            held = held_ref[...]
         leaving_ref[j] = jnp.dot(hand_ref[...], held, preferred_element_type=f32).astype(bf16)
         each(1, count, lambda d: move_copy(j, d).start())
         arrived_ref[j, rows_of(seq, share), :] = leaving_ref[j, rows_of(seq, share), :]
 
     def put(j):
         lanes = slice(j * COLUMNS, (j + 1) * COLUMNS)
-        each(1, count, lambda d: move_arrival(j, d).wait_recv())
+        all_moves(j).wait_recv()
         rows = jnp.dot(place_ref[...], arrived_ref[j], preferred_element_type=f32).astype(bf16)
+        tail_ref[:, lanes] = rows[length - HALO :]
+        full_ref[j, :, own_lanes] = rows
+        for t in range(members):
+            halo_piece(j, t).start()
+        if j < last_piece:
+            send_block(1, j)
+        else:
+            each(0, chunks, lambda k: send_block(1, (k,)))
         out_ref[:, lanes] = rows
-        full_ref[j, :, own_lanes] = rows
-        tail_ref[:, lanes] = rows[length - HALO :]
-        each(0, chunks, lambda k: send_piece(1, j, k))
+
+    def accumulate(j):
+        part = slice(j * width, (j + 1) * width)
+
+        def product(k):
+            rows = rows_of(k, ROWS)
+            result = jnp.dot(
+                full_ref[j, rows, :], w_ref[part, :], preferred_element_type=f32
+            )
+            acc_ref[rows, :] = result if j == 0 else acc_ref[rows, :] + result
+
+        each(0, chunks, product)
 
     for copy in weight_loads(0):
         copy.wait()
@@ -598,35 +635,35 @@
         copy.wait()
 
     def arrive_first(k):
-        for j in range(pieces):
-            forward_piece(0, j, k)
-        for j in range(pieces):
-            rest_of_piece(0, j, k)
+        forward_block(0, k)
+        rest_of_block(0, k)
 
     scan(0, arrive_first)
     exchange(0)
-    gathered(0)
+    each(0, chunks, lambda k: drain_block(0, k))
     for copy in wo_loads:
         copy.wait()
 
+    def product_of(k, j):
+        rows, lanes = rows_of(k, ROWS), lanes_of(j, members * COLUMNS)
+        partial_ref[rows, lanes] = jnp.dot(
+            mixed_ref[rows, :], wo_col_ref[:, lanes], preferred_element_type=f32
+        ).astype(bf16)
+
     def mix(k):
         mixed_ref[rows_of(k, ROWS), :] = mixed_of(0, k)
+        product_of(k, 0)
+        send_near(0, (k,))
+
+        @pl.when(k > 0)
+        def _():
+            send_far(0, (k - 1,))
 
     each(0, chunks, mix)
-
-    def output_columns(j):
-        lanes = lanes_of(j, members * COLUMNS)
-
-        def product(k):
-            rows = rows_of(k, ROWS)
-            partial_ref[rows, lanes] = jnp.dot(
-                mixed_ref[rows, :], wo_col_ref[:, lanes], preferred_element_type=f32
-            ).astype(bf16)
-
-        each(0, chunks, product)
+    for j in range(1, pieces):
+        each(0, chunks, lambda k: product_of(k, j))
         send_near(0, j)
-
-    each(0, pieces, output_columns)
+        send_far(0, j - 1 if j > 1 else (chunks - 1,))
     send_far(0, pieces - 1)
     plan()
     for copy in weight_loads(1):
@@ -638,17 +675,22 @@
             put(j - 1)
         prepare(1, j)
     put(pieces - 1)
-    for t in range(members):
-        halo_copy(1, t, own).start()
-    drain_sums(0)
-
-    for j in range(pieces - 1):
-        each(0, chunks, lambda k: forward_piece(1, j, k))
+    each(0, chunks, lambda k: drain_part(0, (k,)))
+    for j in range(1, pieces):
+        drain_part(0, j)
+
+    for j in range(last_piece):
+        forward_block(1, j)
+        rest_of_block(1, j)
+        accumulate(j)
+    forward_block(1, (0,))
 
     def arrive_second(k):
-        forward_piece(1, pieces - 1, k)
-        for j in range(pieces):
-            rest_of_piece(1, j, k)
+        @pl.when(k + 1 < chunks)
+        def _():
+            forward_block(1, (k + 1,))
+
+        rest_of_block(1, (k,))
 
     scan(1, arrive_second)
     exchange(1)
@@ -659,6 +701,10 @@
         ).astype(bf16)
         send_near(1, k)
 
+        @pl.when(k > 0)
+        def _():
+            send_far(1, k - 1)
+
     each(0, chunks, output_rows)
     send_far(1, chunks - 1)
 
@@ -667,18 +713,20 @@
         out_ref[rows, :] = summed(1, k, out_ref[rows, :])
 
     each(0, chunks, finish)
-    gathered(1)
-    drain_sums(1)
+    for j in range(last_piece):
+        drain_block(1, j)
+
+    def drain_last(k):
+        drain_block(1, (k,))
+        drain_part(1, k)
+
+    each(0, chunks, drain_last)
     for layer in range(2):
         for t in range(members):
             halo_copy(layer, t, own).wait_send()
-
-    def moved(d):
-        order_copy(d).wait_send()
-        for j in range(pieces):
-            move_copy(j, d).wait_send()
-
-    each(1, count, moved)
+    all_orders().wait_send()
+    for j in range(pieces):
+        all_moves(j).wait_send()
 
 
 def body(
@@ -694,7 +742,6 @@
     chunks = length // ROWS
     blocks = length // STRETCH
     pieces = width // COLUMNS
-    peers = count - 1
     state_rows = STATE // count
     vmem = pl.BlockSpec(memory_space=pltpu.VMEM)
     hbm = pl.BlockSpec(memory_space=pl.ANY)
@@ -738,22 +785,23 @@
             pltpu.VMEM((2, pieces, length, COLUMNS), bf16),
             pltpu.VMEM((pieces, length, COLUMNS), bf16),
             pltpu.VMEM((pieces, length, COLUMNS), bf16),
-            pltpu.VMEM((2, chunks, ROWS, width), bf16),
-            pltpu.VMEM((chunks, ROWS, width), bf16),
-            pltpu.VMEM((chunks, ROWS, width), bf16),
+            pltpu.VMEM((2, length, width), bf16),
+            pltpu.VMEM((length, width), bf16),
+            pltpu.VMEM((length, width), bf16),
             pltpu.VMEM((length, inner), bf16),
             pltpu.VMEM((length, length), bf16),
             pltpu.VMEM((length, length), bf16),
             pltpu.VMEM((pieces, length, COLUMNS), bf16),
             pltpu.VMEM((pieces, length, COLUMNS), bf16),
+            pltpu.VMEM((length, COLUMNS), bf16),
+            pltpu.VMEM((length, mixed + LANES), f32),
             dma((2, 2)), dma((pieces * members + 1,)), dma((pieces,)),
-            dma((2, 3, pieces, chunks)), dma((2, 3, pieces, chunks)),
-            dma((2, members)), dma((2, members)), dma((peers,)), dma((peers,)),
-            dma((2, peers)), dma((2, peers)), dma((2, peers)), dma((2, peers)),
-            dma((2, peers)), dma((2, peers)),
-            dma((2, 2, max(pieces, chunks))), dma((2, 2, max(pieces, chunks))),
-            dma((2, max(pieces, chunks))), dma((2, max(pieces, chunks))),
-            dma((pieces, peers)), dma((pieces, peers)),
+            dma((3, 2 * chunks + pieces - 1)), dma((3, 2 * chunks + pieces - 1)),
+            dma((2, members)), dma((2, members)), dma, dma,
+            dma((2,)), dma((2,)), dma((2,)), dma((2,)), dma((2,)), dma((2,)),
+            dma((2, 2, chunks + pieces - 1)), dma((2, 2, chunks + pieces - 1)),
+            dma((2, chunks + pieces - 1)), dma((2, chunks + pieces - 1)),
+            dma((pieces,)), dma((pieces,)),
         ],
         compiler_params=pltpu.CompilerParams(
             collective_id=0, has_side_effects=True, vmem_limit_bytes=63 * 1024 * 1024

time: 162 us -> 148 us (0.914)
  Pallas kernels: 159 us -> 146 us
    pallas_call x1, Pallas kernels: 159 us -> 146 us  [body(): pl.pallas_call(functools.partial(layers_kernel, count, members), in_specs...]
where the time goes in v4:
time: 148 us
  Pallas kernels  146 us (99%)
  local copies, waits for them, and re-layouts  2.26 us (2%)
    pallas_call x1, Pallas kernels, body(): pl.pallas_call(functools.partial(layers_kernel, count, members), in_specs...  146 us

profile of v4, /device:TPU:0, one launch (start us, length us, event | category | flops | bytes accessed | tf_op | source)
XLA Modules:
  0.0 148.1 jit_solution(6279472085342429055)
XLA Ops:
  0.0 145.8 %mixer_layers.1 = bf16[1024,512]{1,0:T(8,128)(2,1)} custom-call(bf16[1024,512]{1,0:T(8,128)(2,1)} %stream_ref.1, s32[1,1024]{1,0:T(1,128)} %bitcast.3, f32[2,2048]{1,0:T(2,128)} %in_gain_ref.1, bf16[2,2048,2,512]{3,2,1,0:T(2,128)(2,1)} %w_in_ref.1, bf16[2,2048,256]{2,1,0:T(8,128)(2,1)} %w_bc_ref.1, bf16[2,8,2048]{2,1,0:T(8,128)(2,1)} %bitcast.2, ...), custom_call_target="tpu_custom_call" | custom-call | tf_op jit(solution)/shard_map/mixer_layers/pallas_call | solution.py:749
  145.8 2.3 %copy.15 = bf16[1024,512]{1,0:T(8,128)(2,1)} copy(bf16[1024,512]{1,0:T(8,128)(2,1)} %mixer_layers.1) | data formatting | bytes 2097152

commit v5 on v4

--- a/solution.py
+++ b/solution.py
@@ -13,6 +13,7 @@
 LANES = 128
 HALO = 16
 ROWS = 256
+FINE = 128
 COLUMNS = 128
 
 epsilon = 1e-05
@@ -46,9 +47,12 @@
     return jnp.dot(pack_pieces(values, heads), spreader, preferred_element_type=f32)
 
 
-def running_sum(tri, logs, heads):
-    parts = jnp.dot(tri, pack_pieces(logs, heads), preferred_element_type=f32)
-    total = parts + pltpu.roll(parts, LANES - heads, 1) + pltpu.roll(parts, LANES - 2 * heads, 1)
+def unpack_sum(pieces, heads):
+    total = (
+        pieces
+        + pltpu.roll(pieces, LANES - heads, 1)
+        + pltpu.roll(pieces, LANES - 2 * heads, 1)
+    )
     return jnp.where(iota(total.shape, 1) < heads, total, 0.0)
 
 
@@ -74,10 +78,10 @@
     state_ref, sofar_ref,
     end_ref, log_ref, got_ref, logs_ref, give_ref, arriving_ref, prefix_ref,
     partial_ref, near_col_ref, sum_col_ref, far_col_ref, near_row_ref, sum_row_ref, far_row_ref,
-    mixed_ref, hand_ref, place_ref, leaving_ref, arrived_ref, held_ref, acc_ref,
+    mixed_ref, hand_ref, place_ref, leaving_ref, arrived_ref, held_ref, acc_ref, own_ref,
     load_sem, wo_sem, self_sem, ag_send, ag_recv, halo_send, halo_recv, order_send, order_recv,
     end_send, end_recv, log_send, log_recv, give_send, give_recv,
-    near_send, near_recv, far_send, far_recv, move_send, move_recv,
+    near_send, near_recv, far_send, far_recv, move_send, move_recv, out_sem,
 ):
     seq = lax.axis_index("seq")
     own = lax.axis_index("tp")
@@ -93,6 +97,7 @@
     mixed = inner + 2 * STATE
     heads = inner // HEAD_DIM
     chunks = length // ROWS
+    fines = length // FINE
     per = ROWS // STRETCH
     blocks = length // STRETCH
     pieces = width // COLUMNS
@@ -107,6 +112,11 @@
             device_id=device, device_id_type=MESH,
         )
 
+    def other_of(i):
+        low = seq < count // 2
+        other = jnp.where(low, count - 1 - i, i)
+        return jnp.where(low, other - (other <= seq), other + (other >= seq))
+
     def each(first, last, act):
         def step(i, _):
             act(i)
@@ -133,7 +143,7 @@
         self_loads.append(
             pltpu.make_async_copy(
                 stream_ref.at[:, j * COLUMNS : (j + 1) * COLUMNS],
-                full_ref.at[j, :, own_lanes], self_sem.at[j],
+                full_ref.at[j, :, own_lanes], self_sem,
             )
         )
         for t in range(members):
@@ -143,10 +153,10 @@
                 pltpu.make_async_copy(
                     w_out_ref.at[0, :, first : first + COLUMNS],
                     wo_col_ref.at[:, place * COLUMNS : (place + 1) * COLUMNS],
-                    wo_sem.at[place],
+                    wo_sem.at[0],
                 )
             )
-    wo_loads.append(pltpu.make_async_copy(w_out_ref.at[1], wo_ref, wo_sem.at[pieces * members]))
+    wo_loads.append(pltpu.make_async_copy(w_out_ref.at[1], wo_ref, wo_sem.at[1]))
     for copy in weight_loads(0) + self_loads + wo_loads:
         copy.start()
 
@@ -157,25 +167,25 @@
     def block_of(layer, i, owner):
         lanes = lanes_of(owner, COLUMNS)
         if layer == 0:
-            return full_ref.at[:, rows_of(i, ROWS), lanes], i
+            return full_ref.at[:, rows_of(i, FINE), lanes], i
         if isinstance(i, int):
-            return full_ref.at[i, :, lanes], chunks + i
-        return full_ref.at[last_piece, rows_of(i[0], ROWS), lanes], chunks + last_piece + i[0]
+            return full_ref.at[i, :, lanes], fines + i
+        return full_ref.at[last_piece, rows_of(i[0], ROWS), lanes], fines + last_piece + i[0]
 
     def gather_copy(layer, kind, i, owner):
         block, slot = block_of(layer, i, owner)
         return remote(
-            block, block, ag_send.at[kind, slot], ag_recv.at[kind, slot],
+            block, block, ag_send.at[layer, kind], ag_recv.at[kind, slot],
             across if kind == 0 else sibling,
         )
 
     def send_rows(k):
-        rows = rows_of(k, ROWS)
+        rows = rows_of(k, FINE)
         for kind, device in ((0, across), (1, sibling)):
             for j in range(pieces):
                 remote(
                     stream_ref.at[rows, lanes_of(j, COLUMNS)], full_ref.at[j, rows, own_lanes],
-                    ag_send.at[kind, k], ag_recv.at[kind, k], device,
+                    ag_send.at[0, kind], ag_recv.at[kind, k], device,
                 ).start()
 
     def send_block(layer, i):
@@ -190,28 +200,28 @@
         gather_copy(layer, 1, i, near_id).wait_recv()
         gather_copy(layer, 2, i, diagonal_id).wait_recv()
 
-    def drain_block(layer, i):
-        gather_copy(layer, 0, i, own).wait_send()
-        gather_copy(layer, 1, i, own).wait_send()
-        gather_copy(layer, 2, i, across_id).wait_send()
+    def drain_gather(layer):
+        for kind, owner in ((0, own), (1, own), (2, across_id)):
+            block = full_ref.at[:, :, lanes_of(owner, COLUMNS)]
+            remote(block, block, ag_send.at[layer, kind], ag_recv.at[kind, 0], sibling).wait_send()
 
     def halo_copy(layer, t, source):
         tail = tail_ref if layer else stream_ref.at[pl.ds(length - HALO, HALO)]
         return remote(
             tail, halo_ref.at[layer, source],
-            halo_send.at[layer, t], halo_recv.at[layer, source], (following, t),
+            halo_send.at[layer], halo_recv.at[layer, source], (following, t),
         )
 
     def halo_piece(j, t):
         lanes = lanes_of(j, COLUMNS)
         return remote(
             tail_ref.at[:, lanes], halo_ref.at[1, own, :, lanes],
-            halo_send.at[1, t], halo_recv.at[1, own], (following, t),
+            halo_send.at[1], halo_recv.at[1, own], (following, t),
         )
 
     def order_copy(d):
         return remote(
-            order_ref, orders_ref.at[seq], order_send, order_recv, ((seq + d) % count, own)
+            order_ref, orders_ref.at[seq], order_send, order_recv, (other_of(d), own)
         )
 
     def all_orders():
@@ -221,8 +231,8 @@
     for t in range(members):
         halo_copy(0, t, own).start()
 
-    each(0, chunks, send_rows)
-    each(1, count, lambda d: order_copy(d).start())
+    each(0, fines, send_rows)
+    each(0, count - 1, lambda d: order_copy(d).start())
 
     row = iota((2 * LANES, 2 * LANES), 0)
     col = iota((2 * LANES, 2 * LANES), 1)
@@ -259,9 +269,12 @@
     tri = jnp.where(lower, 1.0, 0.0).astype(bf16)
     left = iota((STRETCH, 2 * HEAD_DIM), 1) < HEAD_DIM
 
+    def squares_of(v):
+        wide = v.astype(f32)
+        return jnp.sum(wide * wide, axis=-1, keepdims=True)
+
     def scale_of(v):
-        wide = v.astype(f32)
-        return lax.rsqrt(jnp.mean(wide * wide, axis=-1, keepdims=True) + epsilon)
+        return lax.rsqrt(squares_of(v) / depth + epsilon)
 
     def scan(layer, arrive):
         for t in range(members):
@@ -285,69 +298,77 @@
         taps = jnp.concatenate([conv_x_ref[layer], conv_bc_ref[layer]], axis=1)
         tap_count = taps.shape[0]
 
+        size = ROWS if layer else FINE
+        parts = size // STRETCH
+
         def project(k):
-            rows = rows_of(k, ROWS)
+            rows = rows_of(k, size)
             arrive(k)
-            tokens = jnp.concatenate([full_ref[j, rows, :] for j in range(pieces)], axis=1)
-            scale = scale_of(tokens)
-            scale_ref[rows, :] = jnp.broadcast_to(scale, (ROWS, LANES))
             if layer == 0:
+                tokens = jnp.concatenate([full_ref[j, rows, :] for j in range(pieces)], axis=1)
+                scale = scale_of(tokens)
                 projected = jnp.dot(tokens, w_ref[...], preferred_element_type=f32)
             else:
+                tokens = full_ref[last_piece, rows, :]
+                square = scale_ref[rows, 0:1] + squares_of(tokens)
+                scale = lax.rsqrt(square / depth + epsilon)
                 projected = acc_ref[rows, :] + jnp.dot(
-                    full_ref[last_piece, rows, :], w_ref[last_piece * width :, :],
-                    preferred_element_type=f32,
+                    tokens, w_ref[last_piece * width :, :], preferred_element_type=f32
                 )
+            scale_ref[rows, :] = jnp.broadcast_to(scale, (size, LANES))
             projected = projected * scale
-            ext_ref[8 : 8 + ROWS, :] = projected[:, :mixed].astype(bf16).astype(f32)
-            conv = jnp.zeros((ROWS, mixed), f32)
+            raw = projected[:, mixed:] + bias
+            step = jnp.maximum(raw, 0.0) + jnp.log1p(jnp.exp(-jnp.abs(raw)))
+            logs = pack_pieces(-step * rate, heads)
+            sofar = sofar_ref[...]
+            summed_logs = jnp.dot(
+                tri,
+                jnp.concatenate(
+                    [logs[b * STRETCH : (b + 1) * STRETCH] for b in range(parts)], axis=1
+                ),
+                preferred_element_type=f32,
+            )
+            to_end, whole, earlier = [], [], []
+            for b in range(parts):
+                cum = unpack_sum(summed_logs[:, b * LANES : (b + 1) * LANES], heads)
+                last = cum[STRETCH - 1 : STRETCH, :]
+                cum_ref[rows_of(k * parts + b, STRETCH), :] = cum
+                to_end.append(step[b * STRETCH : (b + 1) * STRETCH] * jnp.exp(last - cum))
+                whole.append(jnp.exp(jnp.broadcast_to(last, (8, LANES))))
+                earlier.append(jnp.exp(sofar))
+                sofar = sofar + last
+            sofar_ref[...] = sofar
+            factors = expand(
+                jnp.concatenate([step] + to_end + whole + earlier, axis=0), heads, spreader
+            )
+            ext_ref[8 : 8 + size, :] = projected[:, :mixed].astype(bf16).astype(f32)
+            conv = jnp.zeros((size, mixed), f32)
             for tap in range(tap_count):
                 first = 9 - tap_count + tap
-                conv = conv + taps[tap : tap + 1, :] * ext_ref[first : first + ROWS, :]
+                conv = conv + taps[tap : tap + 1, :] * ext_ref[first : first + size, :]
             conv = conv * jax.nn.sigmoid(conv)
-            ext_ref[0:8, :] = ext_ref[ROWS : ROWS + 8, :]
-            raw = projected[:, mixed:] + bias
-            step = jnp.maximum(raw, 0.0) + jnp.log1p(jnp.exp(-jnp.abs(raw)))
-            logs = -step * rate
+            ext_ref[0:8, :] = ext_ref[size : size + 8, :]
             x = conv[:, :inner]
             b_all = conv[:, inner : inner + STATE]
             b_ref[rows, :] = b_all.astype(bf16)
             c_ref[rows, :] = conv[:, inner + STATE :].astype(bf16)
-            feed = x * expand(step, heads, spreader)
-            feed_ref[rows, :] = feed.astype(bf16)
+            feed_ref[rows, :] = (x * factors[:size]).astype(bf16)
             y_ref[rows, :] = skip * x
+            ending = (x * factors[size : 2 * size]).astype(bf16)
             state = state_ref[...]
-            sofar = sofar_ref[...]
-            for block in range(per):
-                part = slice(block * STRETCH, (block + 1) * STRETCH)
-                index = k * per + block
-                cum = running_sum(tri, logs[part], heads)
-                last = cum[STRETCH - 1 : STRETCH, :]
-                factors = expand(
-                    jnp.concatenate(
-                        [
-                            jnp.exp(last - cum),
-                            jnp.exp(jnp.broadcast_to(last, (8, LANES))),
-                            jnp.exp(sofar),
-                        ],
-                        axis=0,
-                    ),
-                    heads, spreader,
+            for b in range(parts):
+                part = slice(b * STRETCH, (b + 1) * STRETCH)
+                index = k * parts + b
+                fresh = jnp.dot(
+                    b_all[part].T.astype(bf16), ending[part], preferred_element_type=f32
                 )
-                fresh = jnp.dot(
-                    b_all[part].T.astype(bf16),
-                    (feed[part] * factors[:STRETCH]).astype(bf16),
-                    preferred_element_type=f32,
-                )
+                first = 2 * size + 8 * b
                 states_ref[index] = state
-                sofar_exp_ref[index] = factors[STRETCH + 8 :]
-                state = state * factors[STRETCH : STRETCH + 1] + fresh
-                cum_ref[rows_of(index, STRETCH), :] = cum
-                sofar = sofar + last
+                sofar_exp_ref[index] = factors[first + 8 * parts : first + 8 * parts + 8]
+                state = state * factors[first : first + 1] + fresh
             state_ref[...] = state
-            sofar_ref[...] = sofar
-
-        each(0, chunks, project)
+
+        each(0, length // size, project)
 
     def within(k):
         rows = rows_of(k, ROWS)
@@ -384,7 +405,7 @@
 
     def exchange(layer):
         def end_copy(d):
-            other = (seq + d) % count
+            other = other_of(d)
             return remote(
                 end_ref.at[layer, other], got_ref.at[layer, seq],
                 end_send.at[layer], end_recv.at[layer], (other, own),
@@ -393,11 +414,11 @@
         def log_copy(d):
             return remote(
                 log_ref.at[layer], logs_ref.at[layer, seq],
-                log_send.at[layer], log_recv.at[layer], ((seq + d) % count, own),
+                log_send.at[layer], log_recv.at[layer], (other_of(d), own),
             )
 
         def give_copy(d):
-            other = (seq + d) % count
+            other = other_of(d)
             return remote(
                 give_ref.at[layer, other], arriving_ref.at[layer, seq],
                 give_send.at[layer], give_recv.at[layer], (other, own),
@@ -422,7 +443,7 @@
             log_copy(d).start()
             end_copy(d).start()
 
-        each(1, count, send)
+        each(0, count - 1, send)
         each(0, chunks // 2, within)
         all_logs.wait_recv()
         all_ends.wait_recv()
@@ -435,7 +456,7 @@
             give_ref[layer, d] = prefix.astype(bf16)
             if d + 1 < count:
                 prefix = prefix * factors[d : d + 1] + got_ref[layer, d].astype(f32)
-        each(1, count, lambda d: give_copy(d).start())
+        each(0, count - 1, lambda d: give_copy(d).start())
         each(chunks // 2, chunks, within)
         all_given.wait_recv()
         arriving_ref[layer, seq] = give_ref[layer, seq]
@@ -499,12 +520,12 @@
         block = diagonal_id if side == 0 else near_id
         return remote(
             partial_ref.at[rows, lanes(block)], nears[side],
-            near_send.at[layer, side, slot], near_recv.at[layer, side, slot], sibling,
+            near_send.at[layer, side], near_recv.at[layer, side, slot], sibling,
         )
 
     def far_part(layer, i):
         _, _, _, (summing, far), slot = part_of(layer, i)
-        return remote(summing, far, far_send.at[layer, slot], far_recv.at[layer, slot], across)
+        return remote(summing, far, far_send.at[layer], far_recv.at[layer, slot], across)
 
     def send_near(layer, i):
         near_part(layer, 0, i).start()
@@ -529,10 +550,14 @@
             + far[...].astype(f32)
         ).astype(bf16)
 
-    def drain_part(layer, i):
-        near_part(layer, 0, i).wait_send()
-        near_part(layer, 1, i).wait_send()
-        far_part(layer, i).wait_send()
+    def drain_sums(layer):
+        near_ref, sum_ref = ((near_col_ref, sum_col_ref), (near_row_ref, sum_row_ref))[layer]
+        for side in range(2):
+            block = near_ref.at[side]
+            remote(
+                block, block, near_send.at[layer, side], near_recv.at[layer, side, 0], sibling
+            ).wait_send()
+        remote(sum_ref, sum_ref, far_send.at[layer], far_recv.at[layer, 0], across).wait_send()
 
     def plan():
         shift = length.bit_length() - 1
@@ -574,15 +599,15 @@
             ).astype(bf16)
 
     def move_copy(j, d):
-        other = (seq + d) % count
+        other = other_of(d)
         return remote(
             leaving_ref.at[j, rows_of(other, share)], arrived_ref.at[j, rows_of(seq, share)],
-            move_send.at[j], move_recv.at[j], (other, own),
+            move_send, move_recv.at[j], (other, own),
         )
 
     def all_moves(j):
         others = arrived_ref.at[j, pl.ds(0, length - share)]
-        return remote(others, others, move_send.at[j], move_recv.at[j], (following, own))
+        return remote(others, others, move_send, move_recv.at[j], (following, own))
 
     def hand_over(j):
         if j:
@@ -596,7 +621,7 @@
             each(0, chunks, first)
             held = held_ref[...]
         leaving_ref[j] = jnp.dot(hand_ref[...], held, preferred_element_type=f32).astype(bf16)
-        each(1, count, lambda d: move_copy(j, d).start())
+        each(0, count - 1, lambda d: move_copy(j, d).start())
         arrived_ref[j, rows_of(seq, share), :] = leaving_ref[j, rows_of(seq, share), :]
 
     def put(j):
@@ -611,7 +636,7 @@
             send_block(1, j)
         else:
             each(0, chunks, lambda k: send_block(1, (k,)))
-        out_ref[:, lanes] = rows
+        own_ref[:, lanes] = rows
 
     def accumulate(j):
         part = slice(j * width, (j + 1) * width)
@@ -622,6 +647,8 @@
                 full_ref[j, rows, :], w_ref[part, :], preferred_element_type=f32
             )
             acc_ref[rows, :] = result if j == 0 else acc_ref[rows, :] + result
+            square = jnp.broadcast_to(squares_of(full_ref[j, rows, :]), (ROWS, LANES))
+            scale_ref[rows, :] = square if j == 0 else scale_ref[rows, :] + square
 
         each(0, chunks, product)
 
@@ -631,8 +658,8 @@
         prepare(0, j)
     for copy in weight_loads(1):
         copy.start()
-    for copy in self_loads:
-        copy.wait()
+    own_columns = full_ref.at[:, :, own_lanes]
+    pltpu.make_async_copy(own_columns, own_columns, self_sem).wait()
 
     def arrive_first(k):
         forward_block(0, k)
@@ -640,9 +667,9 @@
 
     scan(0, arrive_first)
     exchange(0)
-    each(0, chunks, lambda k: drain_block(0, k))
-    for copy in wo_loads:
-        copy.wait()
+    drain_gather(0)
+    pltpu.make_async_copy(w_out_ref.at[0], wo_col_ref, wo_sem.at[0]).wait()
+    pltpu.make_async_copy(w_out_ref.at[1], wo_ref, wo_sem.at[1]).wait()
 
     def product_of(k, j):
         rows, lanes = rows_of(k, ROWS), lanes_of(j, members * COLUMNS)
@@ -675,9 +702,7 @@
             put(j - 1)
         prepare(1, j)
     put(pieces - 1)
-    each(0, chunks, lambda k: drain_part(0, (k,)))
-    for j in range(1, pieces):
-        drain_part(0, j)
+    drain_sums(0)
 
     for j in range(last_piece):
         forward_block(1, j)
@@ -696,37 +721,40 @@
     exchange(1)
 
     def output_rows(k):
-        partial_ref[rows_of(k, ROWS), :] = jnp.dot(
-            mixed_of(1, k), wo_ref[...], preferred_element_type=f32
-        ).astype(bf16)
-        send_near(1, k)
-
-        @pl.when(k > 0)
-        def _():
-            send_far(1, k - 1)
+        rows = rows_of(k, ROWS)
+        mixed_heads = mixed_of(1, k)
+        for side, block in enumerate((diagonal_id, near_id, across_id, own)):
+            lanes = lanes_of(block, width)
+            partial_ref[rows, lanes] = jnp.dot(
+                mixed_heads, wo_ref[:, lanes], preferred_element_type=f32
+            ).astype(bf16)
+            if side < 2:
+                near_part(1, side, k).start()
+        send_far(1, k)
 
     each(0, chunks, output_rows)
-    send_far(1, chunks - 1)
+
+    def out_copy(k):
+        rows = rows_of(k, ROWS)
+        return pltpu.make_async_copy(own_ref.at[rows], out_ref.at[rows], out_sem.at[k])
 
     def finish(k):
         rows = rows_of(k, ROWS)
-        out_ref[rows, :] = summed(1, k, out_ref[rows, :])
+        own_ref[rows, :] = summed(1, k, own_ref[rows, :])
+        out_copy(k).start()
 
     each(0, chunks, finish)
-    for j in range(last_piece):
-        drain_block(1, j)
-
-    def drain_last(k):
-        drain_block(1, (k,))
-        drain_part(1, k)
-
-    each(0, chunks, drain_last)
+    drain_gather(1)
+    drain_sums(1)
     for layer in range(2):
-        for t in range(members):
-            halo_copy(layer, t, own).wait_send()
+        block = halo_ref.at[layer]
+        remote(
+            block, block, halo_send.at[layer], halo_recv.at[layer, 0], (following, own)
+        ).wait_send()
     all_orders().wait_send()
-    for j in range(pieces):
-        all_moves(j).wait_send()
+    others = arrived_ref.at[:, pl.ds(0, length - share)]
+    remote(others, others, move_send, move_recv.at[0], (following, own)).wait_send()
+    each(0, chunks, lambda k: out_copy(k).wait())
 
 
 def body(
@@ -739,7 +767,7 @@
     heads = inner // HEAD_DIM
     mixed = inner + 2 * STATE
     depth = w_in.shape[1]
-    chunks = length // ROWS
+    chunks, fines = length // ROWS, length // FINE
     blocks = length // STRETCH
     pieces = width // COLUMNS
     state_rows = STATE // count
@@ -749,7 +777,7 @@
     return pl.pallas_call(
         functools.partial(layers_kernel, count, members),
         in_specs=[vmem, vmem, vmem, hbm, hbm] + [vmem] * 7 + [hbm],
-        out_specs=vmem,
+        out_specs=hbm,
         out_shape=jax.ShapeDtypeStruct(tokens.shape, bf16),
         scratch_shapes=[
             pltpu.VMEM((pieces, length, members * COLUMNS), bf16),
@@ -795,13 +823,14 @@
             pltpu.VMEM((pieces, length, COLUMNS), bf16),
             pltpu.VMEM((length, COLUMNS), bf16),
             pltpu.VMEM((length, mixed + LANES), f32),
-            dma((2, 2)), dma((pieces * members + 1,)), dma((pieces,)),
-            dma((3, 2 * chunks + pieces - 1)), dma((3, 2 * chunks + pieces - 1)),
-            dma((2, members)), dma((2, members)), dma, dma,
+            pltpu.VMEM((length, width), bf16),
+            dma((2, 2)), dma((2,)), dma,
+            dma((2, 3)), dma((3, fines + chunks + pieces - 1)),
+            dma((2,)), dma((2, members)), dma, dma,
             dma((2,)), dma((2,)), dma((2,)), dma((2,)), dma((2,)), dma((2,)),
-            dma((2, 2, chunks + pieces - 1)), dma((2, 2, chunks + pieces - 1)),
-            dma((2, chunks + pieces - 1)), dma((2, chunks + pieces - 1)),
-            dma((pieces,)), dma((pieces,)),
+            dma((2, 2)), dma((2, 2, chunks + pieces - 1)),
+            dma((2,)), dma((2, chunks + pieces - 1)),
+            dma, dma((pieces,)), dma((chunks,)),
         ],
         compiler_params=pltpu.CompilerParams(
             collective_id=0, has_side_effects=True, vmem_limit_bytes=63 * 1024 * 1024

time: 148 us -> 143 us (0.966)
  Pallas kernels: 146 us -> 141 us
    pallas_call x1, Pallas kernels: 146 us -> 141 us  [body(): pl.pallas_call(functools.partial(layers_kernel, count, members), in_specs...]
where the time goes in v5:
time: 143 us
  Pallas kernels  141 us (99%)
  local copies, waits for them, and re-layouts  2.26 us (2%)
    pallas_call x1, Pallas kernels, body(): pl.pallas_call(functools.partial(layers_kernel, count, members), in_specs...  141 us

profile of v5, /device:TPU:0, one launch (start us, length us, event | category | flops | bytes accessed | tf_op | source)
XLA Modules:
  0.0 142.9 jit_solution(17780390764782730)
XLA Ops:
  0.0 140.7 %mixer_layers.1 = bf16[1024,512]{1,0:T(8,128)(2,1)} custom-call(bf16[1024,512]{1,0:T(8,128)(2,1)} %stream_ref.1, s32[1,1024]{1,0:T(1,128)} %bitcast.3, f32[2,2048]{1,0:T(2,128)} %in_gain_ref.1, bf16[2,2048,2,512]{3,2,1,0:T(2,128)(2,1)} %w_in_ref.1, bf16[2,2048,256]{2,1,0:T(8,128)(2,1)} %w_bc_ref.1, bf16[2,8,2048]{2,1,0:T(8,128)(2,1)} %bitcast.2, ...), custom_call_target="tpu_custom_call" | custom-call | tf_op jit(solution)/shard_map/mixer_layers/pallas_call | solution.py:777
  140.7 2.3 %copy.15 = bf16[1024,512]{1,0:T(8,128)(2,1)} copy(bf16[1024,512]{1,0:T(8,128)(2,1)} %mixer_layers.1) | data formatting | bytes 2097152

commit v6 on v5

--- a/solution.py
+++ b/solution.py
@@ -78,7 +78,7 @@
     state_ref, sofar_ref,
     end_ref, log_ref, got_ref, logs_ref, give_ref, arriving_ref, prefix_ref,
     partial_ref, near_col_ref, sum_col_ref, far_col_ref, near_row_ref, sum_row_ref, far_row_ref,
-    mixed_ref, hand_ref, place_ref, leaving_ref, arrived_ref, held_ref, acc_ref, own_ref,
+    mixed_ref, hand_ref, place_ref, leaving_ref, arrived_ref, held_ref, acc_ref, gate_ref, own_ref,
     load_sem, wo_sem, self_sem, ag_send, ag_recv, halo_send, halo_recv, order_send, order_recv,
     end_send, end_recv, log_send, log_recv, give_send, give_recv,
     near_send, near_recv, far_send, far_recv, move_send, move_recv, out_sem,
@@ -163,6 +163,7 @@
     pl.semaphore_wait(barrier, len(greeted))
 
     last_piece = pieces - 1
+    late = pieces - 2
 
     def block_of(layer, i, owner):
         lanes = lanes_of(owner, COLUMNS)
@@ -269,6 +270,9 @@
     tri = jnp.where(lower, 1.0, 0.0).astype(bf16)
     left = iota((STRETCH, 2 * HEAD_DIM), 1) < HEAD_DIM
 
+    def late_tokens(rows):
+        return jnp.concatenate([full_ref[j, rows, :] for j in range(late, pieces)], axis=1)
+
     def squares_of(v):
         wide = v.astype(f32)
         return jnp.sum(wide * wide, axis=-1, keepdims=True)
@@ -308,14 +312,16 @@
                 tokens = jnp.concatenate([full_ref[j, rows, :] for j in range(pieces)], axis=1)
                 scale = scale_of(tokens)
                 projected = jnp.dot(tokens, w_ref[...], preferred_element_type=f32)
+                gate = jnp.dot(tokens, wz_ref[...], preferred_element_type=f32)
+                z_ref[rows, :] = (gate * scale).astype(bf16)
             else:
-                tokens = full_ref[last_piece, rows, :]
+                tokens = late_tokens(rows)
                 square = scale_ref[rows, 0:1] + squares_of(tokens)
                 scale = lax.rsqrt(square / depth + epsilon)
                 projected = acc_ref[rows, :] + jnp.dot(
-                    tokens, w_ref[last_piece * width :, :], preferred_element_type=f32
+                    tokens, w_ref[late * width :, :], preferred_element_type=f32
                 )
-            scale_ref[rows, :] = jnp.broadcast_to(scale, (size, LANES))
+                scale_ref[rows, :] = jnp.broadcast_to(scale, (size, LANES))
             projected = projected * scale
             raw = projected[:, mixed:] + bias
             step = jnp.maximum(raw, 0.0) + jnp.log1p(jnp.exp(-jnp.abs(raw)))
@@ -370,11 +376,13 @@
 
         each(0, length // size, project)
 
-    def within(k):
-        rows = rows_of(k, ROWS)
-        tokens = jnp.concatenate([full_ref[j, rows, :] for j in range(pieces)], axis=1)
-        gate = jnp.dot(tokens, wz_ref[...], preferred_element_type=f32)
-        z_ref[rows, :] = (gate * scale_ref[rows, 0:1]).astype(bf16)
+    def within(layer, k):
+        if layer:
+            rows = rows_of(k, ROWS)
+            gate = gate_ref[rows, :] + jnp.dot(
+                late_tokens(rows), wz_ref[late * width :, :], preferred_element_type=f32
+            )
+            z_ref[rows, :] = (gate * scale_ref[rows, 0:1]).astype(bf16)
 
         def block(b):
             rows = rows_of(k * per + b, STRETCH)
@@ -444,7 +452,7 @@
             end_copy(d).start()
 
         each(0, count - 1, send)
-        each(0, chunks // 2, within)
+        each(0, chunks // 2, lambda k: within(layer, k))
         all_logs.wait_recv()
         all_ends.wait_recv()
         got_ref[layer, seq] = end_ref[layer, seq]
@@ -457,7 +465,7 @@
             if d + 1 < count:
                 prefix = prefix * factors[d : d + 1] + got_ref[layer, d].astype(f32)
         each(0, count - 1, lambda d: give_copy(d).start())
-        each(chunks // 2, chunks, within)
+        each(chunks // 2, chunks, lambda k: within(layer, k))
         all_given.wait_recv()
         arriving_ref[layer, seq] = give_ref[layer, seq]
         prefix_ref[...] = jnp.concatenate(
@@ -611,12 +619,12 @@
 
     def hand_over(j):
         if j:
-            held = summed(0, j, stream_ref[:, j * COLUMNS : (j + 1) * COLUMNS])
+            held = summed(0, j, full_ref[j, :, own_lanes])
         else:
 
             def first(k):
                 rows = rows_of(k, ROWS)
-                held_ref[rows, :] = summed(0, (k,), stream_ref[rows, :COLUMNS])
+                held_ref[rows, :] = summed(0, (k,), full_ref[0, rows, own_lanes])
 
             each(0, chunks, first)
             held = held_ref[...]
@@ -647,6 +655,8 @@
                 full_ref[j, rows, :], w_ref[part, :], preferred_element_type=f32
             )
             acc_ref[rows, :] = result if j == 0 else acc_ref[rows, :] + result
+            gate = jnp.dot(full_ref[j, rows, :], wz_ref[part, :], preferred_element_type=f32)
+            gate_ref[rows, :] = gate if j == 0 else gate_ref[rows, :] + gate
             square = jnp.broadcast_to(squares_of(full_ref[j, rows, :]), (ROWS, LANES))
             scale_ref[rows, :] = square if j == 0 else scale_ref[rows, :] + square
 
@@ -698,17 +708,23 @@
 
     for j in range(pieces):
         hand_over(j)
-        if j:
-            put(j - 1)
+        if j > 1:
+            put(j - 2)
         prepare(1, j)
+    put(pieces - 2)
+    forward_block(1, 0)
+    rest_of_block(1, 0)
+    accumulate(0)
     put(pieces - 1)
     drain_sums(0)
 
-    for j in range(last_piece):
+    for j in range(1, last_piece):
         forward_block(1, j)
+        if j == last_piece - 1:
+            forward_block(1, (0,))
         rest_of_block(1, j)
-        accumulate(j)
-    forward_block(1, (0,))
+        if j < late:
+            accumulate(j)
 
     def arrive_second(k):
         @pl.when(k + 1 < chunks)
@@ -776,7 +792,7 @@
     dma = pltpu.SemaphoreType.DMA
     return pl.pallas_call(
         functools.partial(layers_kernel, count, members),
-        in_specs=[vmem, vmem, vmem, hbm, hbm] + [vmem] * 7 + [hbm],
+        in_specs=[hbm, vmem, vmem, hbm, hbm] + [vmem] * 7 + [hbm],
         out_specs=hbm,
         out_shape=jax.ShapeDtypeStruct(tokens.shape, bf16),
         scratch_shapes=[
@@ -823,6 +839,7 @@
             pltpu.VMEM((pieces, length, COLUMNS), bf16),
             pltpu.VMEM((length, COLUMNS), bf16),
             pltpu.VMEM((length, mixed + LANES), f32),
+            pltpu.VMEM((length, inner), f32),
             pltpu.VMEM((length, width), bf16),
             dma((2, 2)), dma((2,)), dma,
             dma((2, 3)), dma((3, fines + chunks + pieces - 1)),

time: 143 us -> 143 us (level)
  no operation moved by 1% of the time
where the time goes in v6:
time: 143 us
  Pallas kernels  141 us (99%)
  local copies, waits for them, and re-layouts  2.26 us (2%)
    pallas_call x1, Pallas kernels, body(): pl.pallas_call(functools.partial(layers_kernel, count, members), in_specs...  141 us

profile of v6, /device:TPU:0, one launch (start us, length us, event | category | flops | bytes accessed | tf_op | source)
XLA Modules:
  0.0 142.8 jit_solution(2043559004588764052)
XLA Ops:
  0.0 140.5 %mixer_layers.1 = bf16[1024,512]{1,0:T(8,128)(2,1)} custom-call(bf16[1024,512]{1,0:T(8,128)(2,1)} %stream_ref.1, s32[1,1024]{1,0:T(1,128)} %bitcast.3, f32[2,2048]{1,0:T(2,128)} %in_gain_ref.1, bf16[2,2048,2,512]{3,2,1,0:T(2,128)(2,1)} %w_in_ref.1, bf16[2,2048,256]{2,1,0:T(8,128)(2,1)} %w_bc_ref.1, bf16[2,8,2048]{2,1,0:T(8,128)(2,1)} %bitcast.2, ...), custom_call_target="tpu_custom_call" | custom-call | tf_op jit(solution)/shard_map/mixer_layers/pallas_call | solution.py:793
  140.5 2.3 %copy.15 = bf16[1024,512]{1,0:T(8,128)(2,1)} copy(bf16[1024,512]{1,0:T(8,128)(2,1)} %mixer_layers.1) | data formatting | bytes 2097152

commit v7 on v6

--- a/solution.py
+++ b/solution.py
@@ -77,7 +77,7 @@
     ext_ref, y_ref, z_ref, feed_ref, b_ref, c_ref, cum_ref, scale_ref, states_ref, sofar_exp_ref,
     state_ref, sofar_ref,
     end_ref, log_ref, got_ref, logs_ref, give_ref, arriving_ref, prefix_ref,
-    partial_ref, near_col_ref, sum_col_ref, far_col_ref, near_row_ref, sum_row_ref, far_row_ref,
+    partial_ref, near_ref, sum_ref, far_ref,
     mixed_ref, hand_ref, place_ref, leaving_ref, arrived_ref, held_ref, acc_ref, gate_ref, own_ref,
     load_sem, wo_sem, self_sem, ag_send, ag_recv, halo_send, halo_recv, order_send, order_recv,
     end_send, end_recv, log_send, log_recv, give_send, give_recv,
@@ -131,11 +131,13 @@
     for device in greeted:
         pl.semaphore_signal(barrier, inc=1, device_id=device, device_id_type=MESH)
 
-    def weight_loads(layer):
-        return [
-            pltpu.make_async_copy(w_in_ref.at[layer], raw_ref, load_sem.at[layer, 0]),
-            pltpu.make_async_copy(w_bc_ref.at[layer], raw_bc_ref, load_sem.at[layer, 1]),
-        ]
+    def load_in(layer, t):
+        return pltpu.make_async_copy(
+            w_in_ref.at[layer, t * width : (t + 1) * width], raw_ref.at[t % 2], load_sem.at[t % 2]
+        )
+
+    def load_bc(layer):
+        return pltpu.make_async_copy(w_bc_ref.at[layer], raw_bc_ref, load_sem.at[2])
 
     own_lanes = lanes_of(own, COLUMNS)
     self_loads, wo_loads = [], []
@@ -157,7 +159,7 @@
                 )
             )
     wo_loads.append(pltpu.make_async_copy(w_out_ref.at[1], wo_ref, wo_sem.at[1]))
-    for copy in weight_loads(0) + self_loads + wo_loads:
+    for copy in [load_in(0, 0), load_bc(0), load_in(0, 1)] + self_loads + wo_loads:
         copy.start()
 
     pl.semaphore_wait(barrier, len(greeted))
@@ -171,7 +173,9 @@
             return full_ref.at[:, rows_of(i, FINE), lanes], i
         if isinstance(i, int):
             return full_ref.at[i, :, lanes], fines + i
-        return full_ref.at[last_piece, rows_of(i[0], ROWS), lanes], fines + last_piece + i[0]
+        k, j = i
+        slot = fines + late + (j - late) * chunks + k
+        return full_ref.at[j, rows_of(k, ROWS), lanes], slot
 
     def gather_copy(layer, kind, i, owner):
         block, slot = block_of(layer, i, owner)
@@ -239,14 +243,16 @@
     col = iota((2 * LANES, 2 * LANES), 1)
     apart = jnp.where(col == 2 * (row % LANES) + row // LANES, 1.0, 0.0).astype(bf16)
 
-    def prepare(layer, j):
-        def block(t):
+    def prepare(layer, t):
+        load_in(layer, t).wait()
+
+        def block(j):
             i = t * pieces + j
             rows = rows_of(i, LANES)
             to = rows_of(j * members + t, LANES)
             gain = in_gain_ref[layer : layer + 1, lanes_of(i, LANES)]
             gain = jnp.broadcast_to(gain, (LANES, LANES)).T
-            both = raw_ref[rows].reshape(2 * LANES, inner)
+            both = raw_ref[t % 2, rows_of(j, LANES)].reshape(2 * LANES, inner)
             halves = jnp.dot(apart, both, preferred_element_type=f32)
             for p in range(inner // LANES):
                 lanes = slice(p * LANES, (p + 1) * LANES)
@@ -261,7 +267,11 @@
             dt = jnp.concatenate([dt, jnp.zeros((LANES - heads, LANES), f32)], axis=0)
             w_ref[to, mixed:] = (dt.T * gain).astype(bf16)
 
-        each(0, members, block)
+        each(0, pieces, block)
+        if t + 2 < members:
+            load_in(layer, t + 2).start()
+        elif layer == 0:
+            load_in(1, t + 2 - members).start()
 
     spreader = spreader_of(heads, inner)
     line = iota((STRETCH, STRETCH), 0)
@@ -445,7 +455,7 @@
         state = state_ref[...]
         for d in range(count):
             end_ref[layer, d] = state[d * state_rows : (d + 1) * state_rows].astype(bf16)
-        log_ref[layer] = sofar_ref[...]
+        log_ref[layer] = sofar_ref[0:1, :]
 
         def send(d):
             log_copy(d).start()
@@ -457,7 +467,7 @@
         all_ends.wait_recv()
         got_ref[layer, seq] = end_ref[layer, seq]
         logs_ref[layer, seq] = log_ref[layer]
-        logs = jnp.concatenate([logs_ref[layer, d, 0:1] for d in range(count)], axis=0)
+        logs = jnp.concatenate([logs_ref[layer, d] for d in range(count)], axis=0)
         factors = expand(jnp.exp(logs), heads, spreader)
         prefix = jnp.zeros((state_rows, inner), f32)
         for d in range(count):
@@ -511,17 +521,16 @@
 
     def part_of(layer, i):
         if layer == 1:
-            rows = rows_of(i, ROWS)
-            blocks_of = [ref.at[rows] for ref in (sum_row_ref, far_row_ref)]
-            nears = [near_row_ref.at[side, rows] for side in range(2)]
-            return rows, lambda t: lanes_of(t, width), nears, blocks_of, i
-        if isinstance(i, int):
-            rows, j, slot = pl.ds(0, length), i, chunks + i - 1
+            rows, slot = rows_of(i, ROWS), i
+            lanes, held = (lambda t: lanes_of(t, width)), pl.ds(0, width)
         else:
-            rows, j, slot = rows_of(i[0], ROWS), 0, i[0]
-        blocks_of = [ref.at[j, rows] for ref in (sum_col_ref, far_col_ref)]
-        nears = [near_col_ref.at[side, j, rows] for side in range(2)]
-        return rows, lambda t: lanes_of(j * members + t, COLUMNS), nears, blocks_of, slot
+            if isinstance(i, int):
+                rows, j, slot = pl.ds(0, length), i, chunks + i - 1
+            else:
+                rows, j, slot = rows_of(i[0], ROWS), 0, i[0]
+            lanes, held = (lambda t: lanes_of(j * members + t, COLUMNS)), lanes_of(j, COLUMNS)
+        nears = [near_ref.at[side, rows, held] for side in range(2)]
+        return rows, lanes, nears, (sum_ref.at[rows, held], far_ref.at[rows, held]), slot
 
     def near_part(layer, side, i):
         rows, lanes, nears, _, slot = part_of(layer, i)
@@ -559,7 +568,6 @@
         ).astype(bf16)
 
     def drain_sums(layer):
-        near_ref, sum_ref = ((near_col_ref, sum_col_ref), (near_row_ref, sum_row_ref))[layer]
         for side in range(2):
             block = near_ref.at[side]
             remote(
@@ -640,10 +648,18 @@
         full_ref[j, :, own_lanes] = rows
         for t in range(members):
             halo_piece(j, t).start()
-        if j < last_piece:
+        if j < late:
             send_block(1, j)
+        elif j < last_piece:
+            send_block(1, (0, j))
         else:
-            each(0, chunks, lambda k: send_block(1, (k,)))
+            send_block(1, (0, j))
+
+            def send_late(k):
+                for other in range(late, pieces):
+                    send_block(1, (k, other))
+
+            each(1, chunks, send_late)
         own_ref[:, lanes] = rows
 
     def accumulate(j):
@@ -662,12 +678,10 @@
 
         each(0, chunks, product)
 
-    for copy in weight_loads(0):
-        copy.wait()
-    for j in range(pieces):
-        prepare(0, j)
-    for copy in weight_loads(1):
-        copy.start()
+    load_bc(0).wait()
+    for t in range(members):
+        prepare(0, t)
+    load_bc(1).start()
     own_columns = full_ref.at[:, :, own_lanes]
     pltpu.make_async_copy(own_columns, own_columns, self_sem).wait()
 
@@ -703,8 +717,7 @@
         send_far(0, j - 1 if j > 1 else (chunks - 1,))
     send_far(0, pieces - 1)
     plan()
-    for copy in weight_loads(1):
-        copy.wait()
+    load_bc(1).wait()
 
     for j in range(pieces):
         hand_over(j)
@@ -718,20 +731,24 @@
     put(pieces - 1)
     drain_sums(0)
 
-    for j in range(1, last_piece):
+    for j in range(1, late):
         forward_block(1, j)
-        if j == last_piece - 1:
-            forward_block(1, (0,))
         rest_of_block(1, j)
-        if j < late:
-            accumulate(j)
+        accumulate(j)
+
+    def forward_late(k):
+        for j in range(late, pieces):
+            forward_block(1, (k, j))
+
+    forward_late(0)
 
     def arrive_second(k):
         @pl.when(k + 1 < chunks)
         def _():
-            forward_block(1, (k + 1,))
-
-        rest_of_block(1, (k,))
+            forward_late(k + 1)
+
+        for j in range(late, pieces):
+            rest_of_block(1, (k, j))
 
     scan(1, arrive_second)
     exchange(1)
@@ -788,7 +805,7 @@
     pieces = width // COLUMNS
     state_rows = STATE // count
     vmem = pl.BlockSpec(memory_space=pltpu.VMEM)
-    hbm = pl.BlockSpec(memory_space=pl.ANY)
+    hbm = pl.BlockSpec(memory_space=pltpu.HBM)
     dma = pltpu.SemaphoreType.DMA
     return pl.pallas_call(
         functools.partial(layers_kernel, count, members),
@@ -800,7 +817,7 @@
             pltpu.VMEM((HALO, width), bf16),
             pltpu.VMEM((2, members, HALO, width), bf16),
             pltpu.VMEM((count, 1, length), jnp.int32),
-            pltpu.VMEM((depth, 2, inner), bf16),
+            pltpu.VMEM((2, width, 2, inner), bf16),
             pltpu.VMEM((depth, 2 * STATE), bf16),
             pltpu.VMEM((depth, mixed + LANES), bf16),
             pltpu.VMEM((depth, inner), bf16),
@@ -819,16 +836,13 @@
             pltpu.VMEM((STATE, inner), f32),
             pltpu.VMEM((8, LANES), f32),
             pltpu.VMEM((2, count, state_rows, inner), bf16),
-            pltpu.VMEM((2, 8, LANES), f32),
+            pltpu.VMEM((2, 1, LANES), f32),
             pltpu.VMEM((2, count, state_rows, inner), bf16),
-            pltpu.VMEM((2, count, 8, LANES), f32),
+            pltpu.VMEM((2, count, 1, LANES), f32),
             pltpu.VMEM((2, count, state_rows, inner), bf16),
             pltpu.VMEM((2, count, state_rows, inner), bf16),
             pltpu.VMEM((STATE, inner), f32),
             pltpu.VMEM((length, depth), bf16),
-            pltpu.VMEM((2, pieces, length, COLUMNS), bf16),
-            pltpu.VMEM((pieces, length, COLUMNS), bf16),
-            pltpu.VMEM((pieces, length, COLUMNS), bf16),
             pltpu.VMEM((2, length, width), bf16),
             pltpu.VMEM((length, width), bf16),
             pltpu.VMEM((length, width), bf16),
@@ -841,8 +855,8 @@
             pltpu.VMEM((length, mixed + LANES), f32),
             pltpu.VMEM((length, inner), f32),
             pltpu.VMEM((length, width), bf16),
-            dma((2, 2)), dma((2,)), dma,
-            dma((2, 3)), dma((3, fines + chunks + pieces - 1)),
+            dma((3,)), dma((2,)), dma,
+            dma((2, 3)), dma((3, fines + 2 * chunks + pieces - 2)),
             dma((2,)), dma((2, members)), dma, dma,
             dma((2,)), dma((2,)), dma((2,)), dma((2,)), dma((2,)), dma((2,)),
             dma((2, 2)), dma((2, 2, chunks + pieces - 1)),

time: 143 us -> 141 us (0.986)
  Pallas kernels: 141 us -> 139 us
    pallas_call x1, Pallas kernels: 141 us -> 139 us  [body(): pl.pallas_call(functools.partial(layers_kernel, count, members), in_specs...]
where the time goes in v7:
time: 141 us
  Pallas kernels  139 us (99%)
  local copies, waits for them, and re-layouts  2.26 us (2%)
    pallas_call x1, Pallas kernels, body(): pl.pallas_call(functools.partial(layers_kernel, count, members), in_specs...  139 us

profile of v7, /device:TPU:0, one launch (start us, length us, event | category | flops | bytes accessed | tf_op | source)
XLA Modules:
  0.0 141.0 jit_solution(16603262561248585804)
XLA Ops:
  0.0 138.7 %mixer_layers.1 = bf16[1024,512]{1,0:T(8,128)(2,1)} custom-call(bf16[1024,512]{1,0:T(8,128)(2,1)} %stream_ref.1, s32[1,1024]{1,0:T(1,128)} %bitcast.3, f32[2,2048]{1,0:T(2,128)} %in_gain_ref.1, bf16[2,2048,2,512]{3,2,1,0:T(2,128)(2,1)} %w_in_ref.1, bf16[2,2048,256]{2,1,0:T(8,128)(2,1)} %w_bc_ref.1, bf16[2,8,2048]{2,1,0:T(8,128)(2,1)} %bitcast.2, ...), custom_call_target="tpu_custom_call" | custom-call | tf_op jit(solution)/shard_map/mixer_layers/pallas_call | solution.py:810
  138.7 2.3 %copy.15 = bf16[1024,512]{1,0:T(8,128)(2,1)} copy(bf16[1024,512]{1,0:T(8,128)(2,1)} %mixer_layers.1) | data formatting | bytes 2097152

commit v8 on v7

--- a/solution.py
+++ b/solution.py
@@ -14,6 +14,7 @@
 HALO = 16
 ROWS = 256
 FINE = 128
+HALVES = 2
 COLUMNS = 128
 
 epsilon = 1e-05
@@ -103,6 +104,7 @@
     pieces = width // COLUMNS
     share = length // count
     state_rows = STATE // count
+    half_rows = state_rows // HALVES
     following = (seq + 1) % count
     before = (seq + count - 1) % count
 
@@ -165,6 +167,7 @@
     pl.semaphore_wait(barrier, len(greeted))
 
     last_piece = pieces - 1
+    early = chunks // 2
     late = pieces - 2
 
     def block_of(layer, i, owner):
@@ -173,9 +176,14 @@
             return full_ref.at[:, rows_of(i, FINE), lanes], i
         if isinstance(i, int):
             return full_ref.at[i, :, lanes], fines + i
-        k, j = i
-        slot = fines + late + (j - late) * chunks + k
-        return full_ref.at[j, rows_of(k, ROWS), lanes], slot
+        slot = fines + late + i[0]
+        return full_ref.at[pl.ds(late, pieces - late), rows_of(i[0], ROWS), lanes], slot
+
+    def send_part(j, k):
+        part = full_ref.at[j, rows_of(k, ROWS), own_lanes]
+        slot = fines + late + k
+        for kind, device in ((0, across), (1, sibling)):
+            remote(part, part, ag_send.at[1, kind], ag_recv.at[kind, slot], device).start()
 
     def gather_copy(layer, kind, i, owner):
         block, slot = block_of(layer, i, owner)
@@ -422,11 +430,11 @@
         each(0, per, block)
 
     def exchange(layer):
-        def end_copy(d):
+        def end_copy(h, d):
             other = other_of(d)
             return remote(
-                end_ref.at[layer, other], got_ref.at[layer, seq],
-                end_send.at[layer], end_recv.at[layer], (other, own),
+                end_ref.at[layer, h, other], got_ref.at[layer, h, seq],
+                end_send.at[layer, h], end_recv.at[layer, h], (other, own),
             )
 
         def log_copy(d):
@@ -435,56 +443,67 @@
                 log_send.at[layer], log_recv.at[layer], (other_of(d), own),
             )
 
-        def give_copy(d):
+        def give_copy(h, d):
             other = other_of(d)
             return remote(
-                give_ref.at[layer, other], arriving_ref.at[layer, seq],
-                give_send.at[layer], give_recv.at[layer], (other, own),
+                give_ref.at[layer, h, other], arriving_ref.at[layer, h, seq],
+                give_send.at[layer, h], give_recv.at[layer, h], (other, own),
             )
 
         others = pl.ds(0, count - 1)
 
-        def all_of(ref, send, recv):
-            block = ref.at[layer, others]
-            return remote(block, block, send.at[layer], recv.at[layer], (following, own))
-
-        all_ends = all_of(got_ref, end_send, end_recv)
-        all_logs = all_of(logs_ref, log_send, log_recv)
-        all_given = all_of(arriving_ref, give_send, give_recv)
+        def all_of(block, send, recv):
+            return remote(block, block, send, recv, (following, own))
+
+        def all_ends(h):
+            block = got_ref.at[layer, h, others]
+            return all_of(block, end_send.at[layer, h], end_recv.at[layer, h])
+
+        def all_given(h):
+            block = arriving_ref.at[layer, h, others]
+            return all_of(block, give_send.at[layer, h], give_recv.at[layer, h])
+
+        all_logs = all_of(logs_ref.at[layer, others], log_send.at[layer], log_recv.at[layer])
 
         state = state_ref[...]
+        log_ref[layer] = sofar_ref[0:1, :]
         for d in range(count):
-            end_ref[layer, d] = state[d * state_rows : (d + 1) * state_rows].astype(bf16)
-        log_ref[layer] = sofar_ref[0:1, :]
-
-        def send(d):
-            log_copy(d).start()
-            end_copy(d).start()
-
-        each(0, count - 1, send)
-        each(0, chunks // 2, lambda k: within(layer, k))
+            for h in range(HALVES):
+                first = d * state_rows + h * half_rows
+                end_ref[layer, h, d] = state[first : first + half_rows].astype(bf16)
+        each(0, count - 1, lambda d: log_copy(d).start())
+        for h in range(HALVES):
+            each(0, count - 1, lambda d: end_copy(h, d).start())
+        first_part = chunks * 3 // 4
+        each(0, first_part, lambda k: within(layer, k))
         all_logs.wait_recv()
-        all_ends.wait_recv()
-        got_ref[layer, seq] = end_ref[layer, seq]
         logs_ref[layer, seq] = log_ref[layer]
         logs = jnp.concatenate([logs_ref[layer, d] for d in range(count)], axis=0)
         factors = expand(jnp.exp(logs), heads, spreader)
-        prefix = jnp.zeros((state_rows, inner), f32)
-        for d in range(count):
-            give_ref[layer, d] = prefix.astype(bf16)
-            if d + 1 < count:
-                prefix = prefix * factors[d : d + 1] + got_ref[layer, d].astype(f32)
-        each(0, count - 1, lambda d: give_copy(d).start())
-        each(chunks // 2, chunks, lambda k: within(layer, k))
-        all_given.wait_recv()
-        arriving_ref[layer, seq] = give_ref[layer, seq]
+        for h in range(HALVES):
+            all_ends(h).wait_recv()
+            got_ref[layer, h, seq] = end_ref[layer, h, seq]
+            prefix = jnp.zeros((half_rows, inner), f32)
+            for d in range(count):
+                give_ref[layer, h, d] = prefix.astype(bf16)
+                if d + 1 < count:
+                    prefix = prefix * factors[d : d + 1] + got_ref[layer, h, d].astype(f32)
+            each(0, count - 1, lambda d: give_copy(h, d).start())
+        each(first_part, chunks, lambda k: within(layer, k))
+        for h in range(HALVES):
+            all_given(h).wait_recv()
+            arriving_ref[layer, h, seq] = give_ref[layer, h, seq]
         prefix_ref[...] = jnp.concatenate(
-            [arriving_ref[layer, d].astype(f32) for d in range(count)], axis=0
-        )
-
+            [
+                arriving_ref[layer, h, d].astype(f32)
+                for d in range(count) for h in range(HALVES)
+            ],
+            axis=0,
+        )
         all_logs.wait_send()
-        all_ends.wait_send()
-        all_given.wait_send()
+        for h in range(HALVES):
+            all_ends(h).wait_send()
+            all_given(h).wait_send()
 
     pair = 2 * HEAD_DIM
     one = iota((2 * pair, pair), 0) % pair // HEAD_DIM
@@ -650,16 +669,10 @@
             halo_piece(j, t).start()
         if j < late:
             send_block(1, j)
-        elif j < last_piece:
-            send_block(1, (0, j))
         else:
-            send_block(1, (0, j))
-
-            def send_late(k):
-                for other in range(late, pieces):
-                    send_block(1, (k, other))
-
-            each(1, chunks, send_late)
+            each(0, early, lambda k: send_part(j, k))
+        if j == last_piece:
+            each(early, chunks, lambda k: send_block(1, (k,)))
         own_ref[:, lanes] = rows
 
     def accumulate(j):
@@ -736,19 +749,14 @@
         rest_of_block(1, j)
         accumulate(j)
 
-    def forward_late(k):
-        for j in range(late, pieces):
-            forward_block(1, (k, j))
-
-    forward_late(0)
+    forward_block(1, (0,))
 
     def arrive_second(k):
         @pl.when(k + 1 < chunks)
         def _():
-            forward_late(k + 1)
-
-        for j in range(late, pieces):
-            rest_of_block(1, (k, j))
+            forward_block(1, (k + 1,))
+
+        rest_of_block(1, (k,))
 
     scan(1, arrive_second)
     exchange(1)
@@ -804,6 +812,7 @@
     blocks = length // STRETCH
     pieces = width // COLUMNS
     state_rows = STATE // count
+    half_rows = state_rows // HALVES
     vmem = pl.BlockSpec(memory_space=pltpu.VMEM)
     hbm = pl.BlockSpec(memory_space=pltpu.HBM)
     dma = pltpu.SemaphoreType.DMA
@@ -835,12 +844,12 @@
             pltpu.VMEM((blocks, 8, inner), f32),
             pltpu.VMEM((STATE, inner), f32),
             pltpu.VMEM((8, LANES), f32),
-            pltpu.VMEM((2, count, state_rows, inner), bf16),
+            pltpu.VMEM((2, HALVES, count, half_rows, inner), bf16),
             pltpu.VMEM((2, 1, LANES), f32),
-            pltpu.VMEM((2, count, state_rows, inner), bf16),
+            pltpu.VMEM((2, HALVES, count, half_rows, inner), bf16),
             pltpu.VMEM((2, count, 1, LANES), f32),
-            pltpu.VMEM((2, count, state_rows, inner), bf16),
-            pltpu.VMEM((2, count, state_rows, inner), bf16),
+            pltpu.VMEM((2, HALVES, count, half_rows, inner), bf16),
+            pltpu.VMEM((2, HALVES, count, half_rows, inner), bf16),
             pltpu.VMEM((STATE, inner), f32),
             pltpu.VMEM((length, depth), bf16),
             pltpu.VMEM((2, length, width), bf16),
@@ -856,9 +865,10 @@
             pltpu.VMEM((length, inner), f32),
             pltpu.VMEM((length, width), bf16),
             dma((3,)), dma((2,)), dma,
-            dma((2, 3)), dma((3, fines + 2 * chunks + pieces - 2)),
+            dma((2, 3)), dma((3, fines + chunks + pieces - 2)),
             dma((2,)), dma((2, members)), dma, dma,
-            dma((2,)), dma((2,)), dma((2,)), dma((2,)), dma((2,)), dma((2,)),
+            dma((2, HALVES)), dma((2, HALVES)), dma((2,)), dma((2,)),
+            dma((2, HALVES)), dma((2, HALVES)),
             dma((2, 2)), dma((2, 2, chunks + pieces - 1)),
             dma((2,)), dma((2, chunks + pieces - 1)),
             dma, dma((pieces,)), dma((chunks,)),

time: 141 us -> 140 us (level)
  Pallas kernels: 139 us -> 137 us
    pallas_call x1, Pallas kernels: 139 us -> 137 us  [body(): pl.pallas_call(functools.partial(layers_kernel, count, members), in_specs...]
where the time goes in v8:
time: 140 us
  Pallas kernels  137 us (98%)
  local copies, waits for them, and re-layouts  2.26 us (2%)
    pallas_call x1, Pallas kernels, body(): pl.pallas_call(functools.partial(layers_kernel, count, members), in_specs...  137 us

profile of v8, /device:TPU:0, one launch (start us, length us, event | category | flops | bytes accessed | tf_op | source)
XLA Modules:
  0.0 139.5 jit_solution(9431594100744556056)
XLA Ops:
  0.0 137.3 %mixer_layers.1 = bf16[1024,512]{1,0:T(8,128)(2,1)} custom-call(bf16[1024,512]{1,0:T(8,128)(2,1)} %stream_ref.1, s32[1,1024]{1,0:T(1,128)} %bitcast.3, f32[2,2048]{1,0:T(2,128)} %in_gain_ref.1, bf16[2,2048,2,512]{3,2,1,0:T(2,128)(2,1)} %w_in_ref.1, bf16[2,2048,256]{2,1,0:T(8,128)(2,1)} %w_bc_ref.1, bf16[2,8,2048]{2,1,0:T(8,128)(2,1)} %bitcast.2, ...), custom_call_target="tpu_custom_call" | custom-call | tf_op jit(solution)/shard_map/mixer_layers/pallas_call | solution.py:819
  137.3 2.3 %copy.15 = bf16[1024,512]{1,0:T(8,128)(2,1)} copy(bf16[1024,512]{1,0:T(8,128)(2,1)} %mixer_layers.1) | data formatting | bytes 2097152

commit v9 on v8

--- a/solution.py
+++ b/solution.py
@@ -15,6 +15,7 @@
 ROWS = 256
 FINE = 128
 HALVES = 2
+SMALLS = 9
 COLUMNS = 128
 
 epsilon = 1e-05
@@ -71,19 +72,23 @@
 
 def layers_kernel(
     count, members,
-    stream_ref, order_ref, in_gain_ref, w_in_ref, w_bc_ref, w_dt_ref, conv_x_ref, conv_bc_ref,
-    bias_ref, a_log_ref, d_skip_ref, out_gain_ref, w_out_ref,
-    out_ref,
-    full_ref, tail_ref, halo_ref, orders_ref, raw_ref, raw_bc_ref, w_ref, wz_ref, wo_col_ref, wo_ref,
-    ext_ref, y_ref, z_ref, feed_ref, b_ref, c_ref, cum_ref, scale_ref, states_ref, sofar_exp_ref,
-    state_ref, sofar_ref,
-    end_ref, log_ref, got_ref, logs_ref, give_ref, arriving_ref, prefix_ref,
-    partial_ref, near_ref, sum_ref, far_ref,
-    mixed_ref, hand_ref, place_ref, leaving_ref, arrived_ref, held_ref, acc_ref, gate_ref, own_ref,
-    load_sem, wo_sem, self_sem, ag_send, ag_recv, halo_send, halo_recv, order_send, order_recv,
-    end_send, end_recv, log_send, log_recv, give_send, give_recv,
-    near_send, near_recv, far_send, far_recv, move_send, move_recv, out_sem,
+    stream_ref, w_in_ref, w_bc_ref, w_out_ref, *refs,
 ):
+    smalls = refs[:SMALLS]
+    (
+        out_ref, order_ref, in_gain_ref, w_dt_ref, conv_x_ref, conv_bc_ref,
+        bias_ref, a_log_ref, d_skip_ref, out_gain_ref,
+        full_ref, tail_ref, halo_ref, orders_ref, raw_ref, raw_bc_ref, w_ref, wz_ref, wo_col_ref, wo_ref,
+        ext_ref, y_ref, z_ref, feed_ref, b_ref, c_ref, cum_ref, scale_ref, states_ref, sofar_exp_ref,
+        state_ref, sofar_ref,
+        end_ref, log_ref, got_ref, logs_ref, give_ref, arriving_ref, prefix_ref,
+        partial_ref, near_ref, sum_ref, far_ref,
+        mixed_ref, hand_ref, place_ref, leaving_ref, arrived_ref, held_ref, acc_ref, gate_ref, own_ref,
+        load_sem, wo_sem, self_sem, ag_send, ag_recv, halo_send, halo_recv, order_send, order_recv,
+        end_send, end_recv, log_send, log_recv, give_send, give_recv,
+        near_send, near_recv, far_send, far_recv, move_send, move_recv, out_sem,
+        small_sem,
+    ) = refs[SMALLS:]
     seq = lax.axis_index("seq")
     own = lax.axis_index("tp")
     chip, core = own // 2, own % 2
@@ -126,12 +131,21 @@
 
         lax.fori_loop(first, last, step, 0)
 
-    greeted = [sibling, across]
+    greeted = [(other_of(d), own) for d in range(count - 1)]
     greeted += [(before, t) for t in range(members)]
-    greeted += [((seq + d) % count, own) for d in range(1, count)]
+    greeted += [across, sibling]
     barrier = pltpu.get_barrier_semaphore()
     for device in greeted:
         pl.semaphore_signal(barrier, inc=1, device_id=device, device_id_type=MESH)
+
+    kept = (
+        order_ref, in_gain_ref, w_dt_ref, conv_x_ref, conv_bc_ref,
+        bias_ref, a_log_ref, d_skip_ref, out_gain_ref,
+    )
+    small_loads = [
+        pltpu.make_async_copy(small, keep, small_sem.at[i])
+        for i, (small, keep) in enumerate(zip(smalls, kept))
+    ]
 
     def load_in(layer, t):
         return pltpu.make_async_copy(
@@ -161,7 +175,7 @@
                 )
             )
     wo_loads.append(pltpu.make_async_copy(w_out_ref.at[1], wo_ref, wo_sem.at[1]))
-    for copy in [load_in(0, 0), load_bc(0), load_in(0, 1)] + self_loads + wo_loads:
+    for copy in small_loads + [load_in(0, 0), load_bc(0), load_in(0, 1)] + self_loads + wo_loads:
         copy.start()
 
     pl.semaphore_wait(barrier, len(greeted))
@@ -245,6 +259,8 @@
         halo_copy(0, t, own).start()
 
     each(0, fines, send_rows)
+    for copy in small_loads:
+        copy.wait()
     each(0, count - 1, lambda d: order_copy(d).start())
 
     row = iota((2 * LANES, 2 * LANES), 0)
@@ -813,15 +829,19 @@
     pieces = width // COLUMNS
     state_rows = STATE // count
     half_rows = state_rows // HALVES
-    vmem = pl.BlockSpec(memory_space=pltpu.VMEM)
+    smalls = (
+        col_order[None], in_gain, jnp.swapaxes(w_dt, 1, 2), conv_x, conv_bc,
+        dt_bias, a_log, d_skip, out_gain,
+    )
     hbm = pl.BlockSpec(memory_space=pltpu.HBM)
     dma = pltpu.SemaphoreType.DMA
     return pl.pallas_call(
         functools.partial(layers_kernel, count, members),
-        in_specs=[hbm, vmem, vmem, hbm, hbm] + [vmem] * 7 + [hbm],
+        in_specs=[hbm] * (4 + SMALLS),
         out_specs=hbm,
         out_shape=jax.ShapeDtypeStruct(tokens.shape, bf16),
         scratch_shapes=[
+            *[pltpu.VMEM(small.shape, small.dtype) for small in smalls],
             pltpu.VMEM((pieces, length, members * COLUMNS), bf16),
             pltpu.VMEM((HALO, width), bf16),
             pltpu.VMEM((2, members, HALO, width), bf16),
@@ -871,15 +891,14 @@
             dma((2, HALVES)), dma((2, HALVES)),
             dma((2, 2)), dma((2, 2, chunks + pieces - 1)),
             dma((2,)), dma((2, chunks + pieces - 1)),
-            dma, dma((pieces,)), dma((chunks,)),
+            dma, dma((pieces,)), dma((chunks,)), dma((SMALLS,)),
         ],
         compiler_params=pltpu.CompilerParams(
             collective_id=0, has_side_effects=True, vmem_limit_bytes=63 * 1024 * 1024
         ),
         name="mixer_layers",
     )(
-        tokens, col_order[None], in_gain, w_in, w_bc, jnp.swapaxes(w_dt, 1, 2), conv_x, conv_bc,
-        dt_bias, a_log, d_skip, out_gain, w_out,
+        tokens, w_in, w_bc, w_out, *smalls,
     )
 
 

time: 140 us -> 139 us (level)
  no operation moved by 1% of the time
where the time goes in v9:
time: 139 us
  Pallas kernels  136 us (98%)
  local copies, waits for them, and re-layouts  2.26 us (2%)
    pallas_call x1, Pallas kernels, body(): pl.pallas_call(functools.partial(layers_kernel, count, members), in_specs...  136 us

profile of v9, /device:TPU:0, one launch (start us, length us, event | category | flops | bytes accessed | tf_op | source)
XLA Modules:
  0.0 138.6 jit_solution(1865874928417709165)
XLA Ops:
  0.0 136.4 %mixer_layers.1 = bf16[1024,512]{1,0:T(8,128)(2,1)} custom-call(bf16[1024,512]{1,0:T(8,128)(2,1)} %stream_ref.1, bf16[2,2048,2,512]{3,2,1,0:T(2,128)(2,1)} %w_in_ref.1, bf16[2,2048,256]{2,1,0:T(8,128)(2,1)} %w_bc_ref.1, bf16[2,512,2048]{2,1,0:T(8,128)(2,1)} %w_out_ref.1, s32[1,1024]{1,0:T(1,128)} %bitcast.3, f32[2,2048]{1,0:T(2,128)} %refs_1_.1, ...), custom_call_target="tpu_custom_call" | custom-call | tf_op jit(solution)/shard_map/mixer_layers/pallas_call | solution.py:838
  136.4 2.3 %copy.15 = bf16[1024,512]{1,0:T(8,128)(2,1)} copy(bf16[1024,512]{1,0:T(8,128)(2,1)} %mixer_layers.1) | data formatting | bytes 2097152

commit v10 on v9

--- a/solution.py
+++ b/solution.py
@@ -490,7 +490,7 @@
         each(0, count - 1, lambda d: log_copy(d).start())
         for h in range(HALVES):
             each(0, count - 1, lambda d: end_copy(h, d).start())
-        first_part = chunks * 3 // 4
+        first_part = chunks // 2
         each(0, first_part, lambda k: within(layer, k))
         all_logs.wait_recv()
         logs_ref[layer, seq] = log_ref[layer]

time: 139 us -> 139 us (level)
  no operation moved by 1% of the time
where the time goes in v10:
time: 139 us; the launch traced here: 138 us
  Pallas kernels  136 us (98%)
  local copies, waits for them, and re-layouts  2.26 us (2%)
    pallas_call x1, Pallas kernels, body(): pl.pallas_call(functools.partial(layers_kernel, count, members), in_specs...  136 us

profile of v10, /device:TPU:0, one launch (start us, length us, event | category | flops | bytes accessed | tf_op | source)
XLA Modules:
  0.0 138.4 jit_solution(10154605312088591552)
XLA Ops:
  0.0 136.2 %mixer_layers.1 = bf16[1024,512]{1,0:T(8,128)(2,1)} custom-call(bf16[1024,512]{1,0:T(8,128)(2,1)} %stream_ref.1, bf16[2,2048,2,512]{3,2,1,0:T(2,128)(2,1)} %w_in_ref.1, bf16[2,2048,256]{2,1,0:T(8,128)(2,1)} %w_bc_ref.1, bf16[2,512,2048]{2,1,0:T(8,128)(2,1)} %w_out_ref.1, s32[1,1024]{1,0:T(1,128)} %bitcast.3, f32[2,2048]{1,0:T(2,128)} %refs_1_.1, ...), custom_call_target="tpu_custom_call" | custom-call | tf_op jit(solution)/shard_map/mixer_layers/pallas_call | solution.py:838
  136.2 2.3 %copy.15 = bf16[1024,512]{1,0:T(8,128)(2,1)} copy(bf16[1024,512]{1,0:T(8,128)(2,1)} %mixer_layers.1) | data formatting | bytes 2097152
